TPU v7x, 256 devices: a whole 4x4x8 slice. The times are simulated.
256 devices in a mesh: section: 16 (over z, core), seq: 16 (over x, y).
Axes of the slice: x: 4, y: 4, z: 8, core: 2. Of those that a mesh axis runs over, the one named last changes fastest.
Arguments:
- frames_in: bfloat16 [4, 16, 128, 1152], P(None, 'seq'), may hold values from -6 to 6
- spatial_qkv: bfloat16 [16, 1152, 1728], P('section'), may hold values from -0.1875 to 0.1875
- spatial_out: bfloat16 [16, 576, 1152], P('section'), may hold values from -0.25 to 0.25
- temporal_qkv: bfloat16 [16, 1152, 1728], P('section'), may hold values from -0.1875 to 0.1875
- temporal_out: bfloat16 [16, 576, 1152], P('section'), may hold values from -0.25 to 0.25
- modulation: float32 [16, 4, 6, 1152], P('section'), may hold values from -3 to 3
Outputs:
- hidden: bfloat16 [16, 4, 16, 128, 1152], P('section', None, 'seq')
All inputs are finite; a program needn't handle non-finite values.
Results may differ from a plain program's by a relative error of at most 0.015.
Values may be sent and summed in bfloat16 or wider, within the bound.
No kernel may reach another device: no remote copies, remote signals or barrier semaphores. Data moves between devices by JAX's collectives and lax.ppermute only.
A program may use at most 64 MiB of HBM per device.

v0:
```python
import math

import jax
import jax.numpy as jnp
from jax import lax
from jax.sharding import PartitionSpec as P

HEADS = 8


def passed_along(block, axis, distance):
    devices = range(lax.axis_size(axis))
    route = [(i - distance, i) for i in devices if i - distance in devices]
    return lax.ppermute(block, axis, route)


def norm_modulate(residual, offset, scaling):
    average = jnp.mean(residual, axis=-1, keepdims=True)
    centered = residual - average
    variance = jnp.mean(centered * centered, axis=-1, keepdims=True)
    return (centered / jnp.sqrt(variance + 1e-06) * (1.0 + scaling) + offset).astype(jnp.bfloat16)


def head_rms(tensor):
    return (tensor / jnp.sqrt(jnp.mean(tensor * tensor, axis=-1, keepdims=True) + 1e-06)).astype(
        jnp.bfloat16
    )


def split_heads(projected, head_count):
    head_width = projected.shape[-1] // 3
    heads_shape = projected.shape[:-1] + (head_count, head_width // head_count)
    queries = head_rms(projected[..., :head_width].reshape(heads_shape))
    lookups = head_rms(projected[..., head_width : 2 * head_width].reshape(heads_shape))
    values = projected[..., 2 * head_width :].reshape(heads_shape).astype(jnp.bfloat16)
    return (queries, lookups, values)


def merge_heads(tensor):
    return tensor.reshape(tensor.shape[:-2] + (tensor.shape[-2] * tensor.shape[-1],))


def attend(queries, lookups, values):
    scores = jnp.einsum(
        "...qhd,...khd->...hqk", queries, lookups, preferred_element_type=jnp.float32
    )
    scores = scores / math.sqrt(queries.shape[-1])
    exponent = jnp.exp(scores)
    totals = jnp.sum(exponent, axis=-1)
    mixed = jnp.einsum(
        "...hqk,...khd->...qhd",
        exponent.astype(jnp.bfloat16),
        values,
        preferred_element_type=jnp.float32,
    )
    return (mixed / jnp.swapaxes(totals, -1, -2)[..., None]).astype(jnp.bfloat16)


def on_device(frames_in, spatial_qkv, spatial_out, temporal_qkv, temporal_out, modulation):
    per_round = 2
    rounds = frames_in.shape[0] // per_round
    sections = lax.axis_size("section")
    rank_count = lax.axis_size("seq")
    section_index = lax.axis_index("section")
    spatial_entry = spatial_qkv[0]
    spatial_exit = spatial_out[0]
    temporal_entry = temporal_qkv[0]
    temporal_exit = temporal_out[0]
    factor_table = modulation[0]
    head_width = spatial_entry.shape[1] // 3
    block_shape = (per_round,) + frames_in.shape[1:]
    patch_shape = (per_round, frames_in.shape[1] * rank_count, frames_in.shape[2] // rank_count)

    def dispatch(payload):
        return lax.all_to_all(payload, "seq", split_axis=2, concat_axis=1, tiled=True)

    def unpack(arrived):
        projected = jnp.dot(arrived, temporal_entry, preferred_element_type=jnp.float32)
        return split_heads(projected, HEADS)

    payload_width = frames_in.shape[3]

    def first_half(incoming, factors):
        residual = incoming.astype(jnp.float32)
        scaled = factors[:, :, None, None, :]
        normed = norm_modulate(residual, scaled[:, 0], scaled[:, 1])
        projected = jnp.dot(normed, spatial_entry, preferred_element_type=jnp.float32)
        queries, lookups, values = split_heads(projected, HEADS)
        mixed = merge_heads(attend(queries, lookups, values))
        middle = residual + scaled[:, 2] * jnp.dot(
            mixed, spatial_exit, preferred_element_type=jnp.float32
        )
        return (middle, norm_modulate(middle, scaled[:, 3], scaled[:, 4]))

    def empty_first(incoming, factors):
        return (
            jnp.zeros(block_shape, jnp.float32),
            jnp.zeros(block_shape[:-1] + (payload_width,), jnp.bfloat16),
        )

    def temporal_mix(arrived):
        queries, lookups, values = unpack(arrived)
        mixed = attend(
            jnp.swapaxes(queries, 1, 2), jnp.swapaxes(lookups, 1, 2), jnp.swapaxes(values, 1, 2)
        )
        return merge_heads(jnp.swapaxes(mixed, 1, 2))

    def empty_mix(arrived):
        return jnp.zeros(patch_shape + (head_width,), jnp.bfloat16)

    def last_half(middle, returned, factors):
        gating = factors[:, 5][:, None, None, :]
        return (
            middle + gating * jnp.dot(returned, temporal_exit, preferred_element_type=jnp.float32)
        ).astype(jnp.bfloat16)

    def empty_last(middle, returned, factors):
        return jnp.zeros(block_shape, jnp.bfloat16)

    def advance(step_index, carried):
        hidden, arriving = carried
        micro_index = step_index - section_index
        active = jnp.logical_and(micro_index >= 0, micro_index < rounds)
        first_row = jnp.clip(micro_index, 0, rounds - 1) * per_round
        fresh_block = lax.dynamic_slice_in_dim(frames_in, first_row, per_round, 0)
        incoming = jnp.where(section_index == 0, fresh_block, arriving)
        factors = lax.dynamic_slice_in_dim(factor_table, first_row, per_round, 0)
        middle, payload = lax.cond(active, first_half, empty_first, incoming, factors)
        arrived = dispatch(payload)
        mixed = lax.cond(active, temporal_mix, empty_mix, arrived)
        returned = lax.all_to_all(mixed, "seq", split_axis=1, concat_axis=2, tiled=True)
        leaving = lax.cond(active, last_half, empty_last, middle, returned, factors)
        previous = lax.dynamic_slice_in_dim(hidden, first_row, per_round, 0)
        hidden = lax.dynamic_update_slice_in_dim(
            hidden, jnp.where(active, leaving, previous), first_row, 0
        )
        arriving = passed_along(leaving, "section", 1)
        return (hidden, arriving)

    initial = (jnp.zeros(frames_in.shape, jnp.bfloat16), jnp.zeros(block_shape, jnp.bfloat16))
    hidden, arriving = lax.fori_loop(0, rounds + sections - 1, advance, initial)
    return hidden[None]


def solution(mesh):
    placed = (
        P(None, "seq", None, None),
        P("section", None, None),
        P("section", None, None),
        P("section", None, None),
        P("section", None, None),
        P("section", None, None, None),
    )
    return jax.shard_map(
        on_device,
        mesh=mesh,
        in_specs=placed,
        out_specs=P("section", None, "seq", None, None),
        check_vma=False,
    )
```

profile of v0, /device:TPU:225, one launch (start us, length us, event | category | flops | bytes accessed | tf_op | source)
XLA Modules:
  0.0 1050.1 jit_solution(989131757668748955)
XLA Ops:
  1.7 1048.4 %while.16 = (s32[]{:T(128)}, bf16[4,1,128,1152]{3,2,0,1:T(8,128)(2,1)}, bf16[2,1,128,1152]{3,2,0,1:T(8,128)(2,1)S(1)}, s32[]{:T(128)}, f32[4,6,1152]{2,0,1:T(4,1...) while((s32[]{:T(128)}, ...), condition=%wide.region_17.18_spmd, body=%wide.region_0.17_spmd.sunk | while | flops 2815239168 | bytes 58655800 | solution.py:141
  12.0 11.0 %all-to-all-done = bf16[2,1,128,1152]{3,0,1,2:T(2,128)(2,1)S(1)} async-done(((bf16[2,1,128,1152]{3,0,1,2:T(2,128)(2,1)}), bf16[2,1,128,1152]{3,0,1,2:T(2,128)(2,1)S(1)}, u32[]{:S(2)}, u32[]{:S(2)}) %all-to-all-start) | async-done | bytes 589856 | tf_op jit(solution)/shard_map/while/body/eval_jaxpr/all_to_all | solution.py:75
  73.8 10.3 collective-permute-done
  91.3 9.3 all-to-all-done
  116.0 10.3 collective-permute-done
  133.5 9.3 all-to-all-done
  158.2 10.3 collective-permute-done
  175.7 9.3 all-to-all-done
  200.5 10.3 collective-permute-done
  217.9 9.3 all-to-all-done
  242.7 10.3 collective-permute-done
  260.2 9.3 all-to-all-done
  284.9 10.3 collective-permute-done
  302.4 9.3 all-to-all-done
  327.1 10.3 collective-permute-done
  344.6 9.3 all-to-all-done
  369.4 10.3 collective-permute-done
  411.6 10.3 collective-permute-done
  453.8 10.3 collective-permute-done
  496.0 10.3 collective-permute-done
  513.5 9.3 all-to-all-done
  538.3 10.3 collective-permute-done
  555.7 9.3 all-to-all-done
  580.5 10.3 collective-permute-done
  597.9 9.3 all-to-all-done
  622.7 301.5 %collective-permute-done = bf16[2,1,128,1152]{3,2,0,1:T(8,128)(2,1)S(1)} collective-permute-done((bf16[2,1,128,1152]{3,2,0,1:T(8,128)(2,1)S(1)}, bf16[2,1,128,1152]{3,2,0,1:T(8,128)(2,1)S(1)}, u32[]{:S(2)}, u32[]{:S(2)}) %collective-permute-start) | collective-permute-done | bytes 589856 | tf_op jit(solution)/shard_map/while/body/eval_jaxpr/ppermute | solution.py:14
  925.1 13.4 %conditional.6 = (f32[2,1,128,1152]{3,2,0,1:T(8,128)}, bf16[2,1,128,1152]{3,2,0,1:T(8,128)(2,1)S(1)}) conditional(s32[]{:T(128)} %convert_element_type.118, () %tuple.83, (pred[]{:T(512)}, bf16[4,1,128,1152]{3,2,0,1:T(8,128)(2,1)}, s32[]{:T(128)}, bf16[2,1,128,1152]{3,2,0,1:T(8,128)(2,1)S(1)}, f32[2,6,1152]{2,0,1:T(2,128)S(1)}, ...), branch_computations={%region_1.1_spmd, %region_2.9_spmd} | conditional | flops 1444092928 | bytes 23405596 | solution.py:128
  952.9 10.1 conditional.7
  980.7 12.3 %collective-permute-done = bf16[2,1,128,1152]{3,2,0,1:T(8,128)(2,1)S(1)} collective-permute-done((bf16[2,1,128,1152]{3,2,0,1:T(8,128)(2,1)S(1)}, bf16[2,1,128,1152]{3,2,0,1:T(8,128)(2,1)S(1)}, u32[]{:S(2)}, u32[]{:S(2)}) %collective-permute-start) | collective-permute-done | bytes 589856 | tf_op jit(solution)/shard_map/while/body/eval_jaxpr/ppermute | solution.py:14
  993.9 13.4 %conditional.6 = (f32[2,1,128,1152]{3,2,0,1:T(8,128)}, bf16[2,1,128,1152]{3,2,0,1:T(8,128)(2,1)S(1)}) conditional(s32[]{:T(128)} %convert_element_type.118, () %tuple.83, (pred[]{:T(512)}, bf16[4,1,128,1152]{3,2,0,1:T(8,128)(2,1)}, s32[]{:T(128)}, bf16[2,1,128,1152]{3,2,0,1:T(8,128)(2,1)S(1)}, f32[2,6,1152]{2,0,1:T(2,128)S(1)}, ...), branch_computations={%region_1.1_spmd, %region_2.9_spmd} | conditional | flops 1444092928 | bytes 23405596 | solution.py:128
  1012.4 9.3 all-to-all-done
  1021.7 10.1 conditional.7
  (362 shorter events, 510.4 us)
Async XLA Ops:
  5.3 17.8 %all-to-all-start = ((bf16[2,1,128,1152]{3,0,1,2:T(2,128)(2,1)}), bf16[2,1,128,1152]{3,0,1,2:T(2,128)(2,1)S(1)}, u32[]{:S(2)}, u32[]{:S(2)}) async-start(bf16[2,1,128,1152]{3,0,1,2:T(2,128)(2,1)} %copy.60), calls=%async_computation | async-start | bytes 1179648 | tf_op jit(solution)/shard_map/while/body/eval_jaxpr/all_to_all | solution.py:75
  45.5 12.8 %all-to-all-start = ((bf16[2,1,128,1152]{3,0,1,2:T(2,128)(2,1)}), bf16[2,1,128,1152]{3,0,1,2:T(2,128)(2,1)S(1)}, u32[]{:S(2)}, u32[]{:S(2)}) async-start(bf16[2,1,128,1152]{3,0,1,2:T(2,128)(2,1)} %copy.60), calls=%async_computation | async-start | bytes 1179648 | tf_op jit(solution)/shard_map/while/body/eval_jaxpr/all_to_all | solution.py:75
  70.4 13.8 %collective-permute-start = (bf16[2,1,128,1152]{3,2,0,1:T(8,128)(2,1)S(1)}, bf16[2,1,128,1152]{3,2,0,1:T(8,128)(2,1)S(1)}, u32[]{:S(2)}, u32[]{:S(2)}) collective-permute-start(bf16[2,1,128,1152]{3,2,0,1:T(8,128)(2,1)S(1)} %get-tuple-element.506), channel_id=1, source_target_pairs={{0,16},{16,32},{32,48},{48,64},{64,80},{80,96},{96,112},{112,128},... | collective-permute-start | bytes 1769480 | tf_op jit(solution)/shard_map/while/body/eval_jaxpr/ppermute | solution.py:14
  87.7 12.8 %all-to-all-start = ((bf16[2,1,128,1152]{3,0,1,2:T(2,128)(2,1)}), bf16[2,1,128,1152]{3,0,1,2:T(2,128)(2,1)S(1)}, u32[]{:S(2)}, u32[]{:S(2)}) async-start(bf16[2,1,128,1152]{3,0,1,2:T(2,128)(2,1)} %copy.60), calls=%async_computation | async-start | bytes 1179648 | tf_op jit(solution)/shard_map/while/body/eval_jaxpr/all_to_all | solution.py:75
  112.6 13.8 %collective-permute-start = (bf16[2,1,128,1152]{3,2,0,1:T(8,128)(2,1)S(1)}, bf16[2,1,128,1152]{3,2,0,1:T(8,128)(2,1)S(1)}, u32[]{:S(2)}, u32[]{:S(2)}) collective-permute-start(bf16[2,1,128,1152]{3,2,0,1:T(8,128)(2,1)S(1)} %get-tuple-element.506), channel_id=1, source_target_pairs={{0,16},{16,32},{32,48},{48,64},{64,80},{80,96},{96,112},{112,128},... | collective-permute-start | bytes 1769480 | tf_op jit(solution)/shard_map/while/body/eval_jaxpr/ppermute | solution.py:14
  129.9 12.8 %all-to-all-start = ((bf16[2,1,128,1152]{3,0,1,2:T(2,128)(2,1)}), bf16[2,1,128,1152]{3,0,1,2:T(2,128)(2,1)S(1)}, u32[]{:S(2)}, u32[]{:S(2)}) async-start(bf16[2,1,128,1152]{3,0,1,2:T(2,128)(2,1)} %copy.60), calls=%async_computation | async-start | bytes 1179648 | tf_op jit(solution)/shard_map/while/body/eval_jaxpr/all_to_all | solution.py:75
  154.8 13.8 %collective-permute-start = (bf16[2,1,128,1152]{3,2,0,1:T(8,128)(2,1)S(1)}, bf16[2,1,128,1152]{3,2,0,1:T(8,128)(2,1)S(1)}, u32[]{:S(2)}, u32[]{:S(2)}) collective-permute-start(bf16[2,1,128,1152]{3,2,0,1:T(8,128)(2,1)S(1)} %get-tuple-element.506), channel_id=1, source_target_pairs={{0,16},{16,32},{32,48},{48,64},{64,80},{80,96},{96,112},{112,128},... | collective-permute-start | bytes 1769480 | tf_op jit(solution)/shard_map/while/body/eval_jaxpr/ppermute | solution.py:14
  172.1 12.8 %all-to-all-start = ((bf16[2,1,128,1152]{3,0,1,2:T(2,128)(2,1)}), bf16[2,1,128,1152]{3,0,1,2:T(2,128)(2,1)S(1)}, u32[]{:S(2)}, u32[]{:S(2)}) async-start(bf16[2,1,128,1152]{3,0,1,2:T(2,128)(2,1)} %copy.60), calls=%async_computation | async-start | bytes 1179648 | tf_op jit(solution)/shard_map/while/body/eval_jaxpr/all_to_all | solution.py:75
  197.0 13.8 %collective-permute-start = (bf16[2,1,128,1152]{3,2,0,1:T(8,128)(2,1)S(1)}, bf16[2,1,128,1152]{3,2,0,1:T(8,128)(2,1)S(1)}, u32[]{:S(2)}, u32[]{:S(2)}) collective-permute-start(bf16[2,1,128,1152]{3,2,0,1:T(8,128)(2,1)S(1)} %get-tuple-element.506), channel_id=1, source_target_pairs={{0,16},{16,32},{32,48},{48,64},{64,80},{80,96},{96,112},{112,128},... | collective-permute-start | bytes 1769480 | tf_op jit(solution)/shard_map/while/body/eval_jaxpr/ppermute | solution.py:14
  214.3 12.8 %all-to-all-start = ((bf16[2,1,128,1152]{3,0,1,2:T(2,128)(2,1)}), bf16[2,1,128,1152]{3,0,1,2:T(2,128)(2,1)S(1)}, u32[]{:S(2)}, u32[]{:S(2)}) async-start(bf16[2,1,128,1152]{3,0,1,2:T(2,128)(2,1)} %copy.60), calls=%async_computation | async-start | bytes 1179648 | tf_op jit(solution)/shard_map/while/body/eval_jaxpr/all_to_all | solution.py:75
  239.2 13.8 %collective-permute-start = (bf16[2,1,128,1152]{3,2,0,1:T(8,128)(2,1)S(1)}, bf16[2,1,128,1152]{3,2,0,1:T(8,128)(2,1)S(1)}, u32[]{:S(2)}, u32[]{:S(2)}) collective-permute-start(bf16[2,1,128,1152]{3,2,0,1:T(8,128)(2,1)S(1)} %get-tuple-element.506), channel_id=1, source_target_pairs={{0,16},{16,32},{32,48},{48,64},{64,80},{80,96},{96,112},{112,128},... | collective-permute-start | bytes 1769480 | tf_op jit(solution)/shard_map/while/body/eval_jaxpr/ppermute | solution.py:14
  256.6 12.8 %all-to-all-start = ((bf16[2,1,128,1152]{3,0,1,2:T(2,128)(2,1)}), bf16[2,1,128,1152]{3,0,1,2:T(2,128)(2,1)S(1)}, u32[]{:S(2)}, u32[]{:S(2)}) async-start(bf16[2,1,128,1152]{3,0,1,2:T(2,128)(2,1)} %copy.60), calls=%async_computation | async-start | bytes 1179648 | tf_op jit(solution)/shard_map/while/body/eval_jaxpr/all_to_all | solution.py:75
  281.5 13.8 %collective-permute-start = (bf16[2,1,128,1152]{3,2,0,1:T(8,128)(2,1)S(1)}, bf16[2,1,128,1152]{3,2,0,1:T(8,128)(2,1)S(1)}, u32[]{:S(2)}, u32[]{:S(2)}) collective-permute-start(bf16[2,1,128,1152]{3,2,0,1:T(8,128)(2,1)S(1)} %get-tuple-element.506), channel_id=1, source_target_pairs={{0,16},{16,32},{32,48},{48,64},{64,80},{80,96},{96,112},{112,128},... | collective-permute-start | bytes 1769480 | tf_op jit(solution)/shard_map/while/body/eval_jaxpr/ppermute | solution.py:14
  298.8 12.8 %all-to-all-start = ((bf16[2,1,128,1152]{3,0,1,2:T(2,128)(2,1)}), bf16[2,1,128,1152]{3,0,1,2:T(2,128)(2,1)S(1)}, u32[]{:S(2)}, u32[]{:S(2)}) async-start(bf16[2,1,128,1152]{3,0,1,2:T(2,128)(2,1)} %copy.60), calls=%async_computation | async-start | bytes 1179648 | tf_op jit(solution)/shard_map/while/body/eval_jaxpr/all_to_all | solution.py:75
  323.7 13.8 %collective-permute-start = (bf16[2,1,128,1152]{3,2,0,1:T(8,128)(2,1)S(1)}, bf16[2,1,128,1152]{3,2,0,1:T(8,128)(2,1)S(1)}, u32[]{:S(2)}, u32[]{:S(2)}) collective-permute-start(bf16[2,1,128,1152]{3,2,0,1:T(8,128)(2,1)S(1)} %get-tuple-element.506), channel_id=1, source_target_pairs={{0,16},{16,32},{32,48},{48,64},{64,80},{80,96},{96,112},{112,128},... | collective-permute-start | bytes 1769480 | tf_op jit(solution)/shard_map/while/body/eval_jaxpr/ppermute | solution.py:14
  341.0 12.8 %all-to-all-start = ((bf16[2,1,128,1152]{3,0,1,2:T(2,128)(2,1)}), bf16[2,1,128,1152]{3,0,1,2:T(2,128)(2,1)S(1)}, u32[]{:S(2)}, u32[]{:S(2)}) async-start(bf16[2,1,128,1152]{3,0,1,2:T(2,128)(2,1)} %copy.60), calls=%async_computation | async-start | bytes 1179648 | tf_op jit(solution)/shard_map/while/body/eval_jaxpr/all_to_all | solution.py:75
  365.9 13.8 %collective-permute-start = (bf16[2,1,128,1152]{3,2,0,1:T(8,128)(2,1)S(1)}, bf16[2,1,128,1152]{3,2,0,1:T(8,128)(2,1)S(1)}, u32[]{:S(2)}, u32[]{:S(2)}) collective-permute-start(bf16[2,1,128,1152]{3,2,0,1:T(8,128)(2,1)S(1)} %get-tuple-element.506), channel_id=1, source_target_pairs={{0,16},{16,32},{32,48},{48,64},{64,80},{80,96},{96,112},{112,128},... | collective-permute-start | bytes 1769480 | tf_op jit(solution)/shard_map/while/body/eval_jaxpr/ppermute | solution.py:14
  383.2 12.8 %all-to-all-start = ((bf16[2,1,128,1152]{3,0,1,2:T(2,128)(2,1)}), bf16[2,1,128,1152]{3,0,1,2:T(2,128)(2,1)S(1)}, u32[]{:S(2)}, u32[]{:S(2)}) async-start(bf16[2,1,128,1152]{3,0,1,2:T(2,128)(2,1)} %copy.60), calls=%async_computation | async-start | bytes 1179648 | tf_op jit(solution)/shard_map/while/body/eval_jaxpr/all_to_all | solution.py:75
  408.1 13.8 %collective-permute-start = (bf16[2,1,128,1152]{3,2,0,1:T(8,128)(2,1)S(1)}, bf16[2,1,128,1152]{3,2,0,1:T(8,128)(2,1)S(1)}, u32[]{:S(2)}, u32[]{:S(2)}) collective-permute-start(bf16[2,1,128,1152]{3,2,0,1:T(8,128)(2,1)S(1)} %get-tuple-element.506), channel_id=1, source_target_pairs={{0,16},{16,32},{32,48},{48,64},{64,80},{80,96},{96,112},{112,128},... | collective-permute-start | bytes 1769480 | tf_op jit(solution)/shard_map/while/body/eval_jaxpr/ppermute | solution.py:14
  425.5 12.8 %all-to-all-start = ((bf16[2,1,128,1152]{3,0,1,2:T(2,128)(2,1)}), bf16[2,1,128,1152]{3,0,1,2:T(2,128)(2,1)S(1)}, u32[]{:S(2)}, u32[]{:S(2)}) async-start(bf16[2,1,128,1152]{3,0,1,2:T(2,128)(2,1)} %copy.60), calls=%async_computation | async-start | bytes 1179648 | tf_op jit(solution)/shard_map/while/body/eval_jaxpr/all_to_all | solution.py:75
  450.4 13.8 %collective-permute-start = (bf16[2,1,128,1152]{3,2,0,1:T(8,128)(2,1)S(1)}, bf16[2,1,128,1152]{3,2,0,1:T(8,128)(2,1)S(1)}, u32[]{:S(2)}, u32[]{:S(2)}) collective-permute-start(bf16[2,1,128,1152]{3,2,0,1:T(8,128)(2,1)S(1)} %get-tuple-element.506), channel_id=1, source_target_pairs={{0,16},{16,32},{32,48},{48,64},{64,80},{80,96},{96,112},{112,128},... | collective-permute-start | bytes 1769480 | tf_op jit(solution)/shard_map/while/body/eval_jaxpr/ppermute | solution.py:14
  467.7 12.8 %all-to-all-start = ((bf16[2,1,128,1152]{3,0,1,2:T(2,128)(2,1)}), bf16[2,1,128,1152]{3,0,1,2:T(2,128)(2,1)S(1)}, u32[]{:S(2)}, u32[]{:S(2)}) async-start(bf16[2,1,128,1152]{3,0,1,2:T(2,128)(2,1)} %copy.60), calls=%async_computation | async-start | bytes 1179648 | tf_op jit(solution)/shard_map/while/body/eval_jaxpr/all_to_all | solution.py:75
  492.6 13.8 %collective-permute-start = (bf16[2,1,128,1152]{3,2,0,1:T(8,128)(2,1)S(1)}, bf16[2,1,128,1152]{3,2,0,1:T(8,128)(2,1)S(1)}, u32[]{:S(2)}, u32[]{:S(2)}) collective-permute-start(bf16[2,1,128,1152]{3,2,0,1:T(8,128)(2,1)S(1)} %get-tuple-element.506), channel_id=1, source_target_pairs={{0,16},{16,32},{32,48},{48,64},{64,80},{80,96},{96,112},{112,128},... | collective-permute-start | bytes 1769480 | tf_op jit(solution)/shard_map/while/body/eval_jaxpr/ppermute | solution.py:14
  509.9 12.8 %all-to-all-start = ((bf16[2,1,128,1152]{3,0,1,2:T(2,128)(2,1)}), bf16[2,1,128,1152]{3,0,1,2:T(2,128)(2,1)S(1)}, u32[]{:S(2)}, u32[]{:S(2)}) async-start(bf16[2,1,128,1152]{3,0,1,2:T(2,128)(2,1)} %copy.60), calls=%async_computation | async-start | bytes 1179648 | tf_op jit(solution)/shard_map/while/body/eval_jaxpr/all_to_all | solution.py:75
  534.8 13.8 %collective-permute-start = (bf16[2,1,128,1152]{3,2,0,1:T(8,128)(2,1)S(1)}, bf16[2,1,128,1152]{3,2,0,1:T(8,128)(2,1)S(1)}, u32[]{:S(2)}, u32[]{:S(2)}) collective-permute-start(bf16[2,1,128,1152]{3,2,0,1:T(8,128)(2,1)S(1)} %get-tuple-element.506), channel_id=1, source_target_pairs={{0,16},{16,32},{32,48},{48,64},{64,80},{80,96},{96,112},{112,128},... | collective-permute-start | bytes 1769480 | tf_op jit(solution)/shard_map/while/body/eval_jaxpr/ppermute | solution.py:14
  552.1 12.8 %all-to-all-start = ((bf16[2,1,128,1152]{3,0,1,2:T(2,128)(2,1)}), bf16[2,1,128,1152]{3,0,1,2:T(2,128)(2,1)S(1)}, u32[]{:S(2)}, u32[]{:S(2)}) async-start(bf16[2,1,128,1152]{3,0,1,2:T(2,128)(2,1)} %copy.60), calls=%async_computation | async-start | bytes 1179648 | tf_op jit(solution)/shard_map/while/body/eval_jaxpr/all_to_all | solution.py:75
  577.0 13.8 %collective-permute-start = (bf16[2,1,128,1152]{3,2,0,1:T(8,128)(2,1)S(1)}, bf16[2,1,128,1152]{3,2,0,1:T(8,128)(2,1)S(1)}, u32[]{:S(2)}, u32[]{:S(2)}) collective-permute-start(bf16[2,1,128,1152]{3,2,0,1:T(8,128)(2,1)S(1)} %get-tuple-element.506), channel_id=1, source_target_pairs={{0,16},{16,32},{32,48},{48,64},{64,80},{80,96},{96,112},{112,128},... | collective-permute-start | bytes 1769480 | tf_op jit(solution)/shard_map/while/body/eval_jaxpr/ppermute | solution.py:14
  594.4 12.8 %all-to-all-start = ((bf16[2,1,128,1152]{3,0,1,2:T(2,128)(2,1)}), bf16[2,1,128,1152]{3,0,1,2:T(2,128)(2,1)S(1)}, u32[]{:S(2)}, u32[]{:S(2)}) async-start(bf16[2,1,128,1152]{3,0,1,2:T(2,128)(2,1)} %copy.60), calls=%async_computation | async-start | bytes 1179648 | tf_op jit(solution)/shard_map/while/body/eval_jaxpr/all_to_all | solution.py:75
  619.2 304.9 %collective-permute-start = (bf16[2,1,128,1152]{3,2,0,1:T(8,128)(2,1)S(1)}, bf16[2,1,128,1152]{3,2,0,1:T(8,128)(2,1)S(1)}, u32[]{:S(2)}, u32[]{:S(2)}) collective-permute-start(bf16[2,1,128,1152]{3,2,0,1:T(8,128)(2,1)S(1)} %get-tuple-element.506), channel_id=1, source_target_pairs={{0,16},{16,32},{32,48},{48,64},{64,80},{80,96},{96,112},{112,128},... | collective-permute-start | bytes 1769480 | tf_op jit(solution)/shard_map/while/body/eval_jaxpr/ppermute | solution.py:14
  940.0 12.8 %all-to-all-start = ((bf16[2,1,128,1152]{3,0,1,2:T(2,128)(2,1)}), bf16[2,1,128,1152]{3,0,1,2:T(2,128)(2,1)S(1)}, u32[]{:S(2)}, u32[]{:S(2)}) async-start(bf16[2,1,128,1152]{3,0,1,2:T(2,128)(2,1)} %copy.60), calls=%async_computation | async-start | bytes 1179648 | tf_op jit(solution)/shard_map/while/body/eval_jaxpr/all_to_all | solution.py:75
  977.2 15.8 %collective-permute-start = (bf16[2,1,128,1152]{3,2,0,1:T(8,128)(2,1)S(1)}, bf16[2,1,128,1152]{3,2,0,1:T(8,128)(2,1)S(1)}, u32[]{:S(2)}, u32[]{:S(2)}) collective-permute-start(bf16[2,1,128,1152]{3,2,0,1:T(8,128)(2,1)S(1)} %get-tuple-element.506), channel_id=1, source_target_pairs={{0,16},{16,32},{32,48},{48,64},{64,80},{80,96},{96,112},{112,128},... | collective-permute-start | bytes 1769480 | tf_op jit(solution)/shard_map/while/body/eval_jaxpr/ppermute | solution.py:14
  1008.9 12.8 %all-to-all-start = ((bf16[2,1,128,1152]{3,0,1,2:T(2,128)(2,1)}), bf16[2,1,128,1152]{3,0,1,2:T(2,128)(2,1)S(1)}, u32[]{:S(2)}, u32[]{:S(2)}) async-start(bf16[2,1,128,1152]{3,0,1,2:T(2,128)(2,1)} %copy.60), calls=%async_computation | async-start | bytes 1179648 | tf_op jit(solution)/shard_map/while/body/eval_jaxpr/all_to_all | solution.py:75
  (39 other events, 715.3 us)
where the time goes:
time: 1060 us; the launch traced here: 1050 us
  waiting for transfers between devices  741 us (70%)
  starting transfers between devices  149 us (14%)
  local copies, waits for them, and re-layouts  79 us (7%)
  other arithmetic  50.7 us (5%)
  matrix products  29.4 us (3%)
    ppermute x17, waiting for transfers between devices, passed_along(): return lax.ppermute(block, axis, route)  452 us
    all_to_all x17, waiting for transfers between devices, dispatch(): lax.all_to_all(payload, 'seq', split_axis=2, concat_axis=1, tiled=True)  159 us
    all_to_all x17, waiting for transfers between devices, advance(): lax.all_to_all(mixed, 'seq', split_axis=1, concat_axis=2, tiled=True)  130 us
    all_to_all x17, starting transfers between devices, dispatch(): lax.all_to_all(payload, 'seq', split_axis=2, concat_axis=1, tiled=True)  64.1 us
    all_to_all x17, starting transfers between devices, advance(): lax.all_to_all(mixed, 'seq', split_axis=1, concat_axis=2, tiled=True)  60.2 us
    dynamic_update_slice x17, other arithmetic, advance(): lax.dynamic_update_slice_in_dim(hidden, jnp.where(active, leaving, previo...  34.4 us
    cond x17, local copies, waits for them, and re-layouts, advance(): lax.cond(active, first_half, empty_first, incoming, factors)  24.8 us
    ppermute x17, starting transfers between devices, passed_along(): return lax.ppermute(block, axis, route)  24.2 us
  transfers between devices with their start and end apart: 51, of which 51 were waited for; matrix products, arithmetic and copies ran while one was open for 3% of the time, Pallas kernels for 0%

commit v1 on v0

v1 whole, which is shorter than its diff:
```python
import jax
import jax.numpy as jnp
from jax import lax
from jax.experimental import pallas as pl
from jax.experimental.pallas import tpu as pltpu
from jax.sharding import PartitionSpec as P

HEADS = 8
F32 = jnp.float32
BF16 = jnp.bfloat16
EPS = 1e-06


def dot(a, b):
    return lax.dot_general(a, b, (((1,), (0,)), ((), ())), preferred_element_type=F32)


def dot_t(a, b):
    return lax.dot_general(a, b, (((1,), (1,)), ((), ())), preferred_element_type=F32)


def dot_split(a, b):
    high = a.astype(BF16)
    low = (a - high.astype(F32)).astype(BF16)
    return dot(high, b) + dot(low, b)


def norm_modulate(x, offset, scaling):
    average = jnp.mean(x, axis=-1, keepdims=True)
    centered = x - average
    variance = jnp.mean(centered * centered, axis=-1, keepdims=True)
    return (centered * lax.rsqrt(variance + EPS) * (1.0 + scaling) + offset).astype(BF16)


def head_rms(t, members, members_t, width):
    square = dot_split(t * t, members) * (1.0 / width)
    return (t * dot_split(lax.rsqrt(square + EPS), members_t)).astype(BF16)


def in_head(shape, axis, start, head, width):
    at = lax.broadcasted_iota(jnp.int32, shape, axis) + start
    return jnp.logical_and(at >= head * width, at < (head + 1) * width)


def attention(projected, patches):
    tokens, total_width = projected.shape
    hw = total_width // 3
    width = hw // HEADS
    row = lax.broadcasted_iota(jnp.int32, (hw, 128), 0)
    col = lax.broadcasted_iota(jnp.int32, (hw, 128), 1) * width
    members = jnp.where(jnp.logical_and(row >= col, row < col + width), 1.0, 0.0).astype(BF16)
    row = lax.broadcasted_iota(jnp.int32, (128, hw), 0) * width
    col = lax.broadcasted_iota(jnp.int32, (128, hw), 1)
    members_t = jnp.where(jnp.logical_and(col >= row, col < row + width), 1.0, 0.0).astype(BF16)
    queries = head_rms(projected[:, :hw], members, members_t, width)
    lookups = head_rms(projected[:, hw : 2 * hw], members, members_t, width)
    values = projected[:, 2 * hw :].astype(BF16)
    scale = width**-0.5
    if patches:
        r = lax.broadcasted_iota(jnp.int32, (tokens, tokens), 0) % patches
        c = lax.broadcasted_iota(jnp.int32, (tokens, tokens), 1) % patches
        same = r == c
    tiles = [None] * (-(-hw // 128))
    for head in range(HEADS):
        first = head * width // 128
        last = ((head + 1) * width - 1) // 128
        start, stop = first * 128, min((last + 1) * 128, hw)
        mine = in_head((1, stop - start), 1, start, head, width)
        window = jnp.where(mine, queries[:, start:stop], jnp.zeros((), BF16))
        e = jnp.exp(dot_t(window, lookups[:, start:stop]) * scale)
        if patches:
            e = jnp.where(same, e, 0.0)
        inverse = 1.0 / jnp.sum(e, axis=-1, keepdims=True)
        mixed = dot(e.astype(BF16), values[:, start:stop]) * inverse
        for tile in range(first, last + 1):
            begin, end = tile * 128, min(tile * 128 + 128, hw)
            own = in_head((1, end - begin), 1, begin, head, width)
            part = mixed[:, begin - start : end - start]
            base = 0.0 if tiles[tile] is None else tiles[tile]
            tiles[tile] = jnp.where(own, part, base)
    return jnp.concatenate(tiles, axis=1).astype(BF16)


def start_either(flag, mine, other, target, sem):
    @pl.when(flag == 0)
    def _():
        pltpu.make_async_copy(mine, target, sem).start()

    @pl.when(flag != 0)
    def _():
        pltpu.make_async_copy(other, target, sem).start()


def factors_of(flag, video, mine, other):
    return jnp.where(flag == 0, mine[0, video], other[0, video])


def spatial_part(x, factors, qkv, out, waits):
    normed = norm_modulate(x, factors[0:1], factors[1:2])
    waits[0].wait()
    mixed = attention(dot(normed, qkv[...]), 0)
    waits[1].wait()
    y = x + factors[2:3] * dot(mixed, out[...])
    return y, norm_modulate(y, factors[3:4], factors[4:5])


def head_kernel(flags, frames, arriving, mod, mod2, qkv, qkv2, out, out2, y, g, x_v, qkv_v, out_v, sems):
    pick, video = flags[0], flags[1]
    start_either(flags[2], frames.at[video], arriving, x_v, sems.at[0])
    start_either(pick, qkv.at[0], qkv2.at[0], qkv_v, sems.at[1])
    start_either(pick, out.at[0], out2.at[0], out_v, sems.at[2])
    wq = pltpu.make_async_copy(qkv.at[0], qkv_v, sems.at[1])
    wo = pltpu.make_async_copy(out.at[0], out_v, sems.at[2])
    factors = factors_of(pick, video, mod, mod2)
    pltpu.make_async_copy(arriving, x_v, sems.at[0]).wait()
    y[...], g[...] = spatial_part(x_v[...].astype(F32), factors, qkv_v, out_v, (wq, wo))


def temporal_kernel(flags, arrived, qkv, qkv2, mixed, qkv_v, sems):
    start_either(flags[0], qkv.at[0], qkv2.at[0], qkv_v, sems.at[0])
    h = arrived[...]
    pltpu.make_async_copy(qkv.at[0], qkv_v, sems.at[0]).wait()
    mixed[...] = attention(dot(h, qkv_v[...]), 8)


def joint_kernel(
    flags, returned, y_in, mod, mod2, tout, tout2, qkv, qkv2, out, out2,
    x, y, g, tout_v, qkv_v, out_v, sems,
):
    pick, video = flags[0], flags[1]
    start_either(pick, tout.at[0], tout2.at[0], tout_v, sems.at[0])
    start_either(1 - pick, qkv.at[0], qkv2.at[0], qkv_v, sems.at[1])
    start_either(1 - pick, out.at[0], out2.at[0], out_v, sems.at[2])
    wq = pltpu.make_async_copy(qkv.at[0], qkv_v, sems.at[1])
    wo = pltpu.make_async_copy(out.at[0], out_v, sems.at[2])
    factors = factors_of(pick, video, mod, mod2)
    following = factors_of(1 - pick, video, mod, mod2)
    pltpu.make_async_copy(tout.at[0], tout_v, sems.at[0]).wait()
    leaving = (y_in[...] + factors[5:6] * dot(returned[...], tout_v[...])).astype(BF16)
    x[...] = leaving
    y[...], g[...] = spatial_part(leaving.astype(F32), following, qkv_v, out_v, (wq, wo))


def tail_kernel(flags, returned, y_in, mod, mod2, tout, tout2, x, tout_v, sems):
    pick, video = flags[0], flags[1]
    start_either(pick, tout.at[0], tout2.at[0], tout_v, sems.at[0])
    factors = factors_of(pick, video, mod, mod2)
    pltpu.make_async_copy(tout.at[0], tout_v, sems.at[0]).wait()
    x[...] = (y_in[...] + factors[5:6] * dot(returned[...], tout_v[...])).astype(BF16)


SMEM = pl.BlockSpec(memory_space=pltpu.SMEM)
VMEM = pl.BlockSpec(memory_space=pltpu.VMEM)
ANY = pl.BlockSpec(memory_space=pl.ANY)


def call(kernel, name, ins, outs, scratch, sems):
    return pl.pallas_call(
        kernel,
        name=name,
        in_specs=ins,
        out_specs=[VMEM] * len(outs),
        out_shape=outs,
        scratch_shapes=scratch + [pltpu.SemaphoreType.DMA((sems,))],
        compiler_params=pltpu.CompilerParams(vmem_limit_bytes=40 * 2**20),
    )


def on_device(frames_in, spatial_qkv, spatial_out, temporal_qkv, temporal_out, modulation):
    videos, frames, patches, model = frames_in.shape
    wide, hw = spatial_qkv.shape[2], spatial_out.shape[1]
    per_core = videos // 2
    sections = lax.axis_size("section")
    ranks = lax.axis_size("seq")
    stages = sections // 2
    section = lax.axis_index("section")
    stage, core = section // 2, section % 2
    tokens = frames * patches
    share = patches // ranks

    def swapped(a):
        return lax.ppermute(a, "section", [(i, i ^ 1) for i in range(sections)])

    mod2 = swapped(modulation)
    sqkv, sqkv2 = spatial_qkv, swapped(spatial_qkv)
    sout, sout2 = spatial_out, swapped(spatial_out)
    tqkv, tqkv2 = temporal_qkv, swapped(temporal_qkv)
    tout, tout2 = temporal_out, swapped(temporal_out)
    mod = modulation
    source = frames_in.reshape(videos, tokens, model)

    x_s = jax.ShapeDtypeStruct((tokens, model), BF16)
    y_s = jax.ShapeDtypeStruct((tokens, model), F32)
    mixed_s = jax.ShapeDtypeStruct((tokens, hw), BF16)
    w_qkv = pltpu.VMEM((model, wide), BF16)
    w_out = pltpu.VMEM((hw, model), BF16)
    head = call(
        head_kernel, "head", [SMEM, ANY, ANY, VMEM, VMEM, ANY, ANY, ANY, ANY], [y_s, x_s],
        [pltpu.VMEM((tokens, model), BF16), w_qkv, w_out], 3,
    )
    temporal = call(temporal_kernel, "temporal", [SMEM, VMEM, ANY, ANY], [mixed_s], [w_qkv], 1)
    joint = call(
        joint_kernel, "joint", [SMEM, VMEM, VMEM, VMEM, VMEM] + [ANY] * 6, [x_s, y_s, x_s],
        [w_out, w_qkv, w_out], 3,
    )
    tail = call(tail_kernel, "tail", [SMEM, VMEM, VMEM, VMEM, VMEM, ANY, ANY], [x_s], [w_out], 1)

    def exchange(a):
        out = lax.all_to_all(a.reshape(ranks, share, a.shape[1]), "seq", 0, 0, tiled=True)
        return out.reshape(a.shape)

    def advance(step, carried):
        even, odd, arriving = carried
        micro = step - stage
        active = jnp.logical_and(micro >= 0, micro < per_core)
        clipped = jnp.clip(micro, 0, per_core - 1)
        slot = jnp.where(active, clipped, per_core)
        video = core * per_core + clipped
        later = jnp.where(stage == 0, 0, 1)
        first = jnp.stack([core, video, later]).astype(jnp.int32)
        second = jnp.stack([1 - core, video, later]).astype(jnp.int32)
        y, g = head(first, source, arriving, mod, mod2, sqkv, sqkv2, sout, sout2)
        (mixed,) = temporal(first, exchange(g), tqkv, tqkv2)
        x, y, g = joint(
            first, exchange(mixed), y, mod, mod2, tout, tout2, sqkv, sqkv2, sout, sout2
        )
        even = lax.dynamic_update_slice_in_dim(even, x[None], slot, 0)
        (mixed,) = temporal(second, exchange(g), tqkv, tqkv2)
        (x,) = tail(second, exchange(mixed), y, mod, mod2, tout, tout2)
        arriving = lax.ppermute(x, "section", [(i, i + 2) for i in range(sections - 2)])
        odd = lax.dynamic_update_slice_in_dim(odd, x[None], slot, 0)
        return even, odd, arriving

    kept = jnp.zeros((per_core + 1, tokens, model), BF16)
    even, odd, _ = lax.fori_loop(
        0, stages + per_core - 1, advance, (kept, kept, jnp.zeros((tokens, model), BF16))
    )
    even, odd = even[:per_core], odd[:per_core]
    own = jnp.where(core == 0, even, odd)
    other = swapped(jnp.where(core == 0, odd, even))
    low, high = jnp.where(core == 0, own, other), jnp.where(core == 0, other, own)
    hidden = jnp.concatenate([low, high], axis=0)
    return hidden.reshape((1,) + frames_in.shape)


def solution(mesh):
    placed = (
        P(None, "seq", None, None),
        P("section", None, None),
        P("section", None, None),
        P("section", None, None),
        P("section", None, None),
        P("section", None, None, None),
    )
    return jax.shard_map(
        on_device,
        mesh=mesh,
        in_specs=placed,
        out_specs=P("section", None, "seq", None, None),
        check_vma=False,
    )
```

time: 1060 us -> 796 us (0.75)
  waiting for transfers between devices: 741 us -> 247 us
  Pallas kernels: 0 us -> 168 us
  blocking collectives: 0 us -> 100 us
  other arithmetic: 50.7 us -> 4.1 us
  matrix products: 29.4 us -> 0 us
  local copies, waits for them, and re-layouts: 79 us -> 98.8 us
  starting transfers between devices: 149 us -> 166 us
    ppermute x17 -> x15, waiting for transfers between devices: 452 us -> 57.3 us  [the longest x9 55.6 us: advance(): lax.ppermute(x, 'section', [(i, i + 2) for i in range(sections - 2)])]
    pallas_call x0 -> x36, Pallas kernels: none -> 168 us  [the longest x9 56.3 us: advance(): y, g = head(first, source, arriving, mod, mod2, sqkv, sqkv2, sout, sout2)]
    all_to_all x0 -> x9, blocking collectives: none -> 100 us  [exchange(): lax.all_to_all(a.reshape(ranks, share, a.shape[1]), 'seq', 0, 0, tiled=True)]
    all_to_all x34 -> x27, waiting for transfers between devices: 289 us -> 190 us  [exchange(): lax.all_to_all(a.reshape(ranks, share, a.shape[1]), 'seq', 0, 0, tiled=True)]
    pallas_call x0 -> x9, local copies, waits for them, and re-layouts: none -> 63.4 us  [advance(): joint(first, exchange(mixed), y, mod, mod2, tout, tout2, sqkv, sqkv2, sou...]
    ppermute x17 -> x15, starting transfers between devices: 24.2 us -> 69.9 us  [the longest x6 58.3 us: swapped(): return lax.ppermute(a, 'section', [(i, i ^ 1) for i in range(sections)])]
    cond x38 -> x0, local copies, waits for them, and re-layouts: 38.8 us -> none  [the longest x17 24.8 us: advance(): lax.cond(active, first_half, empty_first, incoming, factors)]
    dynamic_update_slice x17 -> x0, other arithmetic: 34.4 us -> none  [advance(): lax.dynamic_update_slice_in_dim(hidden, jnp.where(active, leaving, previo...]
  transfers between devices with their start and end apart: 51 -> 42, of which waited for: 51 -> 37; matrix products, arithmetic and copies ran while one was open for 3% -> 4% of each run, Pallas kernels for 0% -> 0%
where the time goes in v1:
time: 796 us; the launch traced here: 785 us
  waiting for transfers between devices  247 us (31%)
  Pallas kernels  168 us (21%)
  starting transfers between devices  166 us (21%)
  blocking collectives  100 us (13%)
  local copies, waits for them, and re-layouts  98.8 us (12%)
    all_to_all x27, waiting for transfers between devices, exchange(): lax.all_to_all(a.reshape(ranks, share, a.shape[1]), 'seq', 0, 0, tiled=True)  190 us
    all_to_all x9, blocking collectives, exchange(): lax.all_to_all(a.reshape(ranks, share, a.shape[1]), 'seq', 0, 0, tiled=True)  100 us
    all_to_all x27, starting transfers between devices, exchange(): lax.all_to_all(a.reshape(ranks, share, a.shape[1]), 'seq', 0, 0, tiled=True)  96.5 us
    pallas_call x9, local copies, waits for them, and re-layouts, advance(): joint(first, exchange(mixed), y, mod, mod2, tout, tout2, sqkv, sqkv2, sou...  63.4 us
    ppermute x6, starting transfers between devices, swapped(): return lax.ppermute(a, 'section', [(i, i ^ 1) for i in range(sections)])  58.3 us
    pallas_call x9, Pallas kernels, advance(): y, g = head(first, source, arriving, mod, mod2, sqkv, sqkv2, sout, sout2)  56.3 us
    ppermute x9, waiting for transfers between devices, advance(): lax.ppermute(x, 'section', [(i, i + 2) for i in range(sections - 2)])  55.6 us
    pallas_call x9, Pallas kernels, advance(): mixed, = temporal(second, exchange(g), tqkv, tqkv2)  52.8 us
  transfers between devices with their start and end apart: 42, of which 37 were waited for; matrix products, arithmetic and copies ran while one was open for 4% of the time, Pallas kernels for 0%

profile of v1, /device:TPU:225, one launch (start us, length us, event | category | flops | bytes accessed | tf_op | source)
XLA Modules:
  0.0 785.3 jit_solution(1470595234339965613)
XLA Ops:
  30.4 694.0 %while.19 = (s32[]{:T(128)}, bf16[3,128,1152]{2,1,0:T(8,128)(2,1)}, bf16[3,128,1152]{2,1,0:T(8,128)(2,1)}, bf16[128,1152]{1,0:T(8,128)(2,1)S(1)}, s32[]{:T(128)}...) while((s32[]{:T(128)}, bf16[3,128,1152]{2,1,0:T(8,128)(2,1)}, ...), condition=%wide.region_1.2_spmd, body=%wide.region_0.1_spmd.sunk | while | flops 22 | bytes 51749412 | solution.py:235
  37.0 14.6 %all_to_all.48 = bf16[16,8,1152]{2,1,0:T(8,128)(2,1)S(1)} all-to-all(bf16[16,8,1152]{2,1,0:T(8,128)(2,1)S(1)} %bitcast.50), channel_id=1, replica_groups=mesh['section'=16,'seq'=16] {'seq'}, dimensions={0} | all-to-all | bytes 589824 | tf_op jit(solution)/shard_map/while/body/eval_jaxpr/all_to_all | solution.py:209
  66.6 7.0 joint.8
  77.4 7.5 all-to-all-done.2
  117.3 10.7 %all_to_all.48 = bf16[16,8,1152]{2,1,0:T(8,128)(2,1)S(1)} all-to-all(bf16[16,8,1152]{2,1,0:T(8,128)(2,1)S(1)} %bitcast.50), channel_id=1, replica_groups=mesh['section'=16,'seq'=16] {'seq'}, dimensions={0} | all-to-all | bytes 589824 | tf_op jit(solution)/shard_map/while/body/eval_jaxpr/all_to_all | solution.py:209
  142.6 7.1 joint.8
  153.3 7.4 all-to-all-done.2
  193.2 10.7 %all_to_all.48 = bf16[16,8,1152]{2,1,0:T(8,128)(2,1)S(1)} all-to-all(bf16[16,8,1152]{2,1,0:T(8,128)(2,1)S(1)} %bitcast.50), channel_id=1, replica_groups=mesh['section'=16,'seq'=16] {'seq'}, dimensions={0} | all-to-all | bytes 589824 | tf_op jit(solution)/shard_map/while/body/eval_jaxpr/all_to_all | solution.py:209
  218.5 7.0 joint.8
  229.2 7.4 all-to-all-done.2
  246.0 7.2 all-to-all-done.3
  269.2 10.6 %all_to_all.48 = bf16[16,8,1152]{2,1,0:T(8,128)(2,1)S(1)} all-to-all(bf16[16,8,1152]{2,1,0:T(8,128)(2,1)S(1)} %bitcast.50), channel_id=1, replica_groups=mesh['section'=16,'seq'=16] {'seq'}, dimensions={0} | all-to-all | bytes 589824 | tf_op jit(solution)/shard_map/while/body/eval_jaxpr/all_to_all | solution.py:209
  294.4 7.1 joint.8
  305.1 7.4 all-to-all-done.2
  345.0 10.7 %all_to_all.48 = bf16[16,8,1152]{2,1,0:T(8,128)(2,1)S(1)} all-to-all(bf16[16,8,1152]{2,1,0:T(8,128)(2,1)S(1)} %bitcast.50), channel_id=1, replica_groups=mesh['section'=16,'seq'=16] {'seq'}, dimensions={0} | all-to-all | bytes 589824 | tf_op jit(solution)/shard_map/while/body/eval_jaxpr/all_to_all | solution.py:209
  370.2 7.1 joint.8
  380.9 7.4 all-to-all-done.2
  421.2 10.7 %all_to_all.48 = bf16[16,8,1152]{2,1,0:T(8,128)(2,1)S(1)} all-to-all(bf16[16,8,1152]{2,1,0:T(8,128)(2,1)S(1)} %bitcast.50), channel_id=1, replica_groups=mesh['section'=16,'seq'=16] {'seq'}, dimensions={0} | all-to-all | bytes 589824 | tf_op jit(solution)/shard_map/while/body/eval_jaxpr/all_to_all | solution.py:209
  446.6 7.1 joint.8
  457.3 8.1 %all-to-all-done.2 = bf16[16,8,1152]{2,1,0:T(8,128)(2,1)S(1)} async-done(((bf16[16,8,1152]{2,1,0:T(8,128)(2,1)}), bf16[16,8,1152]{2,1,0:T(8,128)(2,1)S(1)}, u32[]{:S(2)}, u32[]{:S(2)}) %all-to-all-start.2) | async-done | bytes 294944 | tf_op jit(solution)/shard_map/while/body/eval_jaxpr/all_to_all | solution.py:209
  498.7 10.7 %all_to_all.48 = bf16[16,8,1152]{2,1,0:T(8,128)(2,1)S(1)} all-to-all(bf16[16,8,1152]{2,1,0:T(8,128)(2,1)S(1)} %bitcast.50), channel_id=1, replica_groups=mesh['section'=16,'seq'=16] {'seq'}, dimensions={0} | all-to-all | bytes 589824 | tf_op jit(solution)/shard_map/while/body/eval_jaxpr/all_to_all | solution.py:209
  523.9 7.1 joint.8
  534.6 7.4 all-to-all-done.2
  575.8 10.7 %all_to_all.48 = bf16[16,8,1152]{2,1,0:T(8,128)(2,1)S(1)} all-to-all(bf16[16,8,1152]{2,1,0:T(8,128)(2,1)S(1)} %bitcast.50), channel_id=1, replica_groups=mesh['section'=16,'seq'=16] {'seq'}, dimensions={0} | all-to-all | bytes 589824 | tf_op jit(solution)/shard_map/while/body/eval_jaxpr/all_to_all | solution.py:209
  601.1 7.0 joint.8
  611.8 7.4 all-to-all-done.2
  639.6 7.4 collective-permute-done
  653.4 10.7 %all_to_all.48 = bf16[16,8,1152]{2,1,0:T(8,128)(2,1)S(1)} all-to-all(bf16[16,8,1152]{2,1,0:T(8,128)(2,1)S(1)} %bitcast.50), channel_id=1, replica_groups=mesh['section'=16,'seq'=16] {'seq'}, dimensions={0} | all-to-all | bytes 589824 | tf_op jit(solution)/shard_map/while/body/eval_jaxpr/all_to_all | solution.py:209
  678.9 7.1 joint.8
  689.6 7.4 all-to-all-done.2
  706.4 6.9 all-to-all-done.3
  725.9 56.5 %collective-permute-start.6 = (bf16[2,128,1152]{2,1,0:T(8,128)(2,1)S(1)}, bf16[2,128,1152]{2,1,0:T(8,128)(2,1)S(1)}, u32[]{:S(2)}, u32[]{:S(2)}) collective-permute-start(bf16[2,128,1152]{2,1,0:T(8,128)(2,1)S(1)} %broadcast_select_fusion.2), channel_id=1, source_target_pairs={{0,16},{16,0},{32,48},{48,32},{64,80},{80,64},{96,112},{112,96},{1... | collective-permute-start | bytes 1769480 | tf_op jit(solution)/shard_map/ppermute | solution.py:182
  (187 shorter events, 475.4 us)
Async XLA Ops:
  0.0 15.5 %collective-permute-start.2 = (bf16[1,1152,1728]{1,2,0:T(8,128)(2,1)}, bf16[1,1152,1728]{1,2,0:T(8,128)(2,1)}, u32[]{:S(2)}, u32[]{:S(2)}) collective-permute-start(bf16[1,1152,1728]{1,2,0:T(8,128)(2,1)} %param.9), channel_id=1, source_target_pairs={{0,16},{16,0},{32,48},{48,32},{64,80},{80,64},{96,112},{112,96},{1... | collective-permute-start | bytes 11943944 | tf_op jit(solution)/shard_map/ppermute | solution.py:182
  0.7 21.3 %collective-permute-start.4 = (bf16[1,1152,1728]{1,2,0:T(8,128)(2,1)}, bf16[1,1152,1728]{1,2,0:T(8,128)(2,1)}, u32[]{:S(2)}, u32[]{:S(2)}) collective-permute-start(bf16[1,1152,1728]{1,2,0:T(8,128)(2,1)} %param.11), channel_id=1, source_target_pairs={{0,16},{16,0},{32,48},{48,32},{64,80},{80,64},{96,112},{112,96},{1... | collective-permute-start | bytes 11943944 | tf_op jit(solution)/shard_map/ppermute | solution.py:182
  0.7 27.7 %collective-permute-start.3 = (bf16[1,576,1152]{2,1,0:T(8,128)(2,1)}, bf16[1,576,1152]{2,1,0:T(8,128)(2,1)}, u32[]{:S(2)}, u32[]{:S(2)}) collective-permute-start(bf16[1,576,1152]{2,1,0:T(8,128)(2,1)} %param.10), channel_id=1, source_target_pairs={{0,16},{16,0},{32,48},{48,32},{64,80},{80,64},{96,112},{112,96},{1... | collective-permute-start | bytes 3981320 | tf_op jit(solution)/shard_map/ppermute | solution.py:182
  1.2 27.2 %collective-permute-start.5 = (bf16[1,576,1152]{2,1,0:T(8,128)(2,1)}, bf16[1,576,1152]{2,1,0:T(8,128)(2,1)}, u32[]{:S(2)}, u32[]{:S(2)}) collective-permute-start(bf16[1,576,1152]{2,1,0:T(8,128)(2,1)} %param.12), channel_id=1, source_target_pairs={{0,16},{16,0},{32,48},{48,32},{64,80},{80,64},{96,112},{112,96},{1... | collective-permute-start | bytes 3981320 | tf_op jit(solution)/shard_map/ppermute | solution.py:182
  2.1 26.3 %collective-permute-start.1 = (f32[1,4,6,1152]{3,2,1,0:T(8,128)S(1)}, f32[1,4,6,1152]{3,2,1,0:T(8,128)S(1)}, u32[]{:S(2)}, u32[]{:S(2)}) collective-permute-start(f32[1,4,6,1152]{3,2,1,0:T(8,128)S(1)} %copy.14), channel_id=1, source_target_pairs={{0,16},{16,0},{32,48},{48,32},{64,80},{80,64},{96,112},{112,96},{1... | collective-permute-start | bytes 331784 | tf_op jit(solution)/shard_map/ppermute | solution.py:182
  55.8 10.8 %all-to-all-start.1 = ((bf16[16,8,576]{2,1,0:T(8,128)(2,1)}), bf16[16,8,576]{2,1,0:T(8,128)(2,1)S(1)}, u32[]{:S(2)}, u32[]{:S(2)}) async-start(bf16[16,8,576]{2,1,0:T(8,128)(2,1)} %bitcast.40), calls=%async_computation.1 | async-start | bytes 327680 | tf_op jit(solution)/shard_map/while/body/eval_jaxpr/all_to_all | solution.py:209
  73.6 11.3 %all-to-all-start.2 = ((bf16[16,8,1152]{2,1,0:T(8,128)(2,1)}), bf16[16,8,1152]{2,1,0:T(8,128)(2,1)S(1)}, u32[]{:S(2)}, u32[]{:S(2)}) async-start(bf16[16,8,1152]{2,1,0:T(8,128)(2,1)} %bitcast.43), calls=%async_computation.2 | async-start | bytes 589824 | tf_op jit(solution)/shard_map/while/body/eval_jaxpr/all_to_all | solution.py:209
  90.8 10.4 %all-to-all-start.3 = ((bf16[16,8,576]{2,1,0:T(8,128)(2,1)}), bf16[16,8,576]{2,1,0:T(8,128)(2,1)S(1)}, u32[]{:S(2)}, u32[]{:S(2)}) async-start(bf16[16,8,576]{2,1,0:T(8,128)(2,1)} %bitcast.45), calls=%async_computation.3 | async-start | bytes 327680 | tf_op jit(solution)/shard_map/while/body/eval_jaxpr/all_to_all | solution.py:209
  132.3 10.3 %all-to-all-start.1 = ((bf16[16,8,576]{2,1,0:T(8,128)(2,1)}), bf16[16,8,576]{2,1,0:T(8,128)(2,1)S(1)}, u32[]{:S(2)}, u32[]{:S(2)}) async-start(bf16[16,8,576]{2,1,0:T(8,128)(2,1)} %bitcast.40), calls=%async_computation.1 | async-start | bytes 327680 | tf_op jit(solution)/shard_map/while/body/eval_jaxpr/all_to_all | solution.py:209
  149.6 11.0 %all-to-all-start.2 = ((bf16[16,8,1152]{2,1,0:T(8,128)(2,1)}), bf16[16,8,1152]{2,1,0:T(8,128)(2,1)S(1)}, u32[]{:S(2)}, u32[]{:S(2)}) async-start(bf16[16,8,1152]{2,1,0:T(8,128)(2,1)} %bitcast.43), calls=%async_computation.2 | async-start | bytes 589824 | tf_op jit(solution)/shard_map/while/body/eval_jaxpr/all_to_all | solution.py:209
  166.5 10.3 %all-to-all-start.3 = ((bf16[16,8,576]{2,1,0:T(8,128)(2,1)}), bf16[16,8,576]{2,1,0:T(8,128)(2,1)S(1)}, u32[]{:S(2)}, u32[]{:S(2)}) async-start(bf16[16,8,576]{2,1,0:T(8,128)(2,1)} %bitcast.45), calls=%async_computation.3 | async-start | bytes 327680 | tf_op jit(solution)/shard_map/while/body/eval_jaxpr/all_to_all | solution.py:209
  208.2 10.3 %all-to-all-start.1 = ((bf16[16,8,576]{2,1,0:T(8,128)(2,1)}), bf16[16,8,576]{2,1,0:T(8,128)(2,1)S(1)}, u32[]{:S(2)}, u32[]{:S(2)}) async-start(bf16[16,8,576]{2,1,0:T(8,128)(2,1)} %bitcast.40), calls=%async_computation.1 | async-start | bytes 327680 | tf_op jit(solution)/shard_map/while/body/eval_jaxpr/all_to_all | solution.py:209
  225.5 11.0 %all-to-all-start.2 = ((bf16[16,8,1152]{2,1,0:T(8,128)(2,1)}), bf16[16,8,1152]{2,1,0:T(8,128)(2,1)S(1)}, u32[]{:S(2)}, u32[]{:S(2)}) async-start(bf16[16,8,1152]{2,1,0:T(8,128)(2,1)} %bitcast.43), calls=%async_computation.2 | async-start | bytes 589824 | tf_op jit(solution)/shard_map/while/body/eval_jaxpr/all_to_all | solution.py:209
  242.4 10.7 %all-to-all-start.3 = ((bf16[16,8,576]{2,1,0:T(8,128)(2,1)}), bf16[16,8,576]{2,1,0:T(8,128)(2,1)S(1)}, u32[]{:S(2)}, u32[]{:S(2)}) async-start(bf16[16,8,576]{2,1,0:T(8,128)(2,1)} %bitcast.45), calls=%async_computation.3 | async-start | bytes 327680 | tf_op jit(solution)/shard_map/while/body/eval_jaxpr/all_to_all | solution.py:209
  301.5 11.0 %all-to-all-start.2 = ((bf16[16,8,1152]{2,1,0:T(8,128)(2,1)}), bf16[16,8,1152]{2,1,0:T(8,128)(2,1)S(1)}, u32[]{:S(2)}, u32[]{:S(2)}) async-start(bf16[16,8,1152]{2,1,0:T(8,128)(2,1)} %bitcast.43), calls=%async_computation.2 | async-start | bytes 589824 | tf_op jit(solution)/shard_map/while/body/eval_jaxpr/all_to_all | solution.py:209
  318.4 10.5 %all-to-all-start.3 = ((bf16[16,8,576]{2,1,0:T(8,128)(2,1)}), bf16[16,8,576]{2,1,0:T(8,128)(2,1)S(1)}, u32[]{:S(2)}, u32[]{:S(2)}) async-start(bf16[16,8,576]{2,1,0:T(8,128)(2,1)} %bitcast.45), calls=%async_computation.3 | async-start | bytes 327680 | tf_op jit(solution)/shard_map/while/body/eval_jaxpr/all_to_all | solution.py:209
  359.9 10.3 %all-to-all-start.1 = ((bf16[16,8,576]{2,1,0:T(8,128)(2,1)}), bf16[16,8,576]{2,1,0:T(8,128)(2,1)S(1)}, u32[]{:S(2)}, u32[]{:S(2)}) async-start(bf16[16,8,576]{2,1,0:T(8,128)(2,1)} %bitcast.40), calls=%async_computation.1 | async-start | bytes 327680 | tf_op jit(solution)/shard_map/while/body/eval_jaxpr/all_to_all | solution.py:209
  377.3 11.0 %all-to-all-start.2 = ((bf16[16,8,1152]{2,1,0:T(8,128)(2,1)}), bf16[16,8,1152]{2,1,0:T(8,128)(2,1)S(1)}, u32[]{:S(2)}, u32[]{:S(2)}) async-start(bf16[16,8,1152]{2,1,0:T(8,128)(2,1)} %bitcast.43), calls=%async_computation.2 | async-start | bytes 589824 | tf_op jit(solution)/shard_map/while/body/eval_jaxpr/all_to_all | solution.py:209
  394.2 10.3 %all-to-all-start.3 = ((bf16[16,8,576]{2,1,0:T(8,128)(2,1)}), bf16[16,8,576]{2,1,0:T(8,128)(2,1)S(1)}, u32[]{:S(2)}, u32[]{:S(2)}) async-start(bf16[16,8,576]{2,1,0:T(8,128)(2,1)} %bitcast.45), calls=%async_computation.3 | async-start | bytes 327680 | tf_op jit(solution)/shard_map/while/body/eval_jaxpr/all_to_all | solution.py:209
  436.1 10.5 %all-to-all-start.1 = ((bf16[16,8,576]{2,1,0:T(8,128)(2,1)}), bf16[16,8,576]{2,1,0:T(8,128)(2,1)S(1)}, u32[]{:S(2)}, u32[]{:S(2)}) async-start(bf16[16,8,576]{2,1,0:T(8,128)(2,1)} %bitcast.40), calls=%async_computation.1 | async-start | bytes 327680 | tf_op jit(solution)/shard_map/while/body/eval_jaxpr/all_to_all | solution.py:209
  453.7 11.7 %all-to-all-start.2 = ((bf16[16,8,1152]{2,1,0:T(8,128)(2,1)}), bf16[16,8,1152]{2,1,0:T(8,128)(2,1)S(1)}, u32[]{:S(2)}, u32[]{:S(2)}) async-start(bf16[16,8,1152]{2,1,0:T(8,128)(2,1)} %bitcast.43), calls=%async_computation.2 | async-start | bytes 589824 | tf_op jit(solution)/shard_map/while/body/eval_jaxpr/all_to_all | solution.py:209
  471.2 10.4 %all-to-all-start.3 = ((bf16[16,8,576]{2,1,0:T(8,128)(2,1)}), bf16[16,8,576]{2,1,0:T(8,128)(2,1)S(1)}, u32[]{:S(2)}, u32[]{:S(2)}) async-start(bf16[16,8,576]{2,1,0:T(8,128)(2,1)} %bitcast.45), calls=%async_computation.3 | async-start | bytes 327680 | tf_op jit(solution)/shard_map/while/body/eval_jaxpr/all_to_all | solution.py:209
  513.6 10.3 %all-to-all-start.1 = ((bf16[16,8,576]{2,1,0:T(8,128)(2,1)}), bf16[16,8,576]{2,1,0:T(8,128)(2,1)S(1)}, u32[]{:S(2)}, u32[]{:S(2)}) async-start(bf16[16,8,576]{2,1,0:T(8,128)(2,1)} %bitcast.40), calls=%async_computation.1 | async-start | bytes 327680 | tf_op jit(solution)/shard_map/while/body/eval_jaxpr/all_to_all | solution.py:209
  531.0 11.0 %all-to-all-start.2 = ((bf16[16,8,1152]{2,1,0:T(8,128)(2,1)}), bf16[16,8,1152]{2,1,0:T(8,128)(2,1)S(1)}, u32[]{:S(2)}, u32[]{:S(2)}) async-start(bf16[16,8,1152]{2,1,0:T(8,128)(2,1)} %bitcast.43), calls=%async_computation.2 | async-start | bytes 589824 | tf_op jit(solution)/shard_map/while/body/eval_jaxpr/all_to_all | solution.py:209
  547.9 10.3 %all-to-all-start.3 = ((bf16[16,8,576]{2,1,0:T(8,128)(2,1)}), bf16[16,8,576]{2,1,0:T(8,128)(2,1)S(1)}, u32[]{:S(2)}, u32[]{:S(2)}) async-start(bf16[16,8,576]{2,1,0:T(8,128)(2,1)} %bitcast.45), calls=%async_computation.3 | async-start | bytes 327680 | tf_op jit(solution)/shard_map/while/body/eval_jaxpr/all_to_all | solution.py:209
  590.8 10.3 %all-to-all-start.1 = ((bf16[16,8,576]{2,1,0:T(8,128)(2,1)}), bf16[16,8,576]{2,1,0:T(8,128)(2,1)S(1)}, u32[]{:S(2)}, u32[]{:S(2)}) async-start(bf16[16,8,576]{2,1,0:T(8,128)(2,1)} %bitcast.40), calls=%async_computation.1 | async-start | bytes 327680 | tf_op jit(solution)/shard_map/while/body/eval_jaxpr/all_to_all | solution.py:209
  608.1 11.0 %all-to-all-start.2 = ((bf16[16,8,1152]{2,1,0:T(8,128)(2,1)}), bf16[16,8,1152]{2,1,0:T(8,128)(2,1)S(1)}, u32[]{:S(2)}, u32[]{:S(2)}) async-start(bf16[16,8,1152]{2,1,0:T(8,128)(2,1)} %bitcast.43), calls=%async_computation.2 | async-start | bytes 589824 | tf_op jit(solution)/shard_map/while/body/eval_jaxpr/all_to_all | solution.py:209
  625.0 10.3 %all-to-all-start.3 = ((bf16[16,8,576]{2,1,0:T(8,128)(2,1)}), bf16[16,8,576]{2,1,0:T(8,128)(2,1)S(1)}, u32[]{:S(2)}, u32[]{:S(2)}) async-start(bf16[16,8,576]{2,1,0:T(8,128)(2,1)} %bitcast.45), calls=%async_computation.3 | async-start | bytes 327680 | tf_op jit(solution)/shard_map/while/body/eval_jaxpr/all_to_all | solution.py:209
  668.4 10.5 %all-to-all-start.1 = ((bf16[16,8,576]{2,1,0:T(8,128)(2,1)}), bf16[16,8,576]{2,1,0:T(8,128)(2,1)S(1)}, u32[]{:S(2)}, u32[]{:S(2)}) async-start(bf16[16,8,576]{2,1,0:T(8,128)(2,1)} %bitcast.40), calls=%async_computation.1 | async-start | bytes 327680 | tf_op jit(solution)/shard_map/while/body/eval_jaxpr/all_to_all | solution.py:209
  685.9 11.0 %all-to-all-start.2 = ((bf16[16,8,1152]{2,1,0:T(8,128)(2,1)}), bf16[16,8,1152]{2,1,0:T(8,128)(2,1)S(1)}, u32[]{:S(2)}, u32[]{:S(2)}) async-start(bf16[16,8,1152]{2,1,0:T(8,128)(2,1)} %bitcast.43), calls=%async_computation.2 | async-start | bytes 589824 | tf_op jit(solution)/shard_map/while/body/eval_jaxpr/all_to_all | solution.py:209
  702.8 10.5 %all-to-all-start.3 = ((bf16[16,8,576]{2,1,0:T(8,128)(2,1)}), bf16[16,8,576]{2,1,0:T(8,128)(2,1)S(1)}, u32[]{:S(2)}, u32[]{:S(2)}) async-start(bf16[16,8,576]{2,1,0:T(8,128)(2,1)} %bitcast.45), calls=%async_computation.3 | async-start | bytes 327680 | tf_op jit(solution)/shard_map/while/body/eval_jaxpr/all_to_all | solution.py:209
  725.9 58.1 %collective-permute-start.6 = (bf16[2,128,1152]{2,1,0:T(8,128)(2,1)S(1)}, bf16[2,128,1152]{2,1,0:T(8,128)(2,1)S(1)}, u32[]{:S(2)}, u32[]{:S(2)}) collective-permute-start(bf16[2,128,1152]{2,1,0:T(8,128)(2,1)S(1)} %broadcast_select_fusion.2), channel_id=1, source_target_pairs={{0,16},{16,0},{32,48},{48,32},{64,80},{80,64},{96,112},{112,96},{1... | collective-permute-start | bytes 1769480 | tf_op jit(solution)/shard_map/ppermute | solution.py:182
  (31 other events, 518.6 us)

commit v2 on v1

v2 whole, which is shorter than its diff:
```python
import functools

import jax
import jax.numpy as jnp
from jax import lax
from jax.experimental import pallas as pl
from jax.experimental.pallas import tpu as pltpu
from jax.sharding import PartitionSpec as P

HEADS = 8
LANES = 128
F32 = jnp.float32
BF16 = jnp.bfloat16
EPS = 1e-06


def padded(n):
    return -(-n // LANES) * LANES


def dot(a, b):
    return lax.dot_general(a, b, (((1,), (0,)), ((), ())), preferred_element_type=F32)


def dot_t(a, b):
    return lax.dot_general(a, b, (((1,), (1,)), ((), ())), preferred_element_type=F32)


def split(a):
    high = a.astype(BF16)
    return high, (a - high.astype(F32)).astype(BF16)


def norm_modulate(x, offset, scaling):
    average = jnp.mean(x, axis=-1, keepdims=True)
    centered = x - average
    variance = jnp.mean(centered * centered, axis=-1, keepdims=True)
    return (centered * lax.rsqrt(variance + EPS) * (1.0 + scaling) + offset).astype(BF16)


def in_head(shape, axis, start, head, width):
    at = lax.broadcasted_iota(jnp.int32, shape, axis) + start
    return jnp.logical_and(at >= head * width, at < (head + 1) * width)


def head_members(hw, width):
    row = lax.broadcasted_iota(jnp.int32, (hw, LANES), 0)
    col = lax.broadcasted_iota(jnp.int32, (hw, LANES), 1) * width
    tall = jnp.where(jnp.logical_and(row >= col, row < col + width), 1.0, 0.0)
    row = lax.broadcasted_iota(jnp.int32, (HEADS, hw), 0) * width
    col = lax.broadcasted_iota(jnp.int32, (HEADS, hw), 1)
    flat = jnp.where(jnp.logical_and(col >= row, col < row + width), 1.0, 0.0)
    return tall.astype(BF16), flat.astype(BF16)


def attention(projected, hw, patches):
    tokens = projected.shape[0]
    width = hw // HEADS
    begin = padded(hw)
    tall, flat = head_members(hw, width)
    queries, lookups = projected[:, :hw], projected[:, begin : begin + hw]
    values = projected[:, begin + hw : begin + 2 * hw].astype(BF16)
    high, low = split(queries * queries)
    rows = lax.rsqrt((dot(high, tall) + dot(low, tall)) * (1.0 / width) + EPS) * width**-0.5
    high, low = split(lookups * lookups)
    cols = lax.rsqrt((dot_t(flat, high) + dot_t(flat, low)) * (1.0 / width) + EPS)
    queries, lookups = queries.astype(BF16), lookups.astype(BF16)
    spans, scores = [], []
    for head in range(HEADS):
        first = head * width // LANES
        last = ((head + 1) * width - 1) // LANES
        start, stop = first * LANES, min((last + 1) * LANES, hw)
        mine = in_head((1, stop - start), 1, start, head, width)
        window = jnp.where(mine, queries[:, start:stop], jnp.zeros((), BF16))
        scores.append(dot_t(window, lookups[:, start:stop]))
        spans.append((first, last, start, stop))
    e = [jnp.exp(s * rows[:, h : h + 1] * cols[h : h + 1]) for h, s in enumerate(scores)]
    if patches:
        r = lax.broadcasted_iota(jnp.int32, (tokens, tokens), 0) % patches
        c = lax.broadcasted_iota(jnp.int32, (tokens, tokens), 1) % patches
        same = r == c
        e = [jnp.where(same, a, 0.0) for a in e]
    mixed = [dot(a.astype(BF16), values[:, s[2] : s[3]]) for a, s in zip(e, spans)]
    inverse = [1.0 / jnp.sum(a, axis=-1, keepdims=True) for a in e]
    tiles = [0.0] * (padded(hw) // LANES)
    for head, (first, last, start, stop) in enumerate(spans):
        result = mixed[head] * inverse[head]
        for tile in range(first, last + 1):
            left, right = tile * LANES, min(tile * LANES + LANES, hw)
            own = in_head((1, right - left), 1, left, head, width)
            tiles[tile] = jnp.where(own, result[:, left - start : right - start], tiles[tile])
    return jnp.concatenate(tiles, axis=1).astype(BF16)


def prepare_kernel(core, qkv, qkv2, out, out2, mod, mod2, *refs):
    even, odd, out_e, out_o, mod_e, mod_o = refs[:6]
    turned, done, sems = refs[6:8], refs[8:10], refs[10]
    hw = out.shape[0]
    gap = padded(hw) - hw
    for k in range(2):
        pick = core[0] if k == 0 else 1 - core[0]

        def begin(q, o, m):
            pltpu.make_async_copy(q.at[pl.ds(0, hw)], turned[k].at[pl.ds(0, hw)], sems.at[k, 0]).start()
            pltpu.make_async_copy(
                q.at[pl.ds(hw, 2 * hw)], turned[k].at[pl.ds(hw + gap, 2 * hw)], sems.at[k, 1]
            ).start()
            pltpu.make_async_copy(o, (out_e, out_o)[k], sems.at[k, 2]).start()
            pltpu.make_async_copy(m, (mod_e, mod_o)[k], sems.at[k, 3]).start()

        pl.when(pick == 0)(lambda: begin(qkv, out, mod))
        pl.when(pick != 0)(lambda: begin(qkv2, out2, mod2))
        turned[k][hw : hw + gap, :] = jnp.zeros((gap, qkv.shape[1]), BF16)
    back = []
    for k in range(2):
        pltpu.make_async_copy(qkv.at[pl.ds(0, hw)], turned[k].at[pl.ds(0, hw)], sems.at[k, 0]).wait()
        pltpu.make_async_copy(
            qkv.at[pl.ds(hw, 2 * hw)], turned[k].at[pl.ds(hw + gap, 2 * hw)], sems.at[k, 1]
        ).wait()
        for j in range(turned[k].shape[0] // LANES):
            done[k][:, j * LANES : (j + 1) * LANES] = turned[k][j * LANES : (j + 1) * LANES, :].T
        back.append(pltpu.make_async_copy(done[k], (even, odd)[k], sems.at[k, 4]))
        back[-1].start()
    for k in range(2):
        pltpu.make_async_copy(out, (out_e, out_o)[k], sems.at[k, 2]).wait()
        pltpu.make_async_copy(mod, (mod_e, mod_o)[k], sems.at[k, 3]).wait()
        back[k].wait()


def place_of(ids, step, per_core):
    micro = step[0] - ids[0]
    inside = jnp.logical_and(micro >= 0, micro < per_core)
    clipped = jnp.clip(micro, 0, per_core - 1)
    return ids[1] * per_core + clipped, jnp.where(inside, clipped, per_core)


def spatial_part(x, factors, qkv, out, y, g):
    normed = norm_modulate(x, factors[0:1], factors[1:2])
    mixed = attention(dot(normed, qkv[...]), out.shape[0], 0)
    middle = x + factors[2:3] * dot(mixed, out[...])
    y[...] = middle
    g[...] = norm_modulate(middle, factors[3:4], factors[4:5])


def head_kernel(per_core, ids, step, frames, arriving, mod, qkv, out, y, g, x_v, sem):
    video, _ = place_of(ids, step, per_core)

    @pl.when(ids[0] == 0)
    def _():
        pltpu.make_async_copy(frames.at[video], x_v, sem).start()

    @pl.when(ids[0] != 0)
    def _():
        pltpu.make_async_copy(arriving, x_v, sem).start()

    pltpu.make_async_copy(arriving, x_v, sem).wait()
    spatial_part(x_v[...].astype(F32), mod[video], qkv, out, y, g)


def temporal_kernel(share, arrived, qkv, mixed):
    mixed[...] = attention(dot(arrived[...], qkv[...]), mixed.shape[1], share)


def joint_kernel(
    per_core, ids, step, returned, y_in, mod, following, tout, qkv, out, kept_in,
    y, g, kept, x_v, sem,
):
    video, slot = place_of(ids, step, per_core)
    leaving = (y_in[...] + mod[video][5:6] * dot(returned[...], tout[...])).astype(BF16)
    x_v[...] = leaving
    store = pltpu.make_async_copy(x_v, kept.at[slot], sem)
    store.start()
    spatial_part(leaving.astype(F32), following[video], qkv, out, y, g)
    store.wait()


def tail_kernel(per_core, ids, step, returned, y_in, mod, tout, kept_in, x, kept, x_v, sem):
    video, slot = place_of(ids, step, per_core)
    leaving = (y_in[...] + mod[video][5:6] * dot(returned[...], tout[...])).astype(BF16)
    x_v[...] = leaving
    store = pltpu.make_async_copy(x_v, kept.at[slot], sem)
    store.start()
    x[...] = leaving
    store.wait()


SMEM = pl.BlockSpec(memory_space=pltpu.SMEM)
VMEM = pl.BlockSpec(memory_space=pltpu.VMEM)
ANY = pl.BlockSpec(memory_space=pl.ANY)


def call(kernel, name, ins, outs, specs, scratch, aliases={}):
    return pl.pallas_call(
        kernel,
        name=name,
        in_specs=ins,
        out_specs=specs,
        out_shape=outs,
        scratch_shapes=scratch,
        input_output_aliases=aliases,
        compiler_params=pltpu.CompilerParams(vmem_limit_bytes=24 * 2**20),
    )


def on_device(frames_in, spatial_qkv, spatial_out, temporal_qkv, temporal_out, modulation):
    videos, frames, patches, model = frames_in.shape
    wide, hw = spatial_qkv.shape[2], spatial_out.shape[1]
    per_core = videos // 2
    sections = lax.axis_size("section")
    ranks = lax.axis_size("seq")
    stages = sections // 2
    section = lax.axis_index("section")
    stage, core = section // 2, section % 2
    tokens = frames * patches
    share = patches // ranks
    columns = wide + padded(hw) - hw

    def swapped(a):
        return lax.ppermute(a, "section", [(i, i ^ 1) for i in range(sections)])

    shape = jax.ShapeDtypeStruct
    factors_s = shape(modulation.shape[1:], F32)
    qkv_s, out_s = shape((model, columns), BF16), shape((hw, model), BF16)
    prepare = call(
        prepare_kernel, "prepare", [SMEM] + [ANY] * 6, [qkv_s] * 2 + [out_s] * 2 + [factors_s] * 2,
        [ANY] * 6,
        [pltpu.VMEM((columns, model), BF16)] * 2 + [pltpu.VMEM((model, columns), BF16)] * 2
        + [pltpu.SemaphoreType.DMA((2, 5))],
    )
    core_id = core.reshape(1).astype(jnp.int32)
    ids = jnp.stack([stage, core]).astype(jnp.int32)
    mod2 = swapped(modulation)

    def prepared(qkv, out, rows, rows2):
        qkv2, out2 = swapped(qkv), swapped(out)
        return prepare(
            core_id, jnp.swapaxes(qkv[0], 0, 1), jnp.swapaxes(qkv2[0], 0, 1), out[0], out2[0],
            rows, rows2,
        )

    sqkv_e, sqkv_o, sout_e, sout_o, mod_e, mod_o = prepared(
        spatial_qkv, spatial_out, modulation[0], mod2[0]
    )
    tqkv_e, tqkv_o, tout_e, tout_o, _, _ = prepared(
        temporal_qkv, temporal_out, modulation[0], mod2[0]
    )
    source = frames_in.reshape(videos, tokens, model)

    x_s, y_s = shape((tokens, model), BF16), shape((tokens, model), F32)
    kept_s = shape((per_core + 1, tokens, model), BF16)
    hold = [pltpu.VMEM((tokens, model), BF16), pltpu.SemaphoreType.DMA]
    head = call(
        functools.partial(head_kernel, per_core), "head",
        [SMEM, SMEM, ANY, ANY, VMEM, VMEM, VMEM], [y_s, x_s], [VMEM, VMEM], hold,
    )
    temporal = call(
        functools.partial(temporal_kernel, share), "temporal", [VMEM, VMEM],
        shape((tokens, hw), BF16), VMEM, [],
    )
    joint = call(
        functools.partial(joint_kernel, per_core), "joint",
        [SMEM, SMEM] + [VMEM] * 7 + [ANY], [y_s, x_s, kept_s], [VMEM, VMEM, ANY], hold, {9: 2},
    )
    tail = call(
        functools.partial(tail_kernel, per_core), "tail",
        [SMEM, SMEM] + [VMEM] * 4 + [ANY], [x_s, kept_s], [VMEM, ANY], hold, {6: 1},
    )

    def exchange(a):
        out = lax.all_to_all(a.reshape(ranks, share, a.shape[1]), "seq", 0, 0, tiled=True)
        return out.reshape(a.shape)

    def advance(step, carried):
        even, odd, arriving = carried
        at = step.reshape(1)
        y, g = head(ids, at, source, arriving, mod_e, sqkv_e, sout_e)
        mixed = temporal(exchange(g), tqkv_e)
        y, g, even = joint(
            ids, at, exchange(mixed), y, mod_e, mod_o, tout_e, sqkv_o, sout_o, even
        )
        mixed = temporal(exchange(g), tqkv_o)
        x, odd = tail(ids, at, exchange(mixed), y, mod_o, tout_o, odd)
        arriving = lax.ppermute(x, "section", [(i, i + 2) for i in range(sections - 2)])
        return even, odd, arriving

    kept = jnp.zeros(kept_s.shape, BF16)
    even, odd, _ = lax.fori_loop(
        0, stages + per_core - 1, advance, (kept, kept, jnp.zeros((tokens, model), BF16))
    )
    even, odd = even[:per_core], odd[:per_core]
    own = jnp.where(core == 0, even, odd)
    other = swapped(jnp.where(core == 0, odd, even))
    low, high = jnp.where(core == 0, own, other), jnp.where(core == 0, other, own)
    hidden = jnp.concatenate([low, high], axis=0)
    return hidden.reshape((1,) + frames_in.shape)


def solution(mesh):
    placed = (
        P(None, "seq", None, None),
        P("section", None, None),
        P("section", None, None),
        P("section", None, None),
        P("section", None, None),
        P("section", None, None, None),
    )
    return jax.shard_map(
        on_device,
        mesh=mesh,
        in_specs=placed,
        out_specs=P("section", None, "seq", None, None),
        check_vma=False,
    )
```

time: 796 us -> 687 us (0.86)
  blocking collectives: 100 us -> 382 us
  waiting for transfers between devices: 247 us -> 78.3 us
  local copies, waits for them, and re-layouts: 98.8 us -> 5.95 us
  starting transfers between devices: 166 us -> 74 us
  Pallas kernels: 168 us -> 137 us
    all_to_all x9 -> x36, blocking collectives: 100 us -> 382 us  [exchange(): lax.all_to_all(a.reshape(ranks, share, a.shape[1]), 'seq', 0, 0, tiled=True)]
    all_to_all x27 -> x0, waiting for transfers between devices: 190 us -> none  [exchange(): lax.all_to_all(a.reshape(ranks, share, a.shape[1]), 'seq', 0, 0, tiled=True)]
    all_to_all x27 -> x0, starting transfers between devices: 96.5 us -> none  [exchange(): lax.all_to_all(a.reshape(ranks, share, a.shape[1]), 'seq', 0, 0, tiled=True)]
    pallas_call x9 -> x0, local copies, waits for them, and re-layouts: 63.4 us -> none  [advance(): joint(first, exchange(mixed), y, mod, mod2, tout, tout2, sqkv, sqkv2, sou...]
    pallas_call x36 -> x47, Pallas kernels: 168 us -> 137 us  [the longest x9 54.5 us: advance(): y, g = head(ids, at, source, arriving, mod_e, sqkv_e, sout_e)]
    while x41 -> x90, local copies, waits for them, and re-layouts: 26.7 us -> 0.17 us  [the longest x5 26.6 us: on_device(): lax.fori_loop(0, stages + per_core - 1, advance, (kept, kept, jnp.zeros((...]
    ppermute x6, waiting for transfers between devices: 1.64 us -> 15.9 us  [swapped(): return lax.ppermute(a, 'section', [(i, i ^ 1) for i in range(sections)])]
  transfers between devices with their start and end apart: 42 -> 15, of which waited for: 37 -> 11; matrix products, arithmetic and copies ran while one was open for 4% -> 0% of each run, Pallas kernels for 0% -> 1%
where the time goes in v2:
time: 687 us; the launch traced here: 679 us
  blocking collectives  382 us (56%)
  Pallas kernels  137 us (20%)
  waiting for transfers between devices  78.3 us (11%)
  starting transfers between devices  74 us (11%)
    all_to_all x36, blocking collectives, exchange(): lax.all_to_all(a.reshape(ranks, share, a.shape[1]), 'seq', 0, 0, tiled=True)  382 us
    ppermute x9, waiting for transfers between devices, advance(): lax.ppermute(x, 'section', [(i, i + 2) for i in range(sections - 2)])  62.4 us
    ppermute x6, starting transfers between devices, swapped(): return lax.ppermute(a, 'section', [(i, i ^ 1) for i in range(sections)])  62.3 us
    pallas_call x9, Pallas kernels, advance(): y, g = head(ids, at, source, arriving, mod_e, sqkv_e, sout_e)  54.5 us
    pallas_call x9, Pallas kernels, advance(): joint(ids, at, exchange(mixed), y, mod_e, mod_o, tout_e, sqkv_o, sout_o,...  33.5 us
    ppermute x6, waiting for transfers between devices, swapped(): return lax.ppermute(a, 'section', [(i, i ^ 1) for i in range(sections)])  15.9 us
    pallas_call x2, Pallas kernels, prepared(): prepare(core_id, jnp.swapaxes(qkv[0], 0, 1), jnp.swapaxes(qkv2[0], 0, 1),...  15.2 us
  transfers between devices with their start and end apart: 15, of which 11 were waited for; matrix products, arithmetic and copies ran while one was open for 0% of the time, Pallas kernels for 1%

profile of v2, /device:TPU:225, one launch (start us, length us, event | category | flops | bytes accessed | tf_op | source)
XLA Modules:
  0.0 678.9 jit_solution(12069771568408099191)
XLA Ops:
  2.8 14.3 %collective-permute-done.3 = f32[1,4,6,1152]{3,2,1,0:T(8,128)S(1)} collective-permute-done((f32[1,4,6,1152]{3,2,1,0:T(8,128)S(1)}, f32[1,4,6,1152]{3,2,1,0:T(8,128)S(1)}, u32[]{:S(2)}, u32[]{:S(2)}) %collective-permute-start.3) | collective-permute-done | bytes 110624 | tf_op jit(solution)/shard_map/ppermute | solution.py:219
  37.2 578.1 %while.17 = (s32[]{:T(128)}, bf16[3,128,1152]{2,1,0:T(8,128)(2,1)S(1)}, bf16[3,128,1152]{2,1,0:T(8,128)(2,1)S(1)}, bf16[128,1152]{1,0:T(8,128)(2,1)}, s32[2]{0:T...) while((s32[]{:T(128)}, ...), condition=%wide.region_1.2_spmd, body=%wide.region_0.1_spmd.sunk | while | flops 2 | bytes 63111504 | solution.py:287
  43.3 14.2 %all_to_all.40 = bf16[16,8,1152]{2,1,0:T(8,128)(2,1)S(1)} all-to-all(bf16[16,8,1152]{2,1,0:T(8,128)(2,1)S(1)} %bitcast.58), channel_id=1, replica_groups=mesh['section'=16,'seq'=16] {'seq'}, dimensions={0} | all-to-all | bytes 589824 | tf_op jit(solution)/shard_map/while/body/eval_jaxpr/all_to_all | solution.py:270
  58.9 10.3 %all_to_all.41 = bf16[16,8,576]{2,1,0:T(8,128)(2,1)S(1)} all-to-all(bf16[16,8,576]{2,1,0:T(8,128)(2,1)S(1)} %bitcast.54), channel_id=1, replica_groups=mesh['section'=16,'seq'=16] {'seq'}, dimensions={0} | all-to-all | bytes 294912 | tf_op jit(solution)/shard_map/while/body/eval_jaxpr/all_to_all | solution.py:270
  72.9 10.7 %all_to_all.42 = bf16[16,8,1152]{2,1,0:T(8,128)(2,1)S(1)} all-to-all(bf16[16,8,1152]{2,1,0:T(8,128)(2,1)S(1)} %bitcast.57), channel_id=1, replica_groups=mesh['section'=16,'seq'=16] {'seq'}, dimensions={0} | all-to-all | bytes 589824 | tf_op jit(solution)/shard_map/while/body/eval_jaxpr/all_to_all | solution.py:270
  85.0 10.0 %all_to_all.43 = bf16[16,8,576]{2,1,0:T(8,128)(2,1)S(1)} all-to-all(bf16[16,8,576]{2,1,0:T(8,128)(2,1)S(1)} %bitcast.55), channel_id=1, replica_groups=mesh['section'=16,'seq'=16] {'seq'}, dimensions={0} | all-to-all | bytes 294912 | tf_op jit(solution)/shard_map/while/body/eval_jaxpr/all_to_all | solution.py:270
  109.6 10.8 %all_to_all.40 = bf16[16,8,1152]{2,1,0:T(8,128)(2,1)S(1)} all-to-all(bf16[16,8,1152]{2,1,0:T(8,128)(2,1)S(1)} %bitcast.58), channel_id=1, replica_groups=mesh['section'=16,'seq'=16] {'seq'}, dimensions={0} | all-to-all | bytes 589824 | tf_op jit(solution)/shard_map/while/body/eval_jaxpr/all_to_all | solution.py:270
  135.5 10.7 %all_to_all.42 = bf16[16,8,1152]{2,1,0:T(8,128)(2,1)S(1)} all-to-all(bf16[16,8,1152]{2,1,0:T(8,128)(2,1)S(1)} %bitcast.57), channel_id=1, replica_groups=mesh['section'=16,'seq'=16] {'seq'}, dimensions={0} | all-to-all | bytes 589824 | tf_op jit(solution)/shard_map/while/body/eval_jaxpr/all_to_all | solution.py:270
  147.6 11.2 %all_to_all.43 = bf16[16,8,576]{2,1,0:T(8,128)(2,1)S(1)} all-to-all(bf16[16,8,576]{2,1,0:T(8,128)(2,1)S(1)} %bitcast.55), channel_id=1, replica_groups=mesh['section'=16,'seq'=16] {'seq'}, dimensions={0} | all-to-all | bytes 294912 | tf_op jit(solution)/shard_map/while/body/eval_jaxpr/all_to_all | solution.py:270
  173.5 10.7 %all_to_all.40 = bf16[16,8,1152]{2,1,0:T(8,128)(2,1)S(1)} all-to-all(bf16[16,8,1152]{2,1,0:T(8,128)(2,1)S(1)} %bitcast.58), channel_id=1, replica_groups=mesh['section'=16,'seq'=16] {'seq'}, dimensions={0} | all-to-all | bytes 589824 | tf_op jit(solution)/shard_map/while/body/eval_jaxpr/all_to_all | solution.py:270
  185.5 10.0 %all_to_all.41 = bf16[16,8,576]{2,1,0:T(8,128)(2,1)S(1)} all-to-all(bf16[16,8,576]{2,1,0:T(8,128)(2,1)S(1)} %bitcast.54), channel_id=1, replica_groups=mesh['section'=16,'seq'=16] {'seq'}, dimensions={0} | all-to-all | bytes 294912 | tf_op jit(solution)/shard_map/while/body/eval_jaxpr/all_to_all | solution.py:270
  199.2 10.8 %all_to_all.42 = bf16[16,8,1152]{2,1,0:T(8,128)(2,1)S(1)} all-to-all(bf16[16,8,1152]{2,1,0:T(8,128)(2,1)S(1)} %bitcast.57), channel_id=1, replica_groups=mesh['section'=16,'seq'=16] {'seq'}, dimensions={0} | all-to-all | bytes 589824 | tf_op jit(solution)/shard_map/while/body/eval_jaxpr/all_to_all | solution.py:270
  211.4 10.2 %all_to_all.43 = bf16[16,8,576]{2,1,0:T(8,128)(2,1)S(1)} all-to-all(bf16[16,8,576]{2,1,0:T(8,128)(2,1)S(1)} %bitcast.55), channel_id=1, replica_groups=mesh['section'=16,'seq'=16] {'seq'}, dimensions={0} | all-to-all | bytes 294912 | tf_op jit(solution)/shard_map/while/body/eval_jaxpr/all_to_all | solution.py:270
  236.2 10.8 %all_to_all.40 = bf16[16,8,1152]{2,1,0:T(8,128)(2,1)S(1)} all-to-all(bf16[16,8,1152]{2,1,0:T(8,128)(2,1)S(1)} %bitcast.58), channel_id=1, replica_groups=mesh['section'=16,'seq'=16] {'seq'}, dimensions={0} | all-to-all | bytes 589824 | tf_op jit(solution)/shard_map/while/body/eval_jaxpr/all_to_all | solution.py:270
  262.1 10.7 %all_to_all.42 = bf16[16,8,1152]{2,1,0:T(8,128)(2,1)S(1)} all-to-all(bf16[16,8,1152]{2,1,0:T(8,128)(2,1)S(1)} %bitcast.57), channel_id=1, replica_groups=mesh['section'=16,'seq'=16] {'seq'}, dimensions={0} | all-to-all | bytes 589824 | tf_op jit(solution)/shard_map/while/body/eval_jaxpr/all_to_all | solution.py:270
  274.2 10.0 %all_to_all.43 = bf16[16,8,576]{2,1,0:T(8,128)(2,1)S(1)} all-to-all(bf16[16,8,576]{2,1,0:T(8,128)(2,1)S(1)} %bitcast.55), channel_id=1, replica_groups=mesh['section'=16,'seq'=16] {'seq'}, dimensions={0} | all-to-all | bytes 294912 | tf_op jit(solution)/shard_map/while/body/eval_jaxpr/all_to_all | solution.py:270
  298.9 10.9 %all_to_all.40 = bf16[16,8,1152]{2,1,0:T(8,128)(2,1)S(1)} all-to-all(bf16[16,8,1152]{2,1,0:T(8,128)(2,1)S(1)} %bitcast.58), channel_id=1, replica_groups=mesh['section'=16,'seq'=16] {'seq'}, dimensions={0} | all-to-all | bytes 589824 | tf_op jit(solution)/shard_map/while/body/eval_jaxpr/all_to_all | solution.py:270
  311.1 10.2 %all_to_all.41 = bf16[16,8,576]{2,1,0:T(8,128)(2,1)S(1)} all-to-all(bf16[16,8,576]{2,1,0:T(8,128)(2,1)S(1)} %bitcast.54), channel_id=1, replica_groups=mesh['section'=16,'seq'=16] {'seq'}, dimensions={0} | all-to-all | bytes 294912 | tf_op jit(solution)/shard_map/while/body/eval_jaxpr/all_to_all | solution.py:270
  325.1 10.8 %all_to_all.42 = bf16[16,8,1152]{2,1,0:T(8,128)(2,1)S(1)} all-to-all(bf16[16,8,1152]{2,1,0:T(8,128)(2,1)S(1)} %bitcast.57), channel_id=1, replica_groups=mesh['section'=16,'seq'=16] {'seq'}, dimensions={0} | all-to-all | bytes 589824 | tf_op jit(solution)/shard_map/while/body/eval_jaxpr/all_to_all | solution.py:270
  337.3 10.2 %all_to_all.43 = bf16[16,8,576]{2,1,0:T(8,128)(2,1)S(1)} all-to-all(bf16[16,8,576]{2,1,0:T(8,128)(2,1)S(1)} %bitcast.55), channel_id=1, replica_groups=mesh['section'=16,'seq'=16] {'seq'}, dimensions={0} | all-to-all | bytes 294912 | tf_op jit(solution)/shard_map/while/body/eval_jaxpr/all_to_all | solution.py:270
  363.1 10.8 %all_to_all.40 = bf16[16,8,1152]{2,1,0:T(8,128)(2,1)S(1)} all-to-all(bf16[16,8,1152]{2,1,0:T(8,128)(2,1)S(1)} %bitcast.58), channel_id=1, replica_groups=mesh['section'=16,'seq'=16] {'seq'}, dimensions={0} | all-to-all | bytes 589824 | tf_op jit(solution)/shard_map/while/body/eval_jaxpr/all_to_all | solution.py:270
  389.0 10.7 %all_to_all.42 = bf16[16,8,1152]{2,1,0:T(8,128)(2,1)S(1)} all-to-all(bf16[16,8,1152]{2,1,0:T(8,128)(2,1)S(1)} %bitcast.57), channel_id=1, replica_groups=mesh['section'=16,'seq'=16] {'seq'}, dimensions={0} | all-to-all | bytes 589824 | tf_op jit(solution)/shard_map/while/body/eval_jaxpr/all_to_all | solution.py:270
  401.1 10.0 %all_to_all.43 = bf16[16,8,576]{2,1,0:T(8,128)(2,1)S(1)} all-to-all(bf16[16,8,576]{2,1,0:T(8,128)(2,1)S(1)} %bitcast.55), channel_id=1, replica_groups=mesh['section'=16,'seq'=16] {'seq'}, dimensions={0} | all-to-all | bytes 294912 | tf_op jit(solution)/shard_map/while/body/eval_jaxpr/all_to_all | solution.py:270
  427.1 11.8 %all_to_all.40 = bf16[16,8,1152]{2,1,0:T(8,128)(2,1)S(1)} all-to-all(bf16[16,8,1152]{2,1,0:T(8,128)(2,1)S(1)} %bitcast.58), channel_id=1, replica_groups=mesh['section'=16,'seq'=16] {'seq'}, dimensions={0} | all-to-all | bytes 589824 | tf_op jit(solution)/shard_map/while/body/eval_jaxpr/all_to_all | solution.py:270
  454.0 11.0 %all_to_all.42 = bf16[16,8,1152]{2,1,0:T(8,128)(2,1)S(1)} all-to-all(bf16[16,8,1152]{2,1,0:T(8,128)(2,1)S(1)} %bitcast.57), channel_id=1, replica_groups=mesh['section'=16,'seq'=16] {'seq'}, dimensions={0} | all-to-all | bytes 589824 | tf_op jit(solution)/shard_map/while/body/eval_jaxpr/all_to_all | solution.py:270
  492.4 10.8 %all_to_all.40 = bf16[16,8,1152]{2,1,0:T(8,128)(2,1)S(1)} all-to-all(bf16[16,8,1152]{2,1,0:T(8,128)(2,1)S(1)} %bitcast.58), channel_id=1, replica_groups=mesh['section'=16,'seq'=16] {'seq'}, dimensions={0} | all-to-all | bytes 589824 | tf_op jit(solution)/shard_map/while/body/eval_jaxpr/all_to_all | solution.py:270
  518.3 10.7 %all_to_all.42 = bf16[16,8,1152]{2,1,0:T(8,128)(2,1)S(1)} all-to-all(bf16[16,8,1152]{2,1,0:T(8,128)(2,1)S(1)} %bitcast.57), channel_id=1, replica_groups=mesh['section'=16,'seq'=16] {'seq'}, dimensions={0} | all-to-all | bytes 589824 | tf_op jit(solution)/shard_map/while/body/eval_jaxpr/all_to_all | solution.py:270
  530.4 10.0 %all_to_all.43 = bf16[16,8,576]{2,1,0:T(8,128)(2,1)S(1)} all-to-all(bf16[16,8,576]{2,1,0:T(8,128)(2,1)S(1)} %bitcast.55), channel_id=1, replica_groups=mesh['section'=16,'seq'=16] {'seq'}, dimensions={0} | all-to-all | bytes 294912 | tf_op jit(solution)/shard_map/while/body/eval_jaxpr/all_to_all | solution.py:270
  557.0 10.8 %all_to_all.40 = bf16[16,8,1152]{2,1,0:T(8,128)(2,1)S(1)} all-to-all(bf16[16,8,1152]{2,1,0:T(8,128)(2,1)S(1)} %bitcast.58), channel_id=1, replica_groups=mesh['section'=16,'seq'=16] {'seq'}, dimensions={0} | all-to-all | bytes 589824 | tf_op jit(solution)/shard_map/while/body/eval_jaxpr/all_to_all | solution.py:270
  569.2 10.4 %all_to_all.41 = bf16[16,8,576]{2,1,0:T(8,128)(2,1)S(1)} all-to-all(bf16[16,8,576]{2,1,0:T(8,128)(2,1)S(1)} %bitcast.54), channel_id=1, replica_groups=mesh['section'=16,'seq'=16] {'seq'}, dimensions={0} | all-to-all | bytes 294912 | tf_op jit(solution)/shard_map/while/body/eval_jaxpr/all_to_all | solution.py:270
  583.3 11.8 %all_to_all.42 = bf16[16,8,1152]{2,1,0:T(8,128)(2,1)S(1)} all-to-all(bf16[16,8,1152]{2,1,0:T(8,128)(2,1)S(1)} %bitcast.57), channel_id=1, replica_groups=mesh['section'=16,'seq'=16] {'seq'}, dimensions={0} | all-to-all | bytes 589824 | tf_op jit(solution)/shard_map/while/body/eval_jaxpr/all_to_all | solution.py:270
  615.4 60.5 %collective-permute-start.6 = (bf16[2,128,1152]{2,1,0:T(8,128)(2,1)S(1)}, bf16[2,128,1152]{2,1,0:T(8,128)(2,1)S(1)}, u32[]{:S(2)}, u32[]{:S(2)}) collective-permute-start(bf16[2,128,1152]{2,1,0:T(8,128)(2,1)S(1)} %broadcast_select_fusion.2), channel_id=1, source_target_pairs={{0,16},{16,0},{32,48},{48,32},{64,80},{80,64},{96,112},{112,96},{1... | collective-permute-start | bytes 1769480 | tf_op jit(solution)/shard_map/ppermute | solution.py:219
  (190 shorter events, 291.4 us)
Async XLA Ops:
  0.0 17.1 %collective-permute-start.1 = (bf16[1,1152,1728]{1,2,0:T(8,128)(2,1)}, bf16[1,1152,1728]{1,2,0:T(8,128)(2,1)}, u32[]{:S(2)}, u32[]{:S(2)}) collective-permute-start(bf16[1,1152,1728]{1,2,0:T(8,128)(2,1)} %param.9), channel_id=1, source_target_pairs={{0,16},{16,0},{32,48},{48,32},{64,80},{80,64},{96,112},{112,96},{1... | collective-permute-start | bytes 11943944 | tf_op jit(solution)/shard_map/ppermute | solution.py:219
  0.7 27.5 %collective-permute-start.4 = (bf16[1,1152,1728]{1,2,0:T(8,128)(2,1)}, bf16[1,1152,1728]{1,2,0:T(8,128)(2,1)}, u32[]{:S(2)}, u32[]{:S(2)}) collective-permute-start(bf16[1,1152,1728]{1,2,0:T(8,128)(2,1)} %param.11), channel_id=1, source_target_pairs={{0,16},{16,0},{32,48},{48,32},{64,80},{80,64},{96,112},{112,96},{1... | collective-permute-start | bytes 11943944 | tf_op jit(solution)/shard_map/ppermute | solution.py:219
  0.7 16.4 %collective-permute-start.2 = (bf16[1,576,1152]{2,1,0:T(8,128)(2,1)}, bf16[1,576,1152]{2,1,0:T(8,128)(2,1)S(1)}, u32[]{:S(2)}, u32[]{:S(2)}) collective-permute-start(bf16[1,576,1152]{2,1,0:T(8,128)(2,1)} %param.10), channel_id=1, source_target_pairs={{0,16},{16,0},{32,48},{48,32},{64,80},{80,64},{96,112},{112,96},{1... | collective-permute-start | bytes 3981320 | tf_op jit(solution)/shard_map/ppermute | solution.py:219
  1.2 26.9 %collective-permute-start.5 = (bf16[1,576,1152]{2,1,0:T(8,128)(2,1)}, bf16[1,576,1152]{2,1,0:T(8,128)(2,1)S(1)}, u32[]{:S(2)}, u32[]{:S(2)}) collective-permute-start(bf16[1,576,1152]{2,1,0:T(8,128)(2,1)} %param.12), channel_id=1, source_target_pairs={{0,16},{16,0},{32,48},{48,32},{64,80},{80,64},{96,112},{112,96},{1... | collective-permute-start | bytes 3981320 | tf_op jit(solution)/shard_map/ppermute | solution.py:219
  2.1 14.9 %collective-permute-start.3 = (f32[1,4,6,1152]{3,2,1,0:T(8,128)S(1)}, f32[1,4,6,1152]{3,2,1,0:T(8,128)S(1)}, u32[]{:S(2)}, u32[]{:S(2)}) collective-permute-start(f32[1,4,6,1152]{3,2,1,0:T(8,128)S(1)} %copy.13), channel_id=1, source_target_pairs={{0,16},{16,0},{32,48},{48,32},{64,80},{80,64},{96,112},{112,96},{1... | collective-permute-start | bytes 331784 | tf_op jit(solution)/shard_map/ppermute | solution.py:219
  37.2 20.3 %copy-start.4 = (bf16[1152,1792]{1,0:T(8,128)(2,1)S(1)}, bf16[1152,1792]{1,0:T(8,128)(2,1)}, u32[]{:S(2)}) copy-start(bf16[1152,1792]{1,0:T(8,128)(2,1)} %get-tuple-element.455.qkv) | copy-start | bytes 12386308 | tf_op jit(solution)/shard_map/while
  43.3 25.8 %copy-start.8 = (bf16[576,1152]{1,0:T(8,128)(2,1)S(1)}, bf16[576,1152]{1,0:T(8,128)(2,1)}, u32[]{:S(2)}) copy-start(bf16[576,1152]{1,0:T(8,128)(2,1)} %get-tuple-element.457.tout) | copy-start | bytes 3981316 | tf_op jit(solution)/shard_map/while
  96.0 7.6 %collective-permute-start = (bf16[128,1152]{1,0:T(8,128)(2,1)S(1)}, bf16[128,1152]{1,0:T(8,128)(2,1)}, u32[]{:S(2)}, u32[]{:S(2)}) collective-permute-start(bf16[128,1152]{1,0:T(8,128)(2,1)S(1)} %get-tuple-element.411), channel_id=1, source_target_pairs={{0,32},{16,48},{32,64},{48,80},{64,96},{80,112},{96,128},{112,144}... | collective-permute-start | bytes 884744 | tf_op jit(solution)/shard_map/while/body/eval_jaxpr/ppermute | solution.py:283
  103.5 16.9 %copy-start.4 = (bf16[1152,1792]{1,0:T(8,128)(2,1)S(1)}, bf16[1152,1792]{1,0:T(8,128)(2,1)}, u32[]{:S(2)}) copy-start(bf16[1152,1792]{1,0:T(8,128)(2,1)} %get-tuple-element.455.qkv) | copy-start | bytes 12386308 | tf_op jit(solution)/shard_map/while
  109.6 22.2 %copy-start.8 = (bf16[576,1152]{1,0:T(8,128)(2,1)S(1)}, bf16[576,1152]{1,0:T(8,128)(2,1)}, u32[]{:S(2)}) copy-start(bf16[576,1152]{1,0:T(8,128)(2,1)} %get-tuple-element.457.tout) | copy-start | bytes 3981316 | tf_op jit(solution)/shard_map/while
  159.8 7.6 %collective-permute-start = (bf16[128,1152]{1,0:T(8,128)(2,1)S(1)}, bf16[128,1152]{1,0:T(8,128)(2,1)}, u32[]{:S(2)}, u32[]{:S(2)}) collective-permute-start(bf16[128,1152]{1,0:T(8,128)(2,1)S(1)} %get-tuple-element.411), channel_id=1, source_target_pairs={{0,32},{16,48},{32,64},{48,80},{64,96},{80,112},{96,128},{112,144}... | collective-permute-start | bytes 884744 | tf_op jit(solution)/shard_map/while/body/eval_jaxpr/ppermute | solution.py:283
  173.5 22.0 %copy-start.8 = (bf16[576,1152]{1,0:T(8,128)(2,1)S(1)}, bf16[576,1152]{1,0:T(8,128)(2,1)}, u32[]{:S(2)}) copy-start(bf16[576,1152]{1,0:T(8,128)(2,1)} %get-tuple-element.457.tout) | copy-start | bytes 3981316 | tf_op jit(solution)/shard_map/while
  222.6 7.6 %collective-permute-start = (bf16[128,1152]{1,0:T(8,128)(2,1)S(1)}, bf16[128,1152]{1,0:T(8,128)(2,1)}, u32[]{:S(2)}, u32[]{:S(2)}) collective-permute-start(bf16[128,1152]{1,0:T(8,128)(2,1)S(1)} %get-tuple-element.411), channel_id=1, source_target_pairs={{0,32},{16,48},{32,64},{48,80},{64,96},{80,112},{96,128},{112,144}... | collective-permute-start | bytes 884744 | tf_op jit(solution)/shard_map/while/body/eval_jaxpr/ppermute | solution.py:283
  230.2 16.9 %copy-start.4 = (bf16[1152,1792]{1,0:T(8,128)(2,1)S(1)}, bf16[1152,1792]{1,0:T(8,128)(2,1)}, u32[]{:S(2)}) copy-start(bf16[1152,1792]{1,0:T(8,128)(2,1)} %get-tuple-element.455.qkv) | copy-start | bytes 12386308 | tf_op jit(solution)/shard_map/while
  236.2 22.2 %copy-start.8 = (bf16[576,1152]{1,0:T(8,128)(2,1)S(1)}, bf16[576,1152]{1,0:T(8,128)(2,1)}, u32[]{:S(2)}) copy-start(bf16[576,1152]{1,0:T(8,128)(2,1)} %get-tuple-element.457.tout) | copy-start | bytes 3981316 | tf_op jit(solution)/shard_map/while
  285.2 7.6 %collective-permute-start = (bf16[128,1152]{1,0:T(8,128)(2,1)S(1)}, bf16[128,1152]{1,0:T(8,128)(2,1)}, u32[]{:S(2)}, u32[]{:S(2)}) collective-permute-start(bf16[128,1152]{1,0:T(8,128)(2,1)S(1)} %get-tuple-element.411), channel_id=1, source_target_pairs={{0,32},{16,48},{32,64},{48,80},{64,96},{80,112},{96,128},{112,144}... | collective-permute-start | bytes 884744 | tf_op jit(solution)/shard_map/while/body/eval_jaxpr/ppermute | solution.py:283
  292.8 16.9 %copy-start.4 = (bf16[1152,1792]{1,0:T(8,128)(2,1)S(1)}, bf16[1152,1792]{1,0:T(8,128)(2,1)}, u32[]{:S(2)}) copy-start(bf16[1152,1792]{1,0:T(8,128)(2,1)} %get-tuple-element.455.qkv) | copy-start | bytes 12386308 | tf_op jit(solution)/shard_map/while
  298.9 22.5 %copy-start.8 = (bf16[576,1152]{1,0:T(8,128)(2,1)S(1)}, bf16[576,1152]{1,0:T(8,128)(2,1)}, u32[]{:S(2)}) copy-start(bf16[576,1152]{1,0:T(8,128)(2,1)} %get-tuple-element.457.tout) | copy-start | bytes 3981316 | tf_op jit(solution)/shard_map/while
  348.5 8.6 %collective-permute-start = (bf16[128,1152]{1,0:T(8,128)(2,1)S(1)}, bf16[128,1152]{1,0:T(8,128)(2,1)}, u32[]{:S(2)}, u32[]{:S(2)}) collective-permute-start(bf16[128,1152]{1,0:T(8,128)(2,1)S(1)} %get-tuple-element.411), channel_id=1, source_target_pairs={{0,32},{16,48},{32,64},{48,80},{64,96},{80,112},{96,128},{112,144}... | collective-permute-start | bytes 884744 | tf_op jit(solution)/shard_map/while/body/eval_jaxpr/ppermute | solution.py:283
  357.1 16.9 %copy-start.4 = (bf16[1152,1792]{1,0:T(8,128)(2,1)S(1)}, bf16[1152,1792]{1,0:T(8,128)(2,1)}, u32[]{:S(2)}) copy-start(bf16[1152,1792]{1,0:T(8,128)(2,1)} %get-tuple-element.455.qkv) | copy-start | bytes 12386308 | tf_op jit(solution)/shard_map/while
  363.1 22.2 %copy-start.8 = (bf16[576,1152]{1,0:T(8,128)(2,1)S(1)}, bf16[576,1152]{1,0:T(8,128)(2,1)}, u32[]{:S(2)}) copy-start(bf16[576,1152]{1,0:T(8,128)(2,1)} %get-tuple-element.457.tout) | copy-start | bytes 3981316 | tf_op jit(solution)/shard_map/while
  412.1 8.9 %collective-permute-start = (bf16[128,1152]{1,0:T(8,128)(2,1)S(1)}, bf16[128,1152]{1,0:T(8,128)(2,1)}, u32[]{:S(2)}, u32[]{:S(2)}) collective-permute-start(bf16[128,1152]{1,0:T(8,128)(2,1)S(1)} %get-tuple-element.411), channel_id=1, source_target_pairs={{0,32},{16,48},{32,64},{48,80},{64,96},{80,112},{96,128},{112,144}... | collective-permute-start | bytes 884744 | tf_op jit(solution)/shard_map/while/body/eval_jaxpr/ppermute | solution.py:283
  421.1 17.9 %copy-start.4 = (bf16[1152,1792]{1,0:T(8,128)(2,1)S(1)}, bf16[1152,1792]{1,0:T(8,128)(2,1)}, u32[]{:S(2)}) copy-start(bf16[1152,1792]{1,0:T(8,128)(2,1)} %get-tuple-element.455.qkv) | copy-start | bytes 12386308 | tf_op jit(solution)/shard_map/while
  427.1 23.1 %copy-start.8 = (bf16[576,1152]{1,0:T(8,128)(2,1)S(1)}, bf16[576,1152]{1,0:T(8,128)(2,1)}, u32[]{:S(2)}) copy-start(bf16[576,1152]{1,0:T(8,128)(2,1)} %get-tuple-element.457.tout) | copy-start | bytes 3981316 | tf_op jit(solution)/shard_map/while
  477.4 8.9 %collective-permute-start = (bf16[128,1152]{1,0:T(8,128)(2,1)S(1)}, bf16[128,1152]{1,0:T(8,128)(2,1)}, u32[]{:S(2)}, u32[]{:S(2)}) collective-permute-start(bf16[128,1152]{1,0:T(8,128)(2,1)S(1)} %get-tuple-element.411), channel_id=1, source_target_pairs={{0,32},{16,48},{32,64},{48,80},{64,96},{80,112},{96,128},{112,144}... | collective-permute-start | bytes 884744 | tf_op jit(solution)/shard_map/while/body/eval_jaxpr/ppermute | solution.py:283
  486.3 16.9 %copy-start.4 = (bf16[1152,1792]{1,0:T(8,128)(2,1)S(1)}, bf16[1152,1792]{1,0:T(8,128)(2,1)}, u32[]{:S(2)}) copy-start(bf16[1152,1792]{1,0:T(8,128)(2,1)} %get-tuple-element.455.qkv) | copy-start | bytes 12386308 | tf_op jit(solution)/shard_map/while
  492.4 22.2 %copy-start.8 = (bf16[576,1152]{1,0:T(8,128)(2,1)S(1)}, bf16[576,1152]{1,0:T(8,128)(2,1)}, u32[]{:S(2)}) copy-start(bf16[576,1152]{1,0:T(8,128)(2,1)} %get-tuple-element.457.tout) | copy-start | bytes 3981316 | tf_op jit(solution)/shard_map/while
  541.4 9.5 %collective-permute-start = (bf16[128,1152]{1,0:T(8,128)(2,1)S(1)}, bf16[128,1152]{1,0:T(8,128)(2,1)}, u32[]{:S(2)}, u32[]{:S(2)}) collective-permute-start(bf16[128,1152]{1,0:T(8,128)(2,1)S(1)} %get-tuple-element.411), channel_id=1, source_target_pairs={{0,32},{16,48},{32,64},{48,80},{64,96},{80,112},{96,128},{112,144}... | collective-permute-start | bytes 884744 | tf_op jit(solution)/shard_map/while/body/eval_jaxpr/ppermute | solution.py:283
  550.9 16.9 %copy-start.4 = (bf16[1152,1792]{1,0:T(8,128)(2,1)S(1)}, bf16[1152,1792]{1,0:T(8,128)(2,1)}, u32[]{:S(2)}) copy-start(bf16[1152,1792]{1,0:T(8,128)(2,1)} %get-tuple-element.455.qkv) | copy-start | bytes 12386308 | tf_op jit(solution)/shard_map/while
  556.9 22.6 %copy-start.8 = (bf16[576,1152]{1,0:T(8,128)(2,1)S(1)}, bf16[576,1152]{1,0:T(8,128)(2,1)}, u32[]{:S(2)}) copy-start(bf16[576,1152]{1,0:T(8,128)(2,1)} %get-tuple-element.457.tout) | copy-start | bytes 3981316 | tf_op jit(solution)/shard_map/while
  607.5 7.9 %collective-permute-start = (bf16[128,1152]{1,0:T(8,128)(2,1)S(1)}, bf16[128,1152]{1,0:T(8,128)(2,1)}, u32[]{:S(2)}, u32[]{:S(2)}) collective-permute-start(bf16[128,1152]{1,0:T(8,128)(2,1)S(1)} %get-tuple-element.411), channel_id=1, source_target_pairs={{0,32},{16,48},{32,64},{48,80},{64,96},{80,112},{96,128},{112,144}... | collective-permute-start | bytes 884744 | tf_op jit(solution)/shard_map/while/body/eval_jaxpr/ppermute | solution.py:283
  615.4 62.2 %collective-permute-start.6 = (bf16[2,128,1152]{2,1,0:T(8,128)(2,1)S(1)}, bf16[2,128,1152]{2,1,0:T(8,128)(2,1)S(1)}, u32[]{:S(2)}, u32[]{:S(2)}) collective-permute-start(bf16[2,128,1152]{2,1,0:T(8,128)(2,1)S(1)} %broadcast_select_fusion.2), channel_id=1, source_target_pairs={{0,16},{16,0},{32,48},{48,32},{64,80},{80,64},{96,112},{112,96},{1... | collective-permute-start | bytes 1769480 | tf_op jit(solution)/shard_map/ppermute | solution.py:219
  (33 other events, 375.0 us)

commit v3 on v2

--- a/solution.py
+++ b/solution.py
@@ -92,39 +92,51 @@
     return jnp.concatenate(tiles, axis=1).astype(BF16)
 
 
-def prepare_kernel(core, qkv, qkv2, out, out2, mod, mod2, *refs):
-    even, odd, out_e, out_o, mod_e, mod_o = refs[:6]
-    turned, done, sems = refs[6:8], refs[8:10], refs[10]
-    hw = out.shape[0]
+def prepare_kernel(core, qkv, qkv2, out, out2, even, odd, out_e, out_o, *refs):
+    turned, done, sems = refs[:2], refs[2:4], refs[4]
+    hw, model = out.shape
     gap = padded(hw) - hw
+    parts = ((0, 0, hw), (hw, hw + gap, hw), (2 * hw, 2 * hw + gap, hw))
+
+    def piece(k, q, j):
+        at, to, rows = parts[j]
+        return pltpu.make_async_copy(
+            q.at[pl.ds(at, rows)], turned[k].at[pl.ds(to, rows)], sems.at[k, j]
+        )
+
+    def begin(k, q, o):
+        for j in range(len(parts)):
+            piece(k, q, j).start()
+        pltpu.make_async_copy(o, (out_e, out_o)[k], sems.at[k, 3]).start()
+
     for k in range(2):
         pick = core[0] if k == 0 else 1 - core[0]
-
-        def begin(q, o, m):
-            pltpu.make_async_copy(q.at[pl.ds(0, hw)], turned[k].at[pl.ds(0, hw)], sems.at[k, 0]).start()
-            pltpu.make_async_copy(
-                q.at[pl.ds(hw, 2 * hw)], turned[k].at[pl.ds(hw + gap, 2 * hw)], sems.at[k, 1]
-            ).start()
-            pltpu.make_async_copy(o, (out_e, out_o)[k], sems.at[k, 2]).start()
-            pltpu.make_async_copy(m, (mod_e, mod_o)[k], sems.at[k, 3]).start()
-
-        pl.when(pick == 0)(lambda: begin(qkv, out, mod))
-        pl.when(pick != 0)(lambda: begin(qkv2, out2, mod2))
-        turned[k][hw : hw + gap, :] = jnp.zeros((gap, qkv.shape[1]), BF16)
+        pl.when(pick == 0)(functools.partial(begin, k, qkv, out))
+        pl.when(pick != 0)(functools.partial(begin, k, qkv2, out2))
+        turned[k][hw : hw + gap, :] = jnp.zeros((gap, model), BF16)
+    columns = turned[0].shape[0]
+    halves = ((0, columns // 2 // LANES * LANES), (columns // 2 // LANES * LANES, columns))
     back = []
     for k in range(2):
-        pltpu.make_async_copy(qkv.at[pl.ds(0, hw)], turned[k].at[pl.ds(0, hw)], sems.at[k, 0]).wait()
-        pltpu.make_async_copy(
-            qkv.at[pl.ds(hw, 2 * hw)], turned[k].at[pl.ds(hw + gap, 2 * hw)], sems.at[k, 1]
-        ).wait()
-        for j in range(turned[k].shape[0] // LANES):
-            done[k][:, j * LANES : (j + 1) * LANES] = turned[k][j * LANES : (j + 1) * LANES, :].T
-        back.append(pltpu.make_async_copy(done[k], (even, odd)[k], sems.at[k, 4]))
-        back[-1].start()
+        arrived = 0
+        for n, (low, high) in enumerate(halves):
+            while arrived < len(parts) and parts[arrived][1] < high:
+                piece(k, qkv, arrived).wait()
+                arrived += 1
+            for j in range(low, high, LANES):
+                done[k][:, j : j + LANES] = turned[k][j : j + LANES, :].T
+            back.append(
+                pltpu.make_async_copy(
+                    done[k].at[:, pl.ds(low, high - low)],
+                    (even, odd)[k].at[:, pl.ds(low, high - low)],
+                    sems.at[k, 4 + n],
+                )
+            )
+            back[-1].start()
     for k in range(2):
-        pltpu.make_async_copy(out, (out_e, out_o)[k], sems.at[k, 2]).wait()
-        pltpu.make_async_copy(mod, (mod_e, mod_o)[k], sems.at[k, 3]).wait()
-        back[k].wait()
+        pltpu.make_async_copy(out, (out_e, out_o)[k], sems.at[k, 3]).wait()
+    for copy in back:
+        copy.wait()
 
 
 def place_of(ids, step, per_core):
@@ -140,6 +152,11 @@
     middle = x + factors[2:3] * dot(mixed, out[...])
     y[...] = middle
     g[...] = norm_modulate(middle, factors[3:4], factors[4:5])
+
+
+def first_kernel(per_core, ids, frames, mod, qkv, out, y, g):
+    video = ids[1] * per_core
+    spatial_part(frames[video].astype(F32), mod[video], qkv, out, y, g)
 
 
 def head_kernel(per_core, ids, step, frames, arriving, mod, qkv, out, y, g, x_v, sem):
@@ -174,7 +191,10 @@
     store.wait()
 
 
-def tail_kernel(per_core, ids, step, returned, y_in, mod, tout, kept_in, x, kept, x_v, sem):
+def tail_kernel(
+    per_core, ids, step, returned, y_in, mod, tout, kept_in, x, kept, following, x_v, sem
+):
+    following[0] = step[0] + 1
     video, slot = place_of(ids, step, per_core)
     leaving = (y_in[...] + mod[video][5:6] * dot(returned[...], tout[...])).astype(BF16)
     x_v[...] = leaving
@@ -187,9 +207,10 @@
 SMEM = pl.BlockSpec(memory_space=pltpu.SMEM)
 VMEM = pl.BlockSpec(memory_space=pltpu.VMEM)
 ANY = pl.BlockSpec(memory_space=pl.ANY)
-
-
-def call(kernel, name, ins, outs, specs, scratch, aliases={}):
+HBM = pl.BlockSpec(memory_space=pltpu.HBM)
+
+
+def call(kernel, name, ins, outs, specs, scratch, aliases={}, limit=24):
     return pl.pallas_call(
         kernel,
         name=name,
@@ -198,7 +219,7 @@
         out_shape=outs,
         scratch_shapes=scratch,
         input_output_aliases=aliases,
-        compiler_params=pltpu.CompilerParams(vmem_limit_bytes=24 * 2**20),
+        compiler_params=pltpu.CompilerParams(vmem_limit_bytes=limit * 2**20),
     )
 
 
@@ -219,36 +240,36 @@
         return lax.ppermute(a, "section", [(i, i ^ 1) for i in range(sections)])
 
     shape = jax.ShapeDtypeStruct
-    factors_s = shape(modulation.shape[1:], F32)
     qkv_s, out_s = shape((model, columns), BF16), shape((hw, model), BF16)
     prepare = call(
-        prepare_kernel, "prepare", [SMEM] + [ANY] * 6, [qkv_s] * 2 + [out_s] * 2 + [factors_s] * 2,
-        [ANY] * 6,
+        prepare_kernel, "prepare", [SMEM] + [HBM] * 4, [qkv_s] * 2 + [out_s] * 2, [ANY] * 4,
         [pltpu.VMEM((columns, model), BF16)] * 2 + [pltpu.VMEM((model, columns), BF16)] * 2
-        + [pltpu.SemaphoreType.DMA((2, 5))],
-    )
+        + [pltpu.SemaphoreType.DMA((2, 6))],
+        limit=60,
+    )
+    chain = (stage + core) % 2
     core_id = core.reshape(1).astype(jnp.int32)
-    ids = jnp.stack([stage, core]).astype(jnp.int32)
-    mod2 = swapped(modulation)
-
-    def prepared(qkv, out, rows, rows2):
+    ids = jnp.stack([stage, chain]).astype(jnp.int32)
+    mod = modulation[0]
+    mod2 = swapped(mod)
+    mod_e, mod_o = jnp.where(core == 0, mod, mod2), jnp.where(core == 0, mod2, mod)
+
+    def prepared(qkv, out, core_id):
         qkv2, out2 = swapped(qkv), swapped(out)
         return prepare(
-            core_id, jnp.swapaxes(qkv[0], 0, 1), jnp.swapaxes(qkv2[0], 0, 1), out[0], out2[0],
-            rows, rows2,
+            core_id, jnp.swapaxes(qkv[0], 0, 1), jnp.swapaxes(qkv2[0], 0, 1), out[0], out2[0]
         )
 
-    sqkv_e, sqkv_o, sout_e, sout_o, mod_e, mod_o = prepared(
-        spatial_qkv, spatial_out, modulation[0], mod2[0]
-    )
-    tqkv_e, tqkv_o, tout_e, tout_o, _, _ = prepared(
-        temporal_qkv, temporal_out, modulation[0], mod2[0]
-    )
+    sqkv_e, sqkv_o, sout_e, sout_o = prepared(spatial_qkv, spatial_out, core_id)
     source = frames_in.reshape(videos, tokens, model)
 
     x_s, y_s = shape((tokens, model), BF16), shape((tokens, model), F32)
     kept_s = shape((per_core + 1, tokens, model), BF16)
     hold = [pltpu.VMEM((tokens, model), BF16), pltpu.SemaphoreType.DMA]
+    first = call(
+        functools.partial(first_kernel, per_core), "first", [SMEM] + [VMEM] * 4,
+        [y_s, x_s], [VMEM, VMEM], [],
+    )
     head = call(
         functools.partial(head_kernel, per_core), "head",
         [SMEM, SMEM, ANY, ANY, VMEM, VMEM, VMEM], [y_s, x_s], [VMEM, VMEM], hold,
@@ -263,34 +284,44 @@
     )
     tail = call(
         functools.partial(tail_kernel, per_core), "tail",
-        [SMEM, SMEM] + [VMEM] * 4 + [ANY], [x_s, kept_s], [VMEM, ANY], hold, {6: 1},
+        [SMEM, SMEM] + [VMEM] * 4 + [ANY], [x_s, kept_s, shape((1,), jnp.int32)],
+        [VMEM, ANY, SMEM], hold, {6: 1},
     )
 
     def exchange(a):
         out = lax.all_to_all(a.reshape(ranks, share, a.shape[1]), "seq", 0, 0, tiled=True)
         return out.reshape(a.shape)
 
-    def advance(step, carried):
-        even, odd, arriving = carried
-        at = step.reshape(1)
-        y, g = head(ids, at, source, arriving, mod_e, sqkv_e, sout_e)
+    kept = jnp.zeros(kept_s.shape, BF16)
+    y, g = first(ids, source, mod_e, sqkv_e, sout_e)
+    g, core_id = lax.optimization_barrier((g, core_id))
+    tqkv_e, tqkv_o, tout_e, tout_o = prepared(temporal_qkv, temporal_out, core_id)
+
+    def middle(at, even, y, g):
         mixed = temporal(exchange(g), tqkv_e)
         y, g, even = joint(
             ids, at, exchange(mixed), y, mod_e, mod_o, tout_e, sqkv_o, sout_o, even
         )
-        mixed = temporal(exchange(g), tqkv_o)
-        x, odd = tail(ids, at, exchange(mixed), y, mod_o, tout_o, odd)
-        arriving = lax.ppermute(x, "section", [(i, i + 2) for i in range(sections - 2)])
-        return even, odd, arriving
-
-    kept = jnp.zeros(kept_s.shape, BF16)
-    even, odd, _ = lax.fori_loop(
-        0, stages + per_core - 1, advance, (kept, kept, jnp.zeros((tokens, model), BF16))
+        return even, y, exchange(temporal(exchange(g), tqkv_o))
+
+    def advance(step, carried):
+        odd, even, y, returned = carried
+        x, odd, at = tail(ids, step.reshape(1), returned, y, mod_o, tout_o, odd)
+        onward = [(i, (i + 2) ^ 1) for i in range(sections - 2)]
+        arriving = lax.ppermute(x, "section", onward)
+        y, g = head(ids, at, source, arriving, mod_e, sqkv_e, sout_e)
+        return odd, *middle(at, even, y, g)
+
+    last = stages + per_core - 2
+    carried = kept, *middle(jnp.zeros((1,), jnp.int32), kept, y, g)
+    odd, even, y, returned = lax.fori_loop(0, last, advance, carried)
+    _, odd, _ = tail(
+        ids, jnp.full((1,), last, jnp.int32), returned, y, mod_o, tout_o, odd
     )
     even, odd = even[:per_core], odd[:per_core]
     own = jnp.where(core == 0, even, odd)
     other = swapped(jnp.where(core == 0, odd, even))
-    low, high = jnp.where(core == 0, own, other), jnp.where(core == 0, other, own)
+    low, high = jnp.where(chain == 0, own, other), jnp.where(chain == 0, other, own)
     hidden = jnp.concatenate([low, high], axis=0)
     return hidden.reshape((1,) + frames_in.shape)
 

time: 687 us -> 805 us (1.17)
  Pallas kernels: 137 us -> 273 us
  waiting for transfers between devices: 78.3 us -> 187 us
  blocking collectives: 382 us -> 280 us
  starting transfers between devices: 74 us -> 57.8 us
    pallas_call x2, Pallas kernels: 15.2 us -> 123 us  [prepared(): prepare(core_id, jnp.swapaxes(qkv[0], 0, 1), jnp.swapaxes(qkv2[0], 0, 1),...]
    all_to_all x36 -> x26, blocking collectives: 382 us -> 280 us  [exchange(): lax.all_to_all(a.reshape(ranks, share, a.shape[1]), 'seq', 0, 0, tiled=True)]
    all_to_all x0 -> x10, waiting for transfers between devices: none -> 60.8 us  [exchange(): lax.all_to_all(a.reshape(ranks, share, a.shape[1]), 'seq', 0, 0, tiled=True)]
    ppermute x6, starting transfers between devices: 62.3 us -> 8.97 us  [swapped(): return lax.ppermute(a, 'section', [(i, i ^ 1) for i in range(sections)])]
    ppermute x9 -> x8, waiting for transfers between devices: 62.4 us -> 110 us  [advance(): arriving = lax.ppermute(x, 'section', onward)]
    all_to_all x0 -> x10, starting transfers between devices: none -> 38.5 us  [exchange(): lax.all_to_all(a.reshape(ranks, share, a.shape[1]), 'seq', 0, 0, tiled=True)]
    pallas_call x36 -> x37, Pallas kernels: 67.1 us -> 105 us  [the longest x9 42.5 us: middle(): joint(ids, at, exchange(mixed), y, mod_e, mod_o, tout_e, sqkv_o, sout_o,...]
    pallas_call x9 -> x8, Pallas kernels: 54.5 us -> 44.7 us  [advance(): y, g = head(ids, at, source, arriving, mod_e, sqkv_e, sout_e)]
  transfers between devices with their start and end apart: 15 -> 24, of which waited for: 11 -> 19; matrix products, arithmetic and copies ran while one was open for 0% -> 0% of each run, Pallas kernels for 1% -> 16%
where the time goes in v3:
time: 805 us; the launch traced here: 803 us
  blocking collectives  280 us (35%)
  Pallas kernels  273 us (34%)
  waiting for transfers between devices  187 us (23%)
  starting transfers between devices  57.8 us (7%)
    all_to_all x26, blocking collectives, exchange(): lax.all_to_all(a.reshape(ranks, share, a.shape[1]), 'seq', 0, 0, tiled=True)  280 us
    pallas_call x2, Pallas kernels, prepared(): prepare(core_id, jnp.swapaxes(qkv[0], 0, 1), jnp.swapaxes(qkv2[0], 0, 1),...  123 us
    ppermute x8, waiting for transfers between devices, advance(): arriving = lax.ppermute(x, 'section', onward)  110 us
    all_to_all x10, waiting for transfers between devices, exchange(): lax.all_to_all(a.reshape(ranks, share, a.shape[1]), 'seq', 0, 0, tiled=True)  60.8 us
    pallas_call x8, Pallas kernels, advance(): y, g = head(ids, at, source, arriving, mod_e, sqkv_e, sout_e)  44.7 us
    pallas_call x9, Pallas kernels, middle(): joint(ids, at, exchange(mixed), y, mod_e, mod_o, tout_e, sqkv_o, sout_o,...  42.5 us
    all_to_all x10, starting transfers between devices, exchange(): lax.all_to_all(a.reshape(ranks, share, a.shape[1]), 'seq', 0, 0, tiled=True)  38.5 us
    pallas_call x8, Pallas kernels, advance(): x, odd, at = tail(ids, step.reshape(1), returned, y, mod_o, tout_o, odd)  21 us
  transfers between devices with their start and end apart: 24, of which 19 were waited for; matrix products, arithmetic and copies ran while one was open for 0% of the time, Pallas kernels for 16%

profile of v3, /device:TPU:225, one launch (start us, length us, event | category | flops | bytes accessed | tf_op | source)
XLA Modules:
  0.0 802.8 jit_solution(8277580322891248556)
XLA Ops:
  2.8 14.3 %collective-permute-done.1 = f32[4,6,1152]{2,1,0:T(8,128)S(1)} collective-permute-done((f32[4,6,1152]{2,1,0:T(8,128)S(1)}, f32[4,6,1152]{2,1,0:T(8,128)S(1)}, u32[]{:S(2)}, u32[]{:S(2)}) %collective-permute-start.1) | collective-permute-done | bytes 110624 | tf_op jit(solution)/shard_map/ppermute | solution.py:240
  19.2 41.4 %prepare.2 = (bf16[1152,1792]{1,0:T(8,128)(2,1)}, bf16[1152,1792]{1,0:T(8,128)(2,1)}, bf16[576,1152]{1,0:T(8,128)(2,1)}, bf16[576,1152]{1,0:T(8,128)(2,1)S(1)}) custom-call(s32[1]{0:T(128)} %bitcast.13.core, bf16[1728,1152]{1,0:T(8,128)(2,1)} %bitcast.81, bf16[1728,1152]{1,0:T(8,128)(2,1)} %bitcast.17.qkv2, bf16[576,1152]{1,0:T(8,128)(2,1)} %bitcast.83, ...), custom_call_target="tpu_custom_call" | custom-call | tf_op jit(solution)/shard_map/prepare/pallas_call | solution.py:259
  73.7 81.6 %prepare.3 = (bf16[1152,1792]{1,0:T(8,128)(2,1)}, bf16[1152,1792]{1,0:T(8,128)(2,1)}, bf16[576,1152]{1,0:T(8,128)(2,1)}, bf16[576,1152]{1,0:T(8,128)(2,1)}) custom-call(s32[1]{0:T(128)} %bitcast.13.core, bf16[1728,1152]{1,0:T(8,128)(2,1)} %bitcast.82, bf16[1728,1152]{1,0:T(8,128)(2,1)} %bitcast.25.qkv2, bf16[576,1152]{1,0:T(8,128)(2,1)} %bitcast.84, ...), custom_call_target="tpu_custom_call" | custom-call | tf_op jit(solution)/shard_map/prepare/pallas_call | solution.py:259
  159.0 13.3 %all_to_all.60 = bf16[16,8,576]{2,1,0:T(8,128)(2,1)S(1)} all-to-all(bf16[16,8,576]{2,1,0:T(8,128)(2,1)S(1)} %bitcast.74), channel_id=1, replica_groups=mesh['section'=16,'seq'=16] {'seq'}, dimensions={0} | all-to-all | bytes 294912 | tf_op jit(solution)/shard_map/all_to_all | solution.py:292
  176.4 11.0 %all_to_all.61 = bf16[16,8,1152]{2,1,0:T(8,128)(2,1)S(1)} all-to-all(bf16[16,8,1152]{2,1,0:T(8,128)(2,1)S(1)} %bitcast.76), channel_id=1, replica_groups=mesh['section'=16,'seq'=16] {'seq'}, dimensions={0} | all-to-all | bytes 589824 | tf_op jit(solution)/shard_map/all_to_all | solution.py:292
  200.0 589.9 %while.19 = (s32[]{:T(128)}, bf16[3,128,1152]{2,1,0:T(8,128)(2,1)S(1)}, bf16[3,128,1152]{2,1,0:T(8,128)(2,1)S(1)}, f32[128,1152]{1,0:T(8,128)}, bf16[128,576]{1,...) while((s32[]{:T(128)}, ...), condition=%wide.region_1.2_spmd, body=%wide.region_0.1_spmd.sunk | while | flops 2 | bytes 68600216 | solution.py:317
  204.0 13.3 %collective-permute-done.arriving = bf16[128,1152]{1,0:T(8,128)(2,1)S(1)} collective-permute-done((bf16[128,1152]{1,0:T(8,128)(2,1)S(1)}, bf16[128,1152]{1,0:T(8,128)(2,1)S(1)}, u32[]{:S(2)}, u32[]{:S(2)}) %collective-permute-start) | collective-permute-done | bytes 294944 | tf_op jit(solution)/shard_map/while/body/eval_jaxpr/ppermute | solution.py:311
  222.9 10.9 %all_to_all.62 = bf16[16,8,1152]{2,1,0:T(8,128)(2,1)S(1)} all-to-all(bf16[16,8,1152]{2,1,0:T(8,128)(2,1)S(1)} %bitcast.71), channel_id=1, replica_groups=mesh['section'=16,'seq'=16] {'seq'}, dimensions={0} | all-to-all | bytes 589824 | tf_op jit(solution)/shard_map/while/body/eval_jaxpr/all_to_all | solution.py:292
  235.1 10.4 %all_to_all.63 = bf16[16,8,576]{2,1,0:T(8,128)(2,1)S(1)} all-to-all(bf16[16,8,576]{2,1,0:T(8,128)(2,1)S(1)} %bitcast.68), channel_id=1, replica_groups=mesh['section'=16,'seq'=16] {'seq'}, dimensions={0} | all-to-all | bytes 294912 | tf_op jit(solution)/shard_map/while/body/eval_jaxpr/all_to_all | solution.py:292
  250.4 10.9 %all_to_all.64 = bf16[16,8,1152]{2,1,0:T(8,128)(2,1)S(1)} all-to-all(bf16[16,8,1152]{2,1,0:T(8,128)(2,1)S(1)} %bitcast.70), channel_id=1, replica_groups=mesh['section'=16,'seq'=16] {'seq'}, dimensions={0} | all-to-all | bytes 589824 | tf_op jit(solution)/shard_map/while/body/eval_jaxpr/all_to_all | solution.py:292
  277.5 14.4 %collective-permute-done.arriving = bf16[128,1152]{1,0:T(8,128)(2,1)S(1)} collective-permute-done((bf16[128,1152]{1,0:T(8,128)(2,1)S(1)}, bf16[128,1152]{1,0:T(8,128)(2,1)S(1)}, u32[]{:S(2)}, u32[]{:S(2)}) %collective-permute-start) | collective-permute-done | bytes 294944 | tf_op jit(solution)/shard_map/while/body/eval_jaxpr/ppermute | solution.py:311
  297.4 10.9 %all_to_all.62 = bf16[16,8,1152]{2,1,0:T(8,128)(2,1)S(1)} all-to-all(bf16[16,8,1152]{2,1,0:T(8,128)(2,1)S(1)} %bitcast.71), channel_id=1, replica_groups=mesh['section'=16,'seq'=16] {'seq'}, dimensions={0} | all-to-all | bytes 589824 | tf_op jit(solution)/shard_map/while/body/eval_jaxpr/all_to_all | solution.py:292
  324.8 11.0 %all_to_all.64 = bf16[16,8,1152]{2,1,0:T(8,128)(2,1)S(1)} all-to-all(bf16[16,8,1152]{2,1,0:T(8,128)(2,1)S(1)} %bitcast.70), channel_id=1, replica_groups=mesh['section'=16,'seq'=16] {'seq'}, dimensions={0} | all-to-all | bytes 589824 | tf_op jit(solution)/shard_map/while/body/eval_jaxpr/all_to_all | solution.py:292
  352.0 14.6 %collective-permute-done.arriving = bf16[128,1152]{1,0:T(8,128)(2,1)S(1)} collective-permute-done((bf16[128,1152]{1,0:T(8,128)(2,1)S(1)}, bf16[128,1152]{1,0:T(8,128)(2,1)S(1)}, u32[]{:S(2)}, u32[]{:S(2)}) %collective-permute-start) | collective-permute-done | bytes 294944 | tf_op jit(solution)/shard_map/while/body/eval_jaxpr/ppermute | solution.py:311
  372.2 10.9 %all_to_all.62 = bf16[16,8,1152]{2,1,0:T(8,128)(2,1)S(1)} all-to-all(bf16[16,8,1152]{2,1,0:T(8,128)(2,1)S(1)} %bitcast.71), channel_id=1, replica_groups=mesh['section'=16,'seq'=16] {'seq'}, dimensions={0} | all-to-all | bytes 589824 | tf_op jit(solution)/shard_map/while/body/eval_jaxpr/all_to_all | solution.py:292
  384.4 10.4 %all_to_all.63 = bf16[16,8,576]{2,1,0:T(8,128)(2,1)S(1)} all-to-all(bf16[16,8,576]{2,1,0:T(8,128)(2,1)S(1)} %bitcast.68), channel_id=1, replica_groups=mesh['section'=16,'seq'=16] {'seq'}, dimensions={0} | all-to-all | bytes 294912 | tf_op jit(solution)/shard_map/while/body/eval_jaxpr/all_to_all | solution.py:292
  399.7 10.9 %all_to_all.64 = bf16[16,8,1152]{2,1,0:T(8,128)(2,1)S(1)} all-to-all(bf16[16,8,1152]{2,1,0:T(8,128)(2,1)S(1)} %bitcast.70), channel_id=1, replica_groups=mesh['section'=16,'seq'=16] {'seq'}, dimensions={0} | all-to-all | bytes 589824 | tf_op jit(solution)/shard_map/while/body/eval_jaxpr/all_to_all | solution.py:292
  426.7 12.5 %collective-permute-done.arriving = bf16[128,1152]{1,0:T(8,128)(2,1)S(1)} collective-permute-done((bf16[128,1152]{1,0:T(8,128)(2,1)S(1)}, bf16[128,1152]{1,0:T(8,128)(2,1)S(1)}, u32[]{:S(2)}, u32[]{:S(2)}) %collective-permute-start) | collective-permute-done | bytes 294944 | tf_op jit(solution)/shard_map/while/body/eval_jaxpr/ppermute | solution.py:311
  444.9 10.8 %all_to_all.62 = bf16[16,8,1152]{2,1,0:T(8,128)(2,1)S(1)} all-to-all(bf16[16,8,1152]{2,1,0:T(8,128)(2,1)S(1)} %bitcast.71), channel_id=1, replica_groups=mesh['section'=16,'seq'=16] {'seq'}, dimensions={0} | all-to-all | bytes 589824 | tf_op jit(solution)/shard_map/while/body/eval_jaxpr/all_to_all | solution.py:292
  472.2 10.7 %all_to_all.64 = bf16[16,8,1152]{2,1,0:T(8,128)(2,1)S(1)} all-to-all(bf16[16,8,1152]{2,1,0:T(8,128)(2,1)S(1)} %bitcast.70), channel_id=1, replica_groups=mesh['section'=16,'seq'=16] {'seq'}, dimensions={0} | all-to-all | bytes 589824 | tf_op jit(solution)/shard_map/while/body/eval_jaxpr/all_to_all | solution.py:292
  499.1 13.9 %collective-permute-done.arriving = bf16[128,1152]{1,0:T(8,128)(2,1)S(1)} collective-permute-done((bf16[128,1152]{1,0:T(8,128)(2,1)S(1)}, bf16[128,1152]{1,0:T(8,128)(2,1)S(1)}, u32[]{:S(2)}, u32[]{:S(2)}) %collective-permute-start) | collective-permute-done | bytes 294944 | tf_op jit(solution)/shard_map/while/body/eval_jaxpr/ppermute | solution.py:311
  518.6 10.9 %all_to_all.62 = bf16[16,8,1152]{2,1,0:T(8,128)(2,1)S(1)} all-to-all(bf16[16,8,1152]{2,1,0:T(8,128)(2,1)S(1)} %bitcast.71), channel_id=1, replica_groups=mesh['section'=16,'seq'=16] {'seq'}, dimensions={0} | all-to-all | bytes 589824 | tf_op jit(solution)/shard_map/while/body/eval_jaxpr/all_to_all | solution.py:292
  545.9 10.7 %all_to_all.64 = bf16[16,8,1152]{2,1,0:T(8,128)(2,1)S(1)} all-to-all(bf16[16,8,1152]{2,1,0:T(8,128)(2,1)S(1)} %bitcast.70), channel_id=1, replica_groups=mesh['section'=16,'seq'=16] {'seq'}, dimensions={0} | all-to-all | bytes 589824 | tf_op jit(solution)/shard_map/while/body/eval_jaxpr/all_to_all | solution.py:292
  572.9 13.9 %collective-permute-done.arriving = bf16[128,1152]{1,0:T(8,128)(2,1)S(1)} collective-permute-done((bf16[128,1152]{1,0:T(8,128)(2,1)S(1)}, bf16[128,1152]{1,0:T(8,128)(2,1)S(1)}, u32[]{:S(2)}, u32[]{:S(2)}) %collective-permute-start) | collective-permute-done | bytes 294944 | tf_op jit(solution)/shard_map/while/body/eval_jaxpr/ppermute | solution.py:311
  592.4 10.8 %all_to_all.62 = bf16[16,8,1152]{2,1,0:T(8,128)(2,1)S(1)} all-to-all(bf16[16,8,1152]{2,1,0:T(8,128)(2,1)S(1)} %bitcast.71), channel_id=1, replica_groups=mesh['section'=16,'seq'=16] {'seq'}, dimensions={0} | all-to-all | bytes 589824 | tf_op jit(solution)/shard_map/while/body/eval_jaxpr/all_to_all | solution.py:292
  619.7 10.7 %all_to_all.64 = bf16[16,8,1152]{2,1,0:T(8,128)(2,1)S(1)} all-to-all(bf16[16,8,1152]{2,1,0:T(8,128)(2,1)S(1)} %bitcast.70), channel_id=1, replica_groups=mesh['section'=16,'seq'=16] {'seq'}, dimensions={0} | all-to-all | bytes 589824 | tf_op jit(solution)/shard_map/while/body/eval_jaxpr/all_to_all | solution.py:292
  646.6 13.7 %collective-permute-done.arriving = bf16[128,1152]{1,0:T(8,128)(2,1)S(1)} collective-permute-done((bf16[128,1152]{1,0:T(8,128)(2,1)S(1)}, bf16[128,1152]{1,0:T(8,128)(2,1)S(1)}, u32[]{:S(2)}, u32[]{:S(2)}) %collective-permute-start) | collective-permute-done | bytes 294944 | tf_op jit(solution)/shard_map/while/body/eval_jaxpr/ppermute | solution.py:311
  665.9 10.9 %all_to_all.62 = bf16[16,8,1152]{2,1,0:T(8,128)(2,1)S(1)} all-to-all(bf16[16,8,1152]{2,1,0:T(8,128)(2,1)S(1)} %bitcast.71), channel_id=1, replica_groups=mesh['section'=16,'seq'=16] {'seq'}, dimensions={0} | all-to-all | bytes 589824 | tf_op jit(solution)/shard_map/while/body/eval_jaxpr/all_to_all | solution.py:292
  693.2 10.7 %all_to_all.64 = bf16[16,8,1152]{2,1,0:T(8,128)(2,1)S(1)} all-to-all(bf16[16,8,1152]{2,1,0:T(8,128)(2,1)S(1)} %bitcast.70), channel_id=1, replica_groups=mesh['section'=16,'seq'=16] {'seq'}, dimensions={0} | all-to-all | bytes 589824 | tf_op jit(solution)/shard_map/while/body/eval_jaxpr/all_to_all | solution.py:292
  720.2 13.8 %collective-permute-done.arriving = bf16[128,1152]{1,0:T(8,128)(2,1)S(1)} collective-permute-done((bf16[128,1152]{1,0:T(8,128)(2,1)S(1)}, bf16[128,1152]{1,0:T(8,128)(2,1)S(1)}, u32[]{:S(2)}, u32[]{:S(2)}) %collective-permute-start) | collective-permute-done | bytes 294944 | tf_op jit(solution)/shard_map/while/body/eval_jaxpr/ppermute | solution.py:311
  739.6 10.9 %all_to_all.62 = bf16[16,8,1152]{2,1,0:T(8,128)(2,1)S(1)} all-to-all(bf16[16,8,1152]{2,1,0:T(8,128)(2,1)S(1)} %bitcast.71), channel_id=1, replica_groups=mesh['section'=16,'seq'=16] {'seq'}, dimensions={0} | all-to-all | bytes 589824 | tf_op jit(solution)/shard_map/while/body/eval_jaxpr/all_to_all | solution.py:292
  766.9 10.7 %all_to_all.64 = bf16[16,8,1152]{2,1,0:T(8,128)(2,1)S(1)} all-to-all(bf16[16,8,1152]{2,1,0:T(8,128)(2,1)S(1)} %bitcast.70), channel_id=1, replica_groups=mesh['section'=16,'seq'=16] {'seq'}, dimensions={0} | all-to-all | bytes 589824 | tf_op jit(solution)/shard_map/while/body/eval_jaxpr/all_to_all | solution.py:292
  (214 shorter events, 336.3 us)
Async XLA Ops:
  0.0 18.0 %collective-permute-start.2 = (bf16[1,1152,1728]{1,2,0:T(8,128)(2,1)}, bf16[1,1152,1728]{1,2,0:T(8,128)(2,1)}, u32[]{:S(2)}, u32[]{:S(2)}) collective-permute-start(bf16[1,1152,1728]{1,2,0:T(8,128)(2,1)} %param.9), channel_id=1, source_target_pairs={{0,16},{16,0},{32,48},{48,32},{64,80},{80,64},{96,112},{112,96},{1... | collective-permute-start | bytes 11943944 | tf_op jit(solution)/shard_map/ppermute | solution.py:240
  0.7 73.0 %collective-permute-start.4 = (bf16[1,1152,1728]{1,2,0:T(8,128)(2,1)}, bf16[1,1152,1728]{1,2,0:T(8,128)(2,1)}, u32[]{:S(2)}, u32[]{:S(2)}) collective-permute-start(bf16[1,1152,1728]{1,2,0:T(8,128)(2,1)} %param.11), channel_id=1, source_target_pairs={{0,16},{16,0},{32,48},{48,32},{64,80},{80,64},{96,112},{112,96},{1... | collective-permute-start | bytes 11943944 | tf_op jit(solution)/shard_map/ppermute | solution.py:240
  0.7 17.3 %collective-permute-start.3 = (bf16[1,576,1152]{2,1,0:T(8,128)(2,1)}, bf16[1,576,1152]{2,1,0:T(8,128)(2,1)S(1)}, u32[]{:S(2)}, u32[]{:S(2)}) collective-permute-start(bf16[1,576,1152]{2,1,0:T(8,128)(2,1)} %param.10), channel_id=1, source_target_pairs={{0,16},{16,0},{32,48},{48,32},{64,80},{80,64},{96,112},{112,96},{1... | collective-permute-start | bytes 3981320 | tf_op jit(solution)/shard_map/ppermute | solution.py:240
  1.2 72.5 %collective-permute-start.5 = (bf16[1,576,1152]{2,1,0:T(8,128)(2,1)}, bf16[1,576,1152]{2,1,0:T(8,128)(2,1)}, u32[]{:S(2)}, u32[]{:S(2)}) collective-permute-start(bf16[1,576,1152]{2,1,0:T(8,128)(2,1)} %param.12), channel_id=1, source_target_pairs={{0,16},{16,0},{32,48},{48,32},{64,80},{80,64},{96,112},{112,96},{1... | collective-permute-start | bytes 3981320 | tf_op jit(solution)/shard_map/ppermute | solution.py:240
  2.1 14.9 %collective-permute-start.1 = (f32[4,6,1152]{2,1,0:T(8,128)S(1)}, f32[4,6,1152]{2,1,0:T(8,128)S(1)}, u32[]{:S(2)}, u32[]{:S(2)}) collective-permute-start(f32[4,6,1152]{2,1,0:T(8,128)S(1)} %bitcast.86), channel_id=1, source_target_pairs={{0,16},{16,0},{32,48},{48,32},{64,80},{80,64},{96,112},{112,96},{1... | collective-permute-start | bytes 331784 | tf_op jit(solution)/shard_map/ppermute | solution.py:240
  18.0 154.4 %copy-start.11 = (f32[4,6,1152]{2,1,0:T(8,128)}, f32[4,6,1152]{2,1,0:T(8,128)S(1)}, u32[]{:S(2)}) copy-start(f32[4,6,1152]{2,1,0:T(8,128)S(1)} %get-tuple-element.459.following.mod) | copy-start | bytes 331780
  18.0 154.4 %copy-start.13 = (f32[4,6,1152]{2,1,0:T(8,128)}, f32[4,6,1152]{2,1,0:T(8,128)S(1)}, u32[]{:S(2)}) copy-start(f32[4,6,1152]{2,1,0:T(8,128)S(1)} %get-tuple-element.462.mod) | copy-start | bytes 331780
  60.6 111.8 %copy-start.5 = (bf16[576,1152]{1,0:T(8,128)(2,1)}, bf16[576,1152]{1,0:T(8,128)(2,1)S(1)}, u32[]{:S(2)}) copy-start(bf16[576,1152]{1,0:T(8,128)(2,1)S(1)} %get-tuple-element.468.out) | copy-start | bytes 3981316
  66.9 88.4 %all-to-all-start.4 = ((bf16[16,8,1152]{2,1,0:T(8,128)(2,1)}), bf16[16,8,1152]{2,1,0:T(8,128)(2,1)S(1)}, u32[]{:S(2)}, u32[]{:S(2)}) async-start(bf16[16,8,1152]{2,1,0:T(8,128)(2,1)} %bitcast.20), calls=%async_computation.4 | async-start | bytes 589824 | tf_op jit(solution)/shard_map/all_to_all | solution.py:292
  189.5 10.5 %all-to-all-start.7 = ((bf16[16,8,576]{2,1,0:T(8,128)(2,1)}), bf16[16,8,576]{2,1,0:T(8,128)(2,1)S(1)}, u32[]{:S(2)}, u32[]{:S(2)}) async-start(bf16[16,8,576]{2,1,0:T(8,128)(2,1)} %bitcast.32), calls=%async_computation.7 | async-start | bytes 327680 | tf_op jit(solution)/shard_map/all_to_all | solution.py:292
  202.7 14.6 %collective-permute-start = (bf16[128,1152]{1,0:T(8,128)(2,1)S(1)}, bf16[128,1152]{1,0:T(8,128)(2,1)S(1)}, u32[]{:S(2)}, u32[]{:S(2)}) collective-permute-start(bf16[128,1152]{1,0:T(8,128)(2,1)S(1)} %get-tuple-element.447), channel_id=1, source_target_pairs={{0,48},{16,32},{32,80},{48,64},{64,112},{80,96},{96,144},{112,128}... | collective-permute-start | bytes 884744 | tf_op jit(solution)/shard_map/while/body/eval_jaxpr/ppermute | solution.py:311
  217.3 28.3 %copy-start.8 = (bf16[576,1152]{1,0:T(8,128)(2,1)S(1)}, bf16[576,1152]{1,0:T(8,128)(2,1)}, u32[]{:S(2)}) copy-start(bf16[576,1152]{1,0:T(8,128)(2,1)} %get-tuple-element.502.tout) | copy-start | bytes 3981316 | tf_op jit(solution)/shard_map/while
  263.2 10.3 %all-to-all-start.3 = ((bf16[16,8,576]{2,1,0:T(8,128)(2,1)}), bf16[16,8,576]{2,1,0:T(8,128)(2,1)S(1)}, u32[]{:S(2)}, u32[]{:S(2)}) async-start(bf16[16,8,576]{2,1,0:T(8,128)(2,1)} %bitcast.64), calls=%async_computation.3 | async-start | bytes 327680 | tf_op jit(solution)/shard_map/while/body/eval_jaxpr/all_to_all | solution.py:292
  276.2 15.7 %collective-permute-start = (bf16[128,1152]{1,0:T(8,128)(2,1)S(1)}, bf16[128,1152]{1,0:T(8,128)(2,1)S(1)}, u32[]{:S(2)}, u32[]{:S(2)}) collective-permute-start(bf16[128,1152]{1,0:T(8,128)(2,1)S(1)} %get-tuple-element.447), channel_id=1, source_target_pairs={{0,48},{16,32},{32,80},{48,64},{64,112},{80,96},{96,144},{112,128}... | collective-permute-start | bytes 884744 | tf_op jit(solution)/shard_map/while/body/eval_jaxpr/ppermute | solution.py:311
  291.8 28.1 %copy-start.8 = (bf16[576,1152]{1,0:T(8,128)(2,1)S(1)}, bf16[576,1152]{1,0:T(8,128)(2,1)}, u32[]{:S(2)}) copy-start(bf16[576,1152]{1,0:T(8,128)(2,1)} %get-tuple-element.502.tout) | copy-start | bytes 3981316 | tf_op jit(solution)/shard_map/while
  337.8 10.3 %all-to-all-start.3 = ((bf16[16,8,576]{2,1,0:T(8,128)(2,1)}), bf16[16,8,576]{2,1,0:T(8,128)(2,1)S(1)}, u32[]{:S(2)}, u32[]{:S(2)}) async-start(bf16[16,8,576]{2,1,0:T(8,128)(2,1)} %bitcast.64), calls=%async_computation.3 | async-start | bytes 327680 | tf_op jit(solution)/shard_map/while/body/eval_jaxpr/all_to_all | solution.py:292
  350.7 15.9 %collective-permute-start = (bf16[128,1152]{1,0:T(8,128)(2,1)S(1)}, bf16[128,1152]{1,0:T(8,128)(2,1)S(1)}, u32[]{:S(2)}, u32[]{:S(2)}) collective-permute-start(bf16[128,1152]{1,0:T(8,128)(2,1)S(1)} %get-tuple-element.447), channel_id=1, source_target_pairs={{0,48},{16,32},{32,80},{48,64},{64,112},{80,96},{96,144},{112,128}... | collective-permute-start | bytes 884744 | tf_op jit(solution)/shard_map/while/body/eval_jaxpr/ppermute | solution.py:311
  366.6 28.3 %copy-start.8 = (bf16[576,1152]{1,0:T(8,128)(2,1)S(1)}, bf16[576,1152]{1,0:T(8,128)(2,1)}, u32[]{:S(2)}) copy-start(bf16[576,1152]{1,0:T(8,128)(2,1)} %get-tuple-element.502.tout) | copy-start | bytes 3981316 | tf_op jit(solution)/shard_map/while
  412.5 10.3 %all-to-all-start.3 = ((bf16[16,8,576]{2,1,0:T(8,128)(2,1)}), bf16[16,8,576]{2,1,0:T(8,128)(2,1)S(1)}, u32[]{:S(2)}, u32[]{:S(2)}) async-start(bf16[16,8,576]{2,1,0:T(8,128)(2,1)} %bitcast.64), calls=%async_computation.3 | async-start | bytes 327680 | tf_op jit(solution)/shard_map/while/body/eval_jaxpr/all_to_all | solution.py:292
  425.4 13.8 %collective-permute-start = (bf16[128,1152]{1,0:T(8,128)(2,1)S(1)}, bf16[128,1152]{1,0:T(8,128)(2,1)S(1)}, u32[]{:S(2)}, u32[]{:S(2)}) collective-permute-start(bf16[128,1152]{1,0:T(8,128)(2,1)S(1)} %get-tuple-element.447), channel_id=1, source_target_pairs={{0,48},{16,32},{32,80},{48,64},{64,112},{80,96},{96,144},{112,128}... | collective-permute-start | bytes 884744 | tf_op jit(solution)/shard_map/while/body/eval_jaxpr/ppermute | solution.py:311
  484.9 10.3 %all-to-all-start.3 = ((bf16[16,8,576]{2,1,0:T(8,128)(2,1)}), bf16[16,8,576]{2,1,0:T(8,128)(2,1)S(1)}, u32[]{:S(2)}, u32[]{:S(2)}) async-start(bf16[16,8,576]{2,1,0:T(8,128)(2,1)} %bitcast.64), calls=%async_computation.3 | async-start | bytes 327680 | tf_op jit(solution)/shard_map/while/body/eval_jaxpr/all_to_all | solution.py:292
  497.8 15.2 %collective-permute-start = (bf16[128,1152]{1,0:T(8,128)(2,1)S(1)}, bf16[128,1152]{1,0:T(8,128)(2,1)S(1)}, u32[]{:S(2)}, u32[]{:S(2)}) collective-permute-start(bf16[128,1152]{1,0:T(8,128)(2,1)S(1)} %get-tuple-element.447), channel_id=1, source_target_pairs={{0,48},{16,32},{32,80},{48,64},{64,112},{80,96},{96,144},{112,128}... | collective-permute-start | bytes 884744 | tf_op jit(solution)/shard_map/while/body/eval_jaxpr/ppermute | solution.py:311
  558.7 10.3 %all-to-all-start.3 = ((bf16[16,8,576]{2,1,0:T(8,128)(2,1)}), bf16[16,8,576]{2,1,0:T(8,128)(2,1)S(1)}, u32[]{:S(2)}, u32[]{:S(2)}) async-start(bf16[16,8,576]{2,1,0:T(8,128)(2,1)} %bitcast.64), calls=%async_computation.3 | async-start | bytes 327680 | tf_op jit(solution)/shard_map/while/body/eval_jaxpr/all_to_all | solution.py:292
  571.6 15.2 %collective-permute-start = (bf16[128,1152]{1,0:T(8,128)(2,1)S(1)}, bf16[128,1152]{1,0:T(8,128)(2,1)S(1)}, u32[]{:S(2)}, u32[]{:S(2)}) collective-permute-start(bf16[128,1152]{1,0:T(8,128)(2,1)S(1)} %get-tuple-element.447), channel_id=1, source_target_pairs={{0,48},{16,32},{32,80},{48,64},{64,112},{80,96},{96,144},{112,128}... | collective-permute-start | bytes 884744 | tf_op jit(solution)/shard_map/while/body/eval_jaxpr/ppermute | solution.py:311
  632.4 10.3 %all-to-all-start.3 = ((bf16[16,8,576]{2,1,0:T(8,128)(2,1)}), bf16[16,8,576]{2,1,0:T(8,128)(2,1)S(1)}, u32[]{:S(2)}, u32[]{:S(2)}) async-start(bf16[16,8,576]{2,1,0:T(8,128)(2,1)} %bitcast.64), calls=%async_computation.3 | async-start | bytes 327680 | tf_op jit(solution)/shard_map/while/body/eval_jaxpr/all_to_all | solution.py:292
  645.3 15.0 %collective-permute-start = (bf16[128,1152]{1,0:T(8,128)(2,1)S(1)}, bf16[128,1152]{1,0:T(8,128)(2,1)S(1)}, u32[]{:S(2)}, u32[]{:S(2)}) collective-permute-start(bf16[128,1152]{1,0:T(8,128)(2,1)S(1)} %get-tuple-element.447), channel_id=1, source_target_pairs={{0,48},{16,32},{32,80},{48,64},{64,112},{80,96},{96,144},{112,128}... | collective-permute-start | bytes 884744 | tf_op jit(solution)/shard_map/while/body/eval_jaxpr/ppermute | solution.py:311
  660.3 28.1 %copy-start.8 = (bf16[576,1152]{1,0:T(8,128)(2,1)S(1)}, bf16[576,1152]{1,0:T(8,128)(2,1)}, u32[]{:S(2)}) copy-start(bf16[576,1152]{1,0:T(8,128)(2,1)} %get-tuple-element.502.tout) | copy-start | bytes 3981316 | tf_op jit(solution)/shard_map/while
  706.0 10.3 %all-to-all-start.3 = ((bf16[16,8,576]{2,1,0:T(8,128)(2,1)}), bf16[16,8,576]{2,1,0:T(8,128)(2,1)S(1)}, u32[]{:S(2)}, u32[]{:S(2)}) async-start(bf16[16,8,576]{2,1,0:T(8,128)(2,1)} %bitcast.64), calls=%async_computation.3 | async-start | bytes 327680 | tf_op jit(solution)/shard_map/while/body/eval_jaxpr/all_to_all | solution.py:292
  718.9 15.1 %collective-permute-start = (bf16[128,1152]{1,0:T(8,128)(2,1)S(1)}, bf16[128,1152]{1,0:T(8,128)(2,1)S(1)}, u32[]{:S(2)}, u32[]{:S(2)}) collective-permute-start(bf16[128,1152]{1,0:T(8,128)(2,1)S(1)} %get-tuple-element.447), channel_id=1, source_target_pairs={{0,48},{16,32},{32,80},{48,64},{64,112},{80,96},{96,144},{112,128}... | collective-permute-start | bytes 884744 | tf_op jit(solution)/shard_map/while/body/eval_jaxpr/ppermute | solution.py:311
  734.0 28.1 %copy-start.8 = (bf16[576,1152]{1,0:T(8,128)(2,1)S(1)}, bf16[576,1152]{1,0:T(8,128)(2,1)}, u32[]{:S(2)}) copy-start(bf16[576,1152]{1,0:T(8,128)(2,1)} %get-tuple-element.502.tout) | copy-start | bytes 3981316 | tf_op jit(solution)/shard_map/while
  779.7 10.3 %all-to-all-start.3 = ((bf16[16,8,576]{2,1,0:T(8,128)(2,1)}), bf16[16,8,576]{2,1,0:T(8,128)(2,1)S(1)}, u32[]{:S(2)}, u32[]{:S(2)}) async-start(bf16[16,8,576]{2,1,0:T(8,128)(2,1)} %bitcast.64), calls=%async_computation.3 | async-start | bytes 327680 | tf_op jit(solution)/shard_map/while/body/eval_jaxpr/all_to_all | solution.py:292
  792.7 8.8 %collective-permute-start.6 = (bf16[2,128,1152]{2,1,0:T(8,128)(2,1)S(1)}, bf16[2,128,1152]{2,1,0:T(8,128)(2,1)S(1)}, u32[]{:S(2)}, u32[]{:S(2)}) collective-permute-start(bf16[2,128,1152]{2,1,0:T(8,128)(2,1)S(1)} %broadcast_select_fusion), channel_id=1, source_target_pairs={{0,16},{16,0},{32,48},{48,32},{64,80},{80,64},{96,112},{112,96},{1... | collective-permute-start | bytes 1769480 | tf_op jit(solution)/shard_map/ppermute | solution.py:240
  (50 other events, 844.1 us)

commit v4 on v3

--- a/solution.py
+++ b/solution.py
@@ -143,65 +143,84 @@
     micro = step[0] - ids[0]
     inside = jnp.logical_and(micro >= 0, micro < per_core)
     clipped = jnp.clip(micro, 0, per_core - 1)
-    return ids[1] * per_core + clipped, jnp.where(inside, clipped, per_core)
-
-
-def spatial_part(x, factors, qkv, out, y, g):
+    return inside, ids[1] * per_core + clipped, clipped
+
+
+def spatial_part(x, factors, qkv, out, y, g, ready=None):
     normed = norm_modulate(x, factors[0:1], factors[1:2])
+    if ready is not None:
+        ready()
     mixed = attention(dot(normed, qkv[...]), out.shape[0], 0)
     middle = x + factors[2:3] * dot(mixed, out[...])
     y[...] = middle
     g[...] = norm_modulate(middle, factors[3:4], factors[4:5])
 
 
-def first_kernel(per_core, ids, frames, mod, qkv, out, y, g):
-    video = ids[1] * per_core
-    spatial_part(frames[video].astype(F32), mod[video], qkv, out, y, g)
-
-
-def head_kernel(per_core, ids, step, frames, arriving, mod, qkv, out, y, g, x_v, sem):
-    video, _ = place_of(ids, step, per_core)
-
-    @pl.when(ids[0] == 0)
+def head_kernel(
+    per_core, ids, step, frames, arriving, mod, qkv, out, y, g, x_v, qkv_v, out_v, sems
+):
+    inside, video, _ = place_of(ids, step, per_core)
+
+    @pl.when(inside)
     def _():
-        pltpu.make_async_copy(frames.at[video], x_v, sem).start()
-
-    @pl.when(ids[0] != 0)
+        @pl.when(ids[0] == 0)
+        def _():
+            pltpu.make_async_copy(frames.at[video], x_v, sems.at[0]).start()
+
+        @pl.when(ids[0] != 0)
+        def _():
+            pltpu.make_async_copy(arriving, x_v, sems.at[0]).start()
+
+        weights = (
+            pltpu.make_async_copy(qkv, qkv_v, sems.at[1]),
+            pltpu.make_async_copy(out, out_v, sems.at[2]),
+        )
+        for copy in weights:
+            copy.start()
+
+        def ready():
+            for copy in weights:
+                copy.wait()
+
+        pltpu.make_async_copy(arriving, x_v, sems.at[0]).wait()
+        spatial_part(x_v[...].astype(F32), mod[video], qkv_v, out_v, y, g, ready)
+
+
+def temporal_kernel(per_core, share, ids, step, arrived, qkv, mixed):
+    inside, _, _ = place_of(ids, step, per_core)
+
+    @pl.when(inside)
     def _():
-        pltpu.make_async_copy(arriving, x_v, sem).start()
-
-    pltpu.make_async_copy(arriving, x_v, sem).wait()
-    spatial_part(x_v[...].astype(F32), mod[video], qkv, out, y, g)
-
-
-def temporal_kernel(share, arrived, qkv, mixed):
-    mixed[...] = attention(dot(arrived[...], qkv[...]), mixed.shape[1], share)
+        mixed[...] = attention(dot(arrived[...], qkv[...]), mixed.shape[1], share)
 
 
 def joint_kernel(
     per_core, ids, step, returned, y_in, mod, following, tout, qkv, out, kept_in,
     y, g, kept, x_v, sem,
 ):
-    video, slot = place_of(ids, step, per_core)
-    leaving = (y_in[...] + mod[video][5:6] * dot(returned[...], tout[...])).astype(BF16)
-    x_v[...] = leaving
-    store = pltpu.make_async_copy(x_v, kept.at[slot], sem)
-    store.start()
-    spatial_part(leaving.astype(F32), following[video], qkv, out, y, g)
-    store.wait()
-
-
-def tail_kernel(
-    per_core, ids, step, returned, y_in, mod, tout, kept_in, x, kept, following, x_v, sem
-):
-    following[0] = step[0] + 1
-    video, slot = place_of(ids, step, per_core)
-    leaving = (y_in[...] + mod[video][5:6] * dot(returned[...], tout[...])).astype(BF16)
-    x_v[...] = leaving
-    store = pltpu.make_async_copy(x_v, kept.at[slot], sem)
-    store.start()
-    x[...] = leaving
-    store.wait()
+    inside, video, slot = place_of(ids, step, per_core)
+
+    @pl.when(inside)
+    def _():
+        leaving = (y_in[...] + mod[video][5:6] * dot(returned[...], tout[...])).astype(BF16)
+        x_v[...] = leaving
+        store = pltpu.make_async_copy(x_v, kept.at[slot], sem)
+        store.start()
+        spatial_part(leaving.astype(F32), following[video], qkv, out, y, g)
+        store.wait()
+
+
+def tail_kernel(per_core, ids, step, returned, y_in, mod, tout, kept_in, x, kept, x_v, sem):
+    inside, video, slot = place_of(ids, step, per_core)
+
+    @pl.when(inside)
+    def _():
+        leaving = (y_in[...] + mod[video][5:6] * dot(returned[...], tout[...])).astype(BF16)
+        x_v[...] = leaving
+        store = pltpu.make_async_copy(x_v, kept.at[slot], sem)
+        store.start()
+        x[...] = leaving
+        store.wait()
 
 
 SMEM = pl.BlockSpec(memory_space=pltpu.SMEM)
@@ -210,7 +229,7 @@
 HBM = pl.BlockSpec(memory_space=pltpu.HBM)
 
 
-def call(kernel, name, ins, outs, specs, scratch, aliases={}, limit=24):
+def call(kernel, name, ins, outs, specs, scratch, aliases={}, limit=14):
     return pl.pallas_call(
         kernel,
         name=name,
@@ -242,7 +261,8 @@
     shape = jax.ShapeDtypeStruct
     qkv_s, out_s = shape((model, columns), BF16), shape((hw, model), BF16)
     prepare = call(
-        prepare_kernel, "prepare", [SMEM] + [HBM] * 4, [qkv_s] * 2 + [out_s] * 2, [ANY] * 4,
+        prepare_kernel, "prepare", [SMEM] + [HBM] * 4, [qkv_s] * 2 + [out_s] * 2,
+        [ANY] * 2 + [VMEM] * 2,
         [pltpu.VMEM((columns, model), BF16)] * 2 + [pltpu.VMEM((model, columns), BF16)] * 2
         + [pltpu.SemaphoreType.DMA((2, 6))],
         limit=60,
@@ -250,33 +270,36 @@
     chain = (stage + core) % 2
     core_id = core.reshape(1).astype(jnp.int32)
     ids = jnp.stack([stage, chain]).astype(jnp.int32)
-    mod = modulation[0]
-    mod2 = swapped(mod)
-    mod_e, mod_o = jnp.where(core == 0, mod, mod2), jnp.where(core == 0, mod2, mod)
-
-    def prepared(qkv, out, core_id):
-        qkv2, out2 = swapped(qkv), swapped(out)
+    def prepared(qkv, out, qkv2, out2):
         return prepare(
             core_id, jnp.swapaxes(qkv[0], 0, 1), jnp.swapaxes(qkv2[0], 0, 1), out[0], out2[0]
         )
 
-    sqkv_e, sqkv_o, sout_e, sout_o = prepared(spatial_qkv, spatial_out, core_id)
+    mod = modulation[0]
+    mod2, sqkv2, sout2 = swapped(mod), swapped(spatial_qkv), swapped(spatial_out)
+    tqkv, tout, mod2, sqkv2, sout2 = lax.optimization_barrier(
+        (temporal_qkv, temporal_out, mod2, sqkv2, sout2)
+    )
+    mod_e, mod_o = jnp.where(core == 0, mod, mod2), jnp.where(core == 0, mod2, mod)
+    tqkv2, tout2 = swapped(tqkv), swapped(tout)
+    sqkv_e, sqkv_o, sout_e, sout_o = prepared(spatial_qkv, spatial_out, sqkv2, sout2)
+    tqkv_e, tqkv_o, tout_e, tout_o = prepared(tqkv, tout, tqkv2, tout2)
     source = frames_in.reshape(videos, tokens, model)
 
     x_s, y_s = shape((tokens, model), BF16), shape((tokens, model), F32)
-    kept_s = shape((per_core + 1, tokens, model), BF16)
+    kept_s = shape((per_core, tokens, model), BF16)
     hold = [pltpu.VMEM((tokens, model), BF16), pltpu.SemaphoreType.DMA]
-    first = call(
-        functools.partial(first_kernel, per_core), "first", [SMEM] + [VMEM] * 4,
-        [y_s, x_s], [VMEM, VMEM], [],
-    )
     head = call(
         functools.partial(head_kernel, per_core), "head",
-        [SMEM, SMEM, ANY, ANY, VMEM, VMEM, VMEM], [y_s, x_s], [VMEM, VMEM], hold,
+        [SMEM, SMEM, ANY, ANY, VMEM, ANY, ANY], [y_s, x_s], [VMEM, VMEM],
+        [
+            pltpu.VMEM((tokens, model), BF16), pltpu.VMEM((model, columns), BF16),
+            pltpu.VMEM((hw, model), BF16), pltpu.SemaphoreType.DMA((3,)),
+        ],
     )
     temporal = call(
-        functools.partial(temporal_kernel, share), "temporal", [VMEM, VMEM],
-        shape((tokens, hw), BF16), VMEM, [],
+        functools.partial(temporal_kernel, per_core, share), "temporal",
+        [SMEM, SMEM, VMEM, VMEM], shape((tokens, hw), BF16), VMEM, [],
     )
     joint = call(
         functools.partial(joint_kernel, per_core), "joint",
@@ -284,41 +307,33 @@
     )
     tail = call(
         functools.partial(tail_kernel, per_core), "tail",
-        [SMEM, SMEM] + [VMEM] * 4 + [ANY], [x_s, kept_s, shape((1,), jnp.int32)],
-        [VMEM, ANY, SMEM], hold, {6: 1},
+        [SMEM, SMEM] + [VMEM] * 4 + [ANY], [x_s, kept_s], [VMEM, ANY], hold, {6: 1},
     )
 
     def exchange(a):
         out = lax.all_to_all(a.reshape(ranks, share, a.shape[1]), "seq", 0, 0, tiled=True)
         return out.reshape(a.shape)
 
-    kept = jnp.zeros(kept_s.shape, BF16)
-    y, g = first(ids, source, mod_e, sqkv_e, sout_e)
-    g, core_id = lax.optimization_barrier((g, core_id))
-    tqkv_e, tqkv_o, tout_e, tout_o = prepared(temporal_qkv, temporal_out, core_id)
-
-    def middle(at, even, y, g):
-        mixed = temporal(exchange(g), tqkv_e)
+    def section_pair(at, even, odd, arriving):
+        y, g = head(ids, at, source, arriving, mod_e, sqkv_e, sout_e)
+        mixed = temporal(ids, at, exchange(g), tqkv_e)
         y, g, even = joint(
             ids, at, exchange(mixed), y, mod_e, mod_o, tout_e, sqkv_o, sout_o, even
         )
-        return even, y, exchange(temporal(exchange(g), tqkv_o))
+        mixed = temporal(ids, at, exchange(g), tqkv_o)
+        x, odd = tail(ids, at, exchange(mixed), y, mod_o, tout_o, odd)
+        return even, odd, x
+
+    onward = [(i, (i + 2) ^ 1) for i in range(sections - 2)]
 
     def advance(step, carried):
-        odd, even, y, returned = carried
-        x, odd, at = tail(ids, step.reshape(1), returned, y, mod_o, tout_o, odd)
-        onward = [(i, (i + 2) ^ 1) for i in range(sections - 2)]
-        arriving = lax.ppermute(x, "section", onward)
-        y, g = head(ids, at, source, arriving, mod_e, sqkv_e, sout_e)
-        return odd, *middle(at, even, y, g)
-
+        even, odd, x = section_pair(step.reshape(1), *carried)
+        return even, odd, lax.ppermute(x, "section", onward)
+
+    kept = jnp.zeros(kept_s.shape, BF16)
     last = stages + per_core - 2
-    carried = kept, *middle(jnp.zeros((1,), jnp.int32), kept, y, g)
-    odd, even, y, returned = lax.fori_loop(0, last, advance, carried)
-    _, odd, _ = tail(
-        ids, jnp.full((1,), last, jnp.int32), returned, y, mod_o, tout_o, odd
-    )
-    even, odd = even[:per_core], odd[:per_core]
+    carried = lax.fori_loop(0, last, advance, (kept, kept, jnp.zeros((tokens, model), BF16)))
+    even, odd, _ = section_pair(jnp.full((1,), last, jnp.int32), *carried)
     own = jnp.where(core == 0, even, odd)
     other = swapped(jnp.where(core == 0, odd, even))
     low, high = jnp.where(chain == 0, own, other), jnp.where(chain == 0, other, own)

time: 805 us -> 656 us (0.81)
  Pallas kernels: 273 us -> 76.4 us
  blocking collectives: 280 us -> 386 us
  starting transfers between devices: 57.8 us -> 14 us
  waiting for transfers between devices: 187 us -> 165 us
    pallas_call x2, Pallas kernels: 123 us -> 15.6 us  [prepared(): prepare(core_id, jnp.swapaxes(qkv[0], 0, 1), jnp.swapaxes(qkv2[0], 0, 1),...]
    all_to_all x26 -> x36, blocking collectives: 280 us -> 386 us  [exchange(): lax.all_to_all(a.reshape(ranks, share, a.shape[1]), 'seq', 0, 0, tiled=True)]
    pallas_call x45, Pallas kernels: 150 us -> 60.8 us  [the longest x9 19.7 us: section_pair(): y, g = head(ids, at, source, arriving, mod_e, sqkv_e, sout_e)]
    all_to_all x10 -> x0, waiting for transfers between devices: 60.8 us -> none  [exchange(): lax.all_to_all(a.reshape(ranks, share, a.shape[1]), 'seq', 0, 0, tiled=True)]
    ppermute x8, waiting for transfers between devices: 110 us -> 156 us  [advance(): return (even, odd, lax.ppermute(x, 'section', onward))]
    all_to_all x10 -> x0, starting transfers between devices: 38.5 us -> none  [exchange(): lax.all_to_all(a.reshape(ranks, share, a.shape[1]), 'seq', 0, 0, tiled=True)]
  transfers between devices with their start and end apart: 24 -> 14, of which waited for: 19 -> 10; matrix products, arithmetic and copies ran while one was open for 0% -> 0% of each run, Pallas kernels for 16% -> 1%
where the time goes in v4:
time: 656 us; the launch traced here: 654 us
  blocking collectives  386 us (59%)
  waiting for transfers between devices  165 us (25%)
  Pallas kernels  76.4 us (12%)
  starting transfers between devices  14 us (2%)
  local copies, waits for them, and re-layouts  9.63 us (1%)
    all_to_all x36, blocking collectives, exchange(): lax.all_to_all(a.reshape(ranks, share, a.shape[1]), 'seq', 0, 0, tiled=True)  386 us
    ppermute x8, waiting for transfers between devices, advance(): return (even, odd, lax.ppermute(x, 'section', onward))  156 us
    pallas_call x9, Pallas kernels, section_pair(): y, g = head(ids, at, source, arriving, mod_e, sqkv_e, sout_e)  19.7 us
    pallas_call x9, Pallas kernels, section_pair(): joint(ids, at, exchange(mixed), y, mod_e, mod_o, tout_e, sqkv_o, sout_o,...  15.7 us
    pallas_call x2, Pallas kernels, prepared(): prepare(core_id, jnp.swapaxes(qkv[0], 0, 1), jnp.swapaxes(qkv2[0], 0, 1),...  15.6 us
  transfers between devices with their start and end apart: 14, of which 10 were waited for; matrix products, arithmetic and copies ran while one was open for 0% of the time, Pallas kernels for 1%

profile of v4, /device:TPU:225, one launch (start us, length us, event | category | flops | bytes accessed | tf_op | source)
XLA Modules:
  0.0 654.5 jit_solution(9035784468133592481)
XLA Ops:
  28.7 562.8 %while.17 = (s32[]{:T(128)}, bf16[2,128,1152]{2,1,0:T(8,128)(2,1)S(1)}, bf16[2,128,1152]{2,1,0:T(8,128)(2,1)}, bf16[128,1152]{1,0:T(8,128)(2,1)}, s32[2]{0:T(128...) while((s32[]{:T(128)}, ...), condition=%wide.region_1.2_spmd, body=%wide.region_0.1_spmd.sunk | while | flops 2 | bytes 62521708 | solution.py:335
  29.8 14.4 %all_to_all.64 = bf16[16,8,1152]{2,1,0:T(8,128)(2,1)S(1)} all-to-all(bf16[16,8,1152]{2,1,0:T(8,128)(2,1)S(1)} %bitcast.73), channel_id=1, replica_groups=mesh['section'=16,'seq'=16] {'seq'}, dimensions={0} | all-to-all | bytes 589824 | tf_op jit(solution)/shard_map/while/body/eval_jaxpr/all_to_all | solution.py:314
  44.8 10.7 %all_to_all.65 = bf16[16,8,576]{2,1,0:T(8,128)(2,1)S(1)} all-to-all(bf16[16,8,576]{2,1,0:T(8,128)(2,1)S(1)} %bitcast.69), channel_id=1, replica_groups=mesh['section'=16,'seq'=16] {'seq'}, dimensions={0} | all-to-all | bytes 294912 | tf_op jit(solution)/shard_map/while/body/eval_jaxpr/all_to_all | solution.py:314
  56.7 11.1 %all_to_all.66 = bf16[16,8,1152]{2,1,0:T(8,128)(2,1)S(1)} all-to-all(bf16[16,8,1152]{2,1,0:T(8,128)(2,1)S(1)} %bitcast.72), channel_id=1, replica_groups=mesh['section'=16,'seq'=16] {'seq'}, dimensions={0} | all-to-all | bytes 589824 | tf_op jit(solution)/shard_map/while/body/eval_jaxpr/all_to_all | solution.py:314
  81.7 14.0 %collective-permute-done = bf16[128,1152]{1,0:T(8,128)(2,1)} collective-permute-done((bf16[128,1152]{1,0:T(8,128)(2,1)S(1)}, bf16[128,1152]{1,0:T(8,128)(2,1)}, u32[]{:S(2)}, u32[]{:S(2)}) %collective-permute-start) | collective-permute-done | bytes 294944 | tf_op jit(solution)/shard_map/while/body/eval_jaxpr/ppermute | solution.py:331
  96.8 10.8 %all_to_all.64 = bf16[16,8,1152]{2,1,0:T(8,128)(2,1)S(1)} all-to-all(bf16[16,8,1152]{2,1,0:T(8,128)(2,1)S(1)} %bitcast.73), channel_id=1, replica_groups=mesh['section'=16,'seq'=16] {'seq'}, dimensions={0} | all-to-all | bytes 589824 | tf_op jit(solution)/shard_map/while/body/eval_jaxpr/all_to_all | solution.py:314
  108.2 10.5 %all_to_all.65 = bf16[16,8,576]{2,1,0:T(8,128)(2,1)S(1)} all-to-all(bf16[16,8,576]{2,1,0:T(8,128)(2,1)S(1)} %bitcast.69), channel_id=1, replica_groups=mesh['section'=16,'seq'=16] {'seq'}, dimensions={0} | all-to-all | bytes 294912 | tf_op jit(solution)/shard_map/while/body/eval_jaxpr/all_to_all | solution.py:314
  119.9 11.0 %all_to_all.66 = bf16[16,8,1152]{2,1,0:T(8,128)(2,1)S(1)} all-to-all(bf16[16,8,1152]{2,1,0:T(8,128)(2,1)S(1)} %bitcast.72), channel_id=1, replica_groups=mesh['section'=16,'seq'=16] {'seq'}, dimensions={0} | all-to-all | bytes 589824 | tf_op jit(solution)/shard_map/while/body/eval_jaxpr/all_to_all | solution.py:314
  144.6 14.7 %collective-permute-done = bf16[128,1152]{1,0:T(8,128)(2,1)} collective-permute-done((bf16[128,1152]{1,0:T(8,128)(2,1)S(1)}, bf16[128,1152]{1,0:T(8,128)(2,1)}, u32[]{:S(2)}, u32[]{:S(2)}) %collective-permute-start) | collective-permute-done | bytes 294944 | tf_op jit(solution)/shard_map/while/body/eval_jaxpr/ppermute | solution.py:331
  160.4 10.8 %all_to_all.64 = bf16[16,8,1152]{2,1,0:T(8,128)(2,1)S(1)} all-to-all(bf16[16,8,1152]{2,1,0:T(8,128)(2,1)S(1)} %bitcast.73), channel_id=1, replica_groups=mesh['section'=16,'seq'=16] {'seq'}, dimensions={0} | all-to-all | bytes 589824 | tf_op jit(solution)/shard_map/while/body/eval_jaxpr/all_to_all | solution.py:314
  171.8 10.5 %all_to_all.65 = bf16[16,8,576]{2,1,0:T(8,128)(2,1)S(1)} all-to-all(bf16[16,8,576]{2,1,0:T(8,128)(2,1)S(1)} %bitcast.69), channel_id=1, replica_groups=mesh['section'=16,'seq'=16] {'seq'}, dimensions={0} | all-to-all | bytes 294912 | tf_op jit(solution)/shard_map/while/body/eval_jaxpr/all_to_all | solution.py:314
  183.6 11.0 %all_to_all.66 = bf16[16,8,1152]{2,1,0:T(8,128)(2,1)S(1)} all-to-all(bf16[16,8,1152]{2,1,0:T(8,128)(2,1)S(1)} %bitcast.72), channel_id=1, replica_groups=mesh['section'=16,'seq'=16] {'seq'}, dimensions={0} | all-to-all | bytes 589824 | tf_op jit(solution)/shard_map/while/body/eval_jaxpr/all_to_all | solution.py:314
  208.3 14.7 %collective-permute-done = bf16[128,1152]{1,0:T(8,128)(2,1)} collective-permute-done((bf16[128,1152]{1,0:T(8,128)(2,1)S(1)}, bf16[128,1152]{1,0:T(8,128)(2,1)}, u32[]{:S(2)}, u32[]{:S(2)}) %collective-permute-start) | collective-permute-done | bytes 294944 | tf_op jit(solution)/shard_map/while/body/eval_jaxpr/ppermute | solution.py:331
  224.1 10.8 %all_to_all.64 = bf16[16,8,1152]{2,1,0:T(8,128)(2,1)S(1)} all-to-all(bf16[16,8,1152]{2,1,0:T(8,128)(2,1)S(1)} %bitcast.73), channel_id=1, replica_groups=mesh['section'=16,'seq'=16] {'seq'}, dimensions={0} | all-to-all | bytes 589824 | tf_op jit(solution)/shard_map/while/body/eval_jaxpr/all_to_all | solution.py:314
  235.5 10.5 %all_to_all.65 = bf16[16,8,576]{2,1,0:T(8,128)(2,1)S(1)} all-to-all(bf16[16,8,576]{2,1,0:T(8,128)(2,1)S(1)} %bitcast.69), channel_id=1, replica_groups=mesh['section'=16,'seq'=16] {'seq'}, dimensions={0} | all-to-all | bytes 294912 | tf_op jit(solution)/shard_map/while/body/eval_jaxpr/all_to_all | solution.py:314
  247.2 11.0 %all_to_all.66 = bf16[16,8,1152]{2,1,0:T(8,128)(2,1)S(1)} all-to-all(bf16[16,8,1152]{2,1,0:T(8,128)(2,1)S(1)} %bitcast.72), channel_id=1, replica_groups=mesh['section'=16,'seq'=16] {'seq'}, dimensions={0} | all-to-all | bytes 589824 | tf_op jit(solution)/shard_map/while/body/eval_jaxpr/all_to_all | solution.py:314
  271.9 12.8 %collective-permute-done = bf16[128,1152]{1,0:T(8,128)(2,1)} collective-permute-done((bf16[128,1152]{1,0:T(8,128)(2,1)S(1)}, bf16[128,1152]{1,0:T(8,128)(2,1)}, u32[]{:S(2)}, u32[]{:S(2)}) %collective-permute-start) | collective-permute-done | bytes 294944 | tf_op jit(solution)/shard_map/while/body/eval_jaxpr/ppermute | solution.py:331
  285.9 10.8 %all_to_all.64 = bf16[16,8,1152]{2,1,0:T(8,128)(2,1)S(1)} all-to-all(bf16[16,8,1152]{2,1,0:T(8,128)(2,1)S(1)} %bitcast.73), channel_id=1, replica_groups=mesh['section'=16,'seq'=16] {'seq'}, dimensions={0} | all-to-all | bytes 589824 | tf_op jit(solution)/shard_map/while/body/eval_jaxpr/all_to_all | solution.py:314
  308.8 10.8 %all_to_all.66 = bf16[16,8,1152]{2,1,0:T(8,128)(2,1)S(1)} all-to-all(bf16[16,8,1152]{2,1,0:T(8,128)(2,1)S(1)} %bitcast.72), channel_id=1, replica_groups=mesh['section'=16,'seq'=16] {'seq'}, dimensions={0} | all-to-all | bytes 589824 | tf_op jit(solution)/shard_map/while/body/eval_jaxpr/all_to_all | solution.py:314
  333.4 14.1 %collective-permute-done = bf16[128,1152]{1,0:T(8,128)(2,1)} collective-permute-done((bf16[128,1152]{1,0:T(8,128)(2,1)S(1)}, bf16[128,1152]{1,0:T(8,128)(2,1)}, u32[]{:S(2)}, u32[]{:S(2)}) %collective-permute-start) | collective-permute-done | bytes 294944 | tf_op jit(solution)/shard_map/while/body/eval_jaxpr/ppermute | solution.py:331
  348.6 10.8 %all_to_all.64 = bf16[16,8,1152]{2,1,0:T(8,128)(2,1)S(1)} all-to-all(bf16[16,8,1152]{2,1,0:T(8,128)(2,1)S(1)} %bitcast.73), channel_id=1, replica_groups=mesh['section'=16,'seq'=16] {'seq'}, dimensions={0} | all-to-all | bytes 589824 | tf_op jit(solution)/shard_map/while/body/eval_jaxpr/all_to_all | solution.py:314
  360.0 10.4 %all_to_all.65 = bf16[16,8,576]{2,1,0:T(8,128)(2,1)S(1)} all-to-all(bf16[16,8,576]{2,1,0:T(8,128)(2,1)S(1)} %bitcast.69), channel_id=1, replica_groups=mesh['section'=16,'seq'=16] {'seq'}, dimensions={0} | all-to-all | bytes 294912 | tf_op jit(solution)/shard_map/while/body/eval_jaxpr/all_to_all | solution.py:314
  371.6 10.8 %all_to_all.66 = bf16[16,8,1152]{2,1,0:T(8,128)(2,1)S(1)} all-to-all(bf16[16,8,1152]{2,1,0:T(8,128)(2,1)S(1)} %bitcast.72), channel_id=1, replica_groups=mesh['section'=16,'seq'=16] {'seq'}, dimensions={0} | all-to-all | bytes 589824 | tf_op jit(solution)/shard_map/while/body/eval_jaxpr/all_to_all | solution.py:314
  396.2 14.1 %collective-permute-done = bf16[128,1152]{1,0:T(8,128)(2,1)} collective-permute-done((bf16[128,1152]{1,0:T(8,128)(2,1)S(1)}, bf16[128,1152]{1,0:T(8,128)(2,1)}, u32[]{:S(2)}, u32[]{:S(2)}) %collective-permute-start) | collective-permute-done | bytes 294944 | tf_op jit(solution)/shard_map/while/body/eval_jaxpr/ppermute | solution.py:331
  411.4 10.8 %all_to_all.64 = bf16[16,8,1152]{2,1,0:T(8,128)(2,1)S(1)} all-to-all(bf16[16,8,1152]{2,1,0:T(8,128)(2,1)S(1)} %bitcast.73), channel_id=1, replica_groups=mesh['section'=16,'seq'=16] {'seq'}, dimensions={0} | all-to-all | bytes 589824 | tf_op jit(solution)/shard_map/while/body/eval_jaxpr/all_to_all | solution.py:314
  434.3 10.8 %all_to_all.66 = bf16[16,8,1152]{2,1,0:T(8,128)(2,1)S(1)} all-to-all(bf16[16,8,1152]{2,1,0:T(8,128)(2,1)S(1)} %bitcast.72), channel_id=1, replica_groups=mesh['section'=16,'seq'=16] {'seq'}, dimensions={0} | all-to-all | bytes 589824 | tf_op jit(solution)/shard_map/while/body/eval_jaxpr/all_to_all | solution.py:314
  458.9 57.4 %collective-permute-done = bf16[128,1152]{1,0:T(8,128)(2,1)} collective-permute-done((bf16[128,1152]{1,0:T(8,128)(2,1)S(1)}, bf16[128,1152]{1,0:T(8,128)(2,1)}, u32[]{:S(2)}, u32[]{:S(2)}) %collective-permute-start) | collective-permute-done | bytes 294944 | tf_op jit(solution)/shard_map/while/body/eval_jaxpr/ppermute | solution.py:331
  522.3 10.7 %all_to_all.64 = bf16[16,8,1152]{2,1,0:T(8,128)(2,1)S(1)} all-to-all(bf16[16,8,1152]{2,1,0:T(8,128)(2,1)S(1)} %bitcast.73), channel_id=1, replica_groups=mesh['section'=16,'seq'=16] {'seq'}, dimensions={0} | all-to-all | bytes 589824 | tf_op jit(solution)/shard_map/while/body/eval_jaxpr/all_to_all | solution.py:314
  548.8 12.7 %all_to_all.66 = bf16[16,8,1152]{2,1,0:T(8,128)(2,1)S(1)} all-to-all(bf16[16,8,1152]{2,1,0:T(8,128)(2,1)S(1)} %bitcast.72), channel_id=1, replica_groups=mesh['section'=16,'seq'=16] {'seq'}, dimensions={0} | all-to-all | bytes 589824 | tf_op jit(solution)/shard_map/while/body/eval_jaxpr/all_to_all | solution.py:314
  576.8 14.6 %collective-permute-done = bf16[128,1152]{1,0:T(8,128)(2,1)} collective-permute-done((bf16[128,1152]{1,0:T(8,128)(2,1)S(1)}, bf16[128,1152]{1,0:T(8,128)(2,1)}, u32[]{:S(2)}, u32[]{:S(2)}) %collective-permute-start) | collective-permute-done | bytes 294944 | tf_op jit(solution)/shard_map/while/body/eval_jaxpr/ppermute | solution.py:331
  597.4 10.7 %all_to_all.60 = bf16[16,8,1152]{2,1,0:T(8,128)(2,1)S(1)} all-to-all(bf16[16,8,1152]{2,1,0:T(8,128)(2,1)S(1)} %bitcast.81), channel_id=1, replica_groups=mesh['section'=16,'seq'=16] {'seq'}, dimensions={0} | all-to-all | bytes 589824 | tf_op jit(solution)/shard_map/all_to_all | solution.py:314
  623.8 11.7 %all_to_all.62 = bf16[16,8,1152]{2,1,0:T(8,128)(2,1)S(1)} all-to-all(bf16[16,8,1152]{2,1,0:T(8,128)(2,1)S(1)} %bitcast.80), channel_id=1, replica_groups=mesh['section'=16,'seq'=16] {'seq'}, dimensions={0} | all-to-all | bytes 589824 | tf_op jit(solution)/shard_map/all_to_all | solution.py:314
  (199 shorter events, 242.6 us)
Async XLA Ops:
  0.0 9.5 %collective-permute-start.2 = (bf16[1,1152,1728]{1,2,0:T(8,128)(2,1)}, bf16[1,1152,1728]{1,2,0:T(8,128)(2,1)}, u32[]{:S(2)}, u32[]{:S(2)}) collective-permute-start(bf16[1,1152,1728]{1,2,0:T(8,128)(2,1)} %param.9), channel_id=1, source_target_pairs={{0,16},{16,0},{32,48},{48,32},{64,80},{80,64},{96,112},{112,96},{1... | collective-permute-start | bytes 11943944 | tf_op jit(solution)/shard_map/ppermute | solution.py:259
  0.7 8.8 %collective-permute-start.3 = (bf16[1,576,1152]{2,1,0:T(8,128)(2,1)}, bf16[1,576,1152]{2,1,0:T(8,128)(2,1)S(1)}, u32[]{:S(2)}, u32[]{:S(2)}) collective-permute-start(bf16[1,576,1152]{2,1,0:T(8,128)(2,1)} %param.10), channel_id=1, source_target_pairs={{0,16},{16,0},{32,48},{48,32},{64,80},{80,64},{96,112},{112,96},{1... | collective-permute-start | bytes 3981320 | tf_op jit(solution)/shard_map/ppermute | solution.py:259
  1.6 7.9 %collective-permute-start.1 = (f32[4,6,1152]{2,1,0:T(8,128)S(1)}, f32[4,6,1152]{2,1,0:T(8,128)S(1)}, u32[]{:S(2)}, u32[]{:S(2)}) collective-permute-start(f32[4,6,1152]{2,1,0:T(8,128)S(1)} %bitcast.88), channel_id=1, source_target_pairs={{0,16},{16,0},{32,48},{48,32},{64,80},{80,64},{96,112},{112,96},{1... | collective-permute-start | bytes 331784 | tf_op jit(solution)/shard_map/ppermute | solution.py:259
  9.5 9.7 %collective-permute-start.4 = (bf16[1,1152,1728]{1,2,0:T(8,128)(2,1)}, bf16[1,1152,1728]{1,2,0:T(8,128)(2,1)}, u32[]{:S(2)}, u32[]{:S(2)}) collective-permute-start(bf16[1,1152,1728]{1,2,0:T(8,128)(2,1)} %param.11), channel_id=1, source_target_pairs={{0,16},{16,0},{32,48},{48,32},{64,80},{80,64},{96,112},{112,96},{1... | collective-permute-start | bytes 11943944 | tf_op jit(solution)/shard_map/ppermute | solution.py:259
  9.9 9.3 %collective-permute-start.5 = (bf16[1,576,1152]{2,1,0:T(8,128)(2,1)}, bf16[1,576,1152]{2,1,0:T(8,128)(2,1)}, u32[]{:S(2)}, u32[]{:S(2)}) collective-permute-start(bf16[1,576,1152]{2,1,0:T(8,128)(2,1)} %param.12), channel_id=1, source_target_pairs={{0,16},{16,0},{32,48},{48,32},{64,80},{80,64},{96,112},{112,96},{1... | collective-permute-start | bytes 3981320 | tf_op jit(solution)/shard_map/ppermute | solution.py:259
  28.7 15.5 %copy-start.2 = (bf16[1152,1792]{1,0:T(8,128)(2,1)S(1)}, bf16[1152,1792]{1,0:T(8,128)(2,1)}, u32[]{:S(2)}) copy-start(bf16[1152,1792]{1,0:T(8,128)(2,1)} %get-tuple-element.475.qkv) | copy-start | bytes 12386308 | tf_op jit(solution)/shard_map/while
  55.5 12.3 %copy-start = (bf16[1152,1792]{1,0:T(8,128)(2,1)S(1)}, bf16[1152,1792]{1,0:T(8,128)(2,1)}, u32[]{:S(2)}) copy-start(bf16[1152,1792]{1,0:T(8,128)(2,1)} %get-tuple-element.480.qkv) | copy-start | bytes 12386308 | tf_op jit(solution)/shard_map/while
  80.4 15.2 %collective-permute-start = (bf16[128,1152]{1,0:T(8,128)(2,1)S(1)}, bf16[128,1152]{1,0:T(8,128)(2,1)}, u32[]{:S(2)}, u32[]{:S(2)}) collective-permute-start(bf16[128,1152]{1,0:T(8,128)(2,1)S(1)} %get-tuple-element.431), channel_id=1, source_target_pairs={{0,48},{16,32},{32,80},{48,64},{64,112},{80,96},{96,144},{112,128}... | collective-permute-start | bytes 884744 | tf_op jit(solution)/shard_map/while/body/eval_jaxpr/ppermute | solution.py:331
  95.7 12.0 %copy-start.2 = (bf16[1152,1792]{1,0:T(8,128)(2,1)S(1)}, bf16[1152,1792]{1,0:T(8,128)(2,1)}, u32[]{:S(2)}) copy-start(bf16[1152,1792]{1,0:T(8,128)(2,1)} %get-tuple-element.475.qkv) | copy-start | bytes 12386308 | tf_op jit(solution)/shard_map/while
  118.7 12.2 %copy-start = (bf16[1152,1792]{1,0:T(8,128)(2,1)S(1)}, bf16[1152,1792]{1,0:T(8,128)(2,1)}, u32[]{:S(2)}) copy-start(bf16[1152,1792]{1,0:T(8,128)(2,1)} %get-tuple-element.480.qkv) | copy-start | bytes 12386308 | tf_op jit(solution)/shard_map/while
  143.3 16.0 %collective-permute-start = (bf16[128,1152]{1,0:T(8,128)(2,1)S(1)}, bf16[128,1152]{1,0:T(8,128)(2,1)}, u32[]{:S(2)}, u32[]{:S(2)}) collective-permute-start(bf16[128,1152]{1,0:T(8,128)(2,1)S(1)} %get-tuple-element.431), channel_id=1, source_target_pairs={{0,48},{16,32},{32,80},{48,64},{64,112},{80,96},{96,144},{112,128}... | collective-permute-start | bytes 884744 | tf_op jit(solution)/shard_map/while/body/eval_jaxpr/ppermute | solution.py:331
  159.3 12.0 %copy-start.2 = (bf16[1152,1792]{1,0:T(8,128)(2,1)S(1)}, bf16[1152,1792]{1,0:T(8,128)(2,1)}, u32[]{:S(2)}) copy-start(bf16[1152,1792]{1,0:T(8,128)(2,1)} %get-tuple-element.475.qkv) | copy-start | bytes 12386308 | tf_op jit(solution)/shard_map/while
  182.4 12.2 %copy-start = (bf16[1152,1792]{1,0:T(8,128)(2,1)S(1)}, bf16[1152,1792]{1,0:T(8,128)(2,1)}, u32[]{:S(2)}) copy-start(bf16[1152,1792]{1,0:T(8,128)(2,1)} %get-tuple-element.480.qkv) | copy-start | bytes 12386308 | tf_op jit(solution)/shard_map/while
  207.0 16.0 %collective-permute-start = (bf16[128,1152]{1,0:T(8,128)(2,1)S(1)}, bf16[128,1152]{1,0:T(8,128)(2,1)}, u32[]{:S(2)}, u32[]{:S(2)}) collective-permute-start(bf16[128,1152]{1,0:T(8,128)(2,1)S(1)} %get-tuple-element.431), channel_id=1, source_target_pairs={{0,48},{16,32},{32,80},{48,64},{64,112},{80,96},{96,144},{112,128}... | collective-permute-start | bytes 884744 | tf_op jit(solution)/shard_map/while/body/eval_jaxpr/ppermute | solution.py:331
  223.0 12.0 %copy-start.2 = (bf16[1152,1792]{1,0:T(8,128)(2,1)S(1)}, bf16[1152,1792]{1,0:T(8,128)(2,1)}, u32[]{:S(2)}) copy-start(bf16[1152,1792]{1,0:T(8,128)(2,1)} %get-tuple-element.475.qkv) | copy-start | bytes 12386308 | tf_op jit(solution)/shard_map/while
  246.0 12.2 %copy-start = (bf16[1152,1792]{1,0:T(8,128)(2,1)S(1)}, bf16[1152,1792]{1,0:T(8,128)(2,1)}, u32[]{:S(2)}) copy-start(bf16[1152,1792]{1,0:T(8,128)(2,1)} %get-tuple-element.480.qkv) | copy-start | bytes 12386308 | tf_op jit(solution)/shard_map/while
  270.6 14.1 %collective-permute-start = (bf16[128,1152]{1,0:T(8,128)(2,1)S(1)}, bf16[128,1152]{1,0:T(8,128)(2,1)}, u32[]{:S(2)}, u32[]{:S(2)}) collective-permute-start(bf16[128,1152]{1,0:T(8,128)(2,1)S(1)} %get-tuple-element.431), channel_id=1, source_target_pairs={{0,48},{16,32},{32,80},{48,64},{64,112},{80,96},{96,144},{112,128}... | collective-permute-start | bytes 884744 | tf_op jit(solution)/shard_map/while/body/eval_jaxpr/ppermute | solution.py:331
  284.7 12.0 %copy-start.2 = (bf16[1152,1792]{1,0:T(8,128)(2,1)S(1)}, bf16[1152,1792]{1,0:T(8,128)(2,1)}, u32[]{:S(2)}) copy-start(bf16[1152,1792]{1,0:T(8,128)(2,1)} %get-tuple-element.475.qkv) | copy-start | bytes 12386308 | tf_op jit(solution)/shard_map/while
  307.7 12.0 %copy-start = (bf16[1152,1792]{1,0:T(8,128)(2,1)S(1)}, bf16[1152,1792]{1,0:T(8,128)(2,1)}, u32[]{:S(2)}) copy-start(bf16[1152,1792]{1,0:T(8,128)(2,1)} %get-tuple-element.480.qkv) | copy-start | bytes 12386308 | tf_op jit(solution)/shard_map/while
  332.1 15.4 %collective-permute-start = (bf16[128,1152]{1,0:T(8,128)(2,1)S(1)}, bf16[128,1152]{1,0:T(8,128)(2,1)}, u32[]{:S(2)}, u32[]{:S(2)}) collective-permute-start(bf16[128,1152]{1,0:T(8,128)(2,1)S(1)} %get-tuple-element.431), channel_id=1, source_target_pairs={{0,48},{16,32},{32,80},{48,64},{64,112},{80,96},{96,144},{112,128}... | collective-permute-start | bytes 884744 | tf_op jit(solution)/shard_map/while/body/eval_jaxpr/ppermute | solution.py:331
  347.5 12.0 %copy-start.2 = (bf16[1152,1792]{1,0:T(8,128)(2,1)S(1)}, bf16[1152,1792]{1,0:T(8,128)(2,1)}, u32[]{:S(2)}) copy-start(bf16[1152,1792]{1,0:T(8,128)(2,1)} %get-tuple-element.475.qkv) | copy-start | bytes 12386308 | tf_op jit(solution)/shard_map/while
  370.4 12.0 %copy-start = (bf16[1152,1792]{1,0:T(8,128)(2,1)S(1)}, bf16[1152,1792]{1,0:T(8,128)(2,1)}, u32[]{:S(2)}) copy-start(bf16[1152,1792]{1,0:T(8,128)(2,1)} %get-tuple-element.480.qkv) | copy-start | bytes 12386308 | tf_op jit(solution)/shard_map/while
  394.9 15.4 %collective-permute-start = (bf16[128,1152]{1,0:T(8,128)(2,1)S(1)}, bf16[128,1152]{1,0:T(8,128)(2,1)}, u32[]{:S(2)}, u32[]{:S(2)}) collective-permute-start(bf16[128,1152]{1,0:T(8,128)(2,1)S(1)} %get-tuple-element.431), channel_id=1, source_target_pairs={{0,48},{16,32},{32,80},{48,64},{64,112},{80,96},{96,144},{112,128}... | collective-permute-start | bytes 884744 | tf_op jit(solution)/shard_map/while/body/eval_jaxpr/ppermute | solution.py:331
  410.3 12.0 %copy-start.2 = (bf16[1152,1792]{1,0:T(8,128)(2,1)S(1)}, bf16[1152,1792]{1,0:T(8,128)(2,1)}, u32[]{:S(2)}) copy-start(bf16[1152,1792]{1,0:T(8,128)(2,1)} %get-tuple-element.475.qkv) | copy-start | bytes 12386308 | tf_op jit(solution)/shard_map/while
  433.2 12.0 %copy-start = (bf16[1152,1792]{1,0:T(8,128)(2,1)S(1)}, bf16[1152,1792]{1,0:T(8,128)(2,1)}, u32[]{:S(2)}) copy-start(bf16[1152,1792]{1,0:T(8,128)(2,1)} %get-tuple-element.480.qkv) | copy-start | bytes 12386308 | tf_op jit(solution)/shard_map/while
  457.6 58.7 %collective-permute-start = (bf16[128,1152]{1,0:T(8,128)(2,1)S(1)}, bf16[128,1152]{1,0:T(8,128)(2,1)}, u32[]{:S(2)}, u32[]{:S(2)}) collective-permute-start(bf16[128,1152]{1,0:T(8,128)(2,1)S(1)} %get-tuple-element.431), channel_id=1, source_target_pairs={{0,48},{16,32},{32,80},{48,64},{64,112},{80,96},{96,144},{112,128}... | collective-permute-start | bytes 884744 | tf_op jit(solution)/shard_map/while/body/eval_jaxpr/ppermute | solution.py:331
  516.3 16.7 %copy-start.2 = (bf16[1152,1792]{1,0:T(8,128)(2,1)S(1)}, bf16[1152,1792]{1,0:T(8,128)(2,1)}, u32[]{:S(2)}) copy-start(bf16[1152,1792]{1,0:T(8,128)(2,1)} %get-tuple-element.475.qkv) | copy-start | bytes 12386308 | tf_op jit(solution)/shard_map/while
  545.0 16.6 %copy-start = (bf16[1152,1792]{1,0:T(8,128)(2,1)S(1)}, bf16[1152,1792]{1,0:T(8,128)(2,1)}, u32[]{:S(2)}) copy-start(bf16[1152,1792]{1,0:T(8,128)(2,1)} %get-tuple-element.480.qkv) | copy-start | bytes 12386308 | tf_op jit(solution)/shard_map/while
  575.5 15.9 %collective-permute-start = (bf16[128,1152]{1,0:T(8,128)(2,1)S(1)}, bf16[128,1152]{1,0:T(8,128)(2,1)}, u32[]{:S(2)}, u32[]{:S(2)}) collective-permute-start(bf16[128,1152]{1,0:T(8,128)(2,1)S(1)} %get-tuple-element.431), channel_id=1, source_target_pairs={{0,48},{16,32},{32,80},{48,64},{64,112},{80,96},{96,144},{112,128}... | collective-permute-start | bytes 884744 | tf_op jit(solution)/shard_map/while/body/eval_jaxpr/ppermute | solution.py:331
  591.4 16.7 %copy-start.3 = (bf16[1152,1792]{1,0:T(8,128)(2,1)S(1)}, bf16[1152,1792]{1,0:T(8,128)(2,1)}, u32[]{:S(2)}) copy-start(bf16[1152,1792]{1,0:T(8,128)(2,1)} %get-tuple-element.485) | copy-start | bytes 12386308
  620.0 15.5 %copy-start.1 = (bf16[1152,1792]{1,0:T(8,128)(2,1)S(1)}, bf16[1152,1792]{1,0:T(8,128)(2,1)}, u32[]{:S(2)}) copy-start(bf16[1152,1792]{1,0:T(8,128)(2,1)} %get-tuple-element.484) | copy-start | bytes 12386308
  649.7 3.5 collective-permute-start.6
  (37 other events, 313.7 us)

commit v5 on v4

--- a/solution.py
+++ b/solution.py
@@ -156,34 +156,48 @@
     g[...] = norm_modulate(middle, factors[3:4], factors[4:5])
 
 
-def head_kernel(
-    per_core, ids, step, frames, arriving, mod, qkv, out, y, g, x_v, qkv_v, out_v, sems
+def tick_kernel(step, g_in, now, following, g):
+    now[0] = step[0]
+    following[0] = step[0] + 1
+
+
+def first_kernel(per_core, ids, frames, mod, qkv, out, y, g):
+    video = ids[1] * per_core
+
+    @pl.when(ids[0] == 0)
+    def _():
+        spatial_part(frames[video].astype(F32), mod[video], qkv, out, y, g)
+
+
+def cross_kernel(
+    per_core, stages, ids, step, returned, y_in, mod_p, mod, tout_p, qkv, out, frames, kept_in,
+    y, g, kept, x_v, new_v, sems,
 ):
     inside, video, _ = place_of(ids, step, per_core)
+    micro = jnp.where(ids[0] == 0, step[0] - stages, step[0] - ids[0])
+    finishing = jnp.logical_and(micro >= 0, micro < per_core)
+    slot = jnp.clip(micro, 0, per_core - 1)
+
+    @pl.when(finishing)
+    def _():
+        factor = mod_p[ids[1] * per_core + slot][5:6]
+        x_v[...] = (y_in[...] + factor * dot(returned[...], tout_p[...])).astype(BF16)
+        pltpu.make_async_copy(x_v, kept.at[slot], sems.at[0]).start()
 
     @pl.when(inside)
     def _():
         @pl.when(ids[0] == 0)
         def _():
-            pltpu.make_async_copy(frames.at[video], x_v, sems.at[0]).start()
-
-        @pl.when(ids[0] != 0)
-        def _():
-            pltpu.make_async_copy(arriving, x_v, sems.at[0]).start()
-
-        weights = (
-            pltpu.make_async_copy(qkv, qkv_v, sems.at[1]),
-            pltpu.make_async_copy(out, out_v, sems.at[2]),
-        )
-        for copy in weights:
+            copy = pltpu.make_async_copy(frames.at[video], new_v, sems.at[1])
             copy.start()
-
-        def ready():
-            for copy in weights:
-                copy.wait()
-
-        pltpu.make_async_copy(arriving, x_v, sems.at[0]).wait()
-        spatial_part(x_v[...].astype(F32), mod[video], qkv_v, out_v, y, g, ready)
+            copy.wait()
+
+        x = jnp.where(ids[0] == 0, new_v[...], x_v[...])
+        spatial_part(x.astype(F32), mod[video], qkv, out, y, g)
+
+    @pl.when(finishing)
+    def _():
+        pltpu.make_async_copy(x_v, kept.at[slot], sems.at[0]).wait()
 
 
 def temporal_kernel(per_core, share, ids, step, arrived, qkv, mixed):
@@ -210,7 +224,7 @@
         store.wait()
 
 
-def tail_kernel(per_core, ids, step, returned, y_in, mod, tout, kept_in, x, kept, x_v, sem):
+def tail_kernel(per_core, ids, step, returned, y_in, mod, tout, kept_in, kept, x_v, sem):
     inside, video, slot = place_of(ids, step, per_core)
 
     @pl.when(inside)
@@ -219,7 +233,6 @@
         x_v[...] = leaving
         store = pltpu.make_async_copy(x_v, kept.at[slot], sem)
         store.start()
-        x[...] = leaving
         store.wait()
 
 
@@ -283,19 +296,23 @@
     mod_e, mod_o = jnp.where(core == 0, mod, mod2), jnp.where(core == 0, mod2, mod)
     tqkv2, tout2 = swapped(tqkv), swapped(tout)
     sqkv_e, sqkv_o, sout_e, sout_o = prepared(spatial_qkv, spatial_out, sqkv2, sout2)
-    tqkv_e, tqkv_o, tout_e, tout_o = prepared(tqkv, tout, tqkv2, tout2)
     source = frames_in.reshape(videos, tokens, model)
 
     x_s, y_s = shape((tokens, model), BF16), shape((tokens, model), F32)
     kept_s = shape((per_core, tokens, model), BF16)
     hold = [pltpu.VMEM((tokens, model), BF16), pltpu.SemaphoreType.DMA]
-    head = call(
-        functools.partial(head_kernel, per_core), "head",
-        [SMEM, SMEM, ANY, ANY, VMEM, ANY, ANY], [y_s, x_s], [VMEM, VMEM],
-        [
-            pltpu.VMEM((tokens, model), BF16), pltpu.VMEM((model, columns), BF16),
-            pltpu.VMEM((hw, model), BF16), pltpu.SemaphoreType.DMA((3,)),
-        ],
+    at_s = shape((1,), jnp.int32)
+    tick = call(
+        tick_kernel, "tick", [SMEM, ANY], [at_s, at_s, x_s], [SMEM, SMEM, ANY], [], {1: 2}
+    )
+    first = call(
+        functools.partial(first_kernel, per_core), "first", [SMEM] + [VMEM] * 4, [y_s, x_s],
+        [VMEM, VMEM], [],
+    )
+    cross = call(
+        functools.partial(cross_kernel, per_core, stages), "cross",
+        [SMEM, SMEM] + [VMEM] * 7 + [ANY, ANY], [y_s, x_s, kept_s], [VMEM, VMEM, ANY],
+        [pltpu.VMEM((tokens, model), BF16)] * 2 + [pltpu.SemaphoreType.DMA((2,))], {10: 2},
     )
     temporal = call(
         functools.partial(temporal_kernel, per_core, share), "temporal",
@@ -307,33 +324,53 @@
     )
     tail = call(
         functools.partial(tail_kernel, per_core), "tail",
-        [SMEM, SMEM] + [VMEM] * 4 + [ANY], [x_s, kept_s], [VMEM, ANY], hold, {6: 1},
+        [SMEM, SMEM] + [VMEM] * 4 + [ANY], [kept_s], [ANY], hold, {6: 0},
     )
 
     def exchange(a):
         out = lax.all_to_all(a.reshape(ranks, share, a.shape[1]), "seq", 0, 0, tiled=True)
         return out.reshape(a.shape)
 
-    def section_pair(at, even, odd, arriving):
-        y, g = head(ids, at, source, arriving, mod_e, sqkv_e, sout_e)
+    def sections_of(at, even, y, g):
         mixed = temporal(ids, at, exchange(g), tqkv_e)
         y, g, even = joint(
             ids, at, exchange(mixed), y, mod_e, mod_o, tout_e, sqkv_o, sout_o, even
         )
-        mixed = temporal(ids, at, exchange(g), tqkv_o)
-        x, odd = tail(ids, at, exchange(mixed), y, mod_o, tout_o, odd)
-        return even, odd, x
-
-    onward = [(i, (i + 2) ^ 1) for i in range(sections - 2)]
-
-    def advance(step, carried):
-        even, odd, x = section_pair(step.reshape(1), *carried)
-        return even, odd, lax.ppermute(x, "section", onward)
+        return even, y, g
+
+    onward = [(i, ((i + 2) % sections) ^ 1) for i in range(sections)]
+    back = [(j, i) for i, j in onward]
+
+    def advance(carried):
+        step, even, odd, y, g = carried
+        now, following, g = tick(step, g)
+        even, y, g = sections_of(now, even, y, g)
+        y = lax.ppermute(y, "section", onward)
+        mixed = lax.ppermute(temporal(ids, now, exchange(g), tqkv_o), "section", onward)
+        y, g, odd = cross(
+            ids, following, exchange(mixed), y, mod_p, mod_e, tout_p, sqkv_e, sout_e, source, odd
+        )
+        return following, even, odd, y, g
 
     kept = jnp.zeros(kept_s.shape, BF16)
     last = stages + per_core - 2
-    carried = lax.fori_loop(0, last, advance, (kept, kept, jnp.zeros((tokens, model), BF16)))
-    even, odd, _ = section_pair(jnp.full((1,), last, jnp.int32), *carried)
+    y, g = first(ids, source, mod_e, sqkv_e, sout_e)
+    tqkv2, g = lax.optimization_barrier((tqkv2, g))
+    tqkv_e, tqkv_o, tout_e, tout_o = prepared(tqkv, tout, tqkv2, tout2)
+    before = [(i, (i + 2) % sections) for i in range(1, sections, 2)]
+    tout_p = lax.ppermute(temporal_out[0], "section", before)
+    tout_p, tout_o = lax.optimization_barrier((tout_p, tout_o))
+    tout_p2 = lax.ppermute(tout_p, "section", [(i, i - 1) for i in range(1, sections, 2)])
+    tout_p = jnp.where(core == 0, tout_p2, tout_p)
+    mod_p = lax.ppermute(mod_o, "section", [(i, (i + 2) % sections) for i in range(sections)])
+    start = jnp.zeros((1,), jnp.int32)
+    at, even, odd, y, g = lax.while_loop(
+        lambda carried: carried[0][0] < last, advance, (start, kept, kept, y, g)
+    )
+    odd = lax.ppermute(odd, "section", back)
+    even, y, g = sections_of(at, even, y, g)
+    mixed = temporal(ids, at, exchange(g), tqkv_o)
+    (odd,) = tail(ids, at, exchange(mixed), y, mod_o, tout_o, odd)
     own = jnp.where(core == 0, even, odd)
     other = swapped(jnp.where(core == 0, odd, even))
     low, high = jnp.where(chain == 0, own, other), jnp.where(chain == 0, other, own)

time: 656 us -> 653 us (level)
  waiting for transfers between devices: 165 us -> 65.2 us
  starting transfers between devices: 14 us -> 96.8 us
  Pallas kernels: 76.4 us -> 107 us
  blocking collectives: 386 us -> 367 us
    ppermute x8 -> x20, waiting for transfers between devices: 156 us -> 41.8 us  [the longest x8 38.6 us: advance(): lax.ppermute(temporal(ids, now, exchange(g), tqkv_o), 'section', onward)]
    ppermute x8 -> x20, starting transfers between devices: 10.2 us -> 83.2 us  [the longest x8 59.8 us: advance(): y = lax.ppermute(y, 'section', onward)]
    pallas_call x45, Pallas kernels: 60.8 us -> 91.2 us  [the longest x9 30.4 us: sections_of(): mixed = temporal(ids, at, exchange(g), tqkv_e)]
    all_to_all x36 -> x34, blocking collectives: 386 us -> 367 us  [exchange(): lax.all_to_all(a.reshape(ranks, share, a.shape[1]), 'seq', 0, 0, tiled=True)]
    all_to_all x0 -> x2, waiting for transfers between devices: none -> 14.6 us  [exchange(): lax.all_to_all(a.reshape(ranks, share, a.shape[1]), 'seq', 0, 0, tiled=True)]
    all_to_all x0 -> x2, starting transfers between devices: none -> 7.33 us  [exchange(): lax.all_to_all(a.reshape(ranks, share, a.shape[1]), 'seq', 0, 0, tiled=True)]
  transfers between devices with their start and end apart: 14 -> 28, of which waited for: 10 -> 14; matrix products, arithmetic and copies ran while one was open for 0% -> 1% of each run, Pallas kernels for 1% -> 6%
where the time goes in v5:
time: 653 us; the launch traced here: 650 us
  blocking collectives  367 us (56%)
  Pallas kernels  107 us (16%)
  starting transfers between devices  96.8 us (15%)
  waiting for transfers between devices  65.2 us (10%)
    all_to_all x34, blocking collectives, exchange(): lax.all_to_all(a.reshape(ranks, share, a.shape[1]), 'seq', 0, 0, tiled=True)  367 us
    ppermute x8, starting transfers between devices, advance(): y = lax.ppermute(y, 'section', onward)  59.8 us
    ppermute x8, waiting for transfers between devices, advance(): lax.ppermute(temporal(ids, now, exchange(g), tqkv_o), 'section', onward)  38.6 us
    pallas_call x9, Pallas kernels, sections_of(): mixed = temporal(ids, at, exchange(g), tqkv_e)  30.4 us
    pallas_call x9, Pallas kernels, sections_of(): joint(ids, at, exchange(mixed), y, mod_e, mod_o, tout_e, sqkv_o, sout_o,...  23.3 us
    ppermute x8, starting transfers between devices, advance(): lax.ppermute(temporal(ids, now, exchange(g), tqkv_o), 'section', onward)  17.6 us
    pallas_call x2, Pallas kernels, prepared(): prepare(core_id, jnp.swapaxes(qkv[0], 0, 1), jnp.swapaxes(qkv2[0], 0, 1),...  15.7 us
    pallas_call x8, Pallas kernels, advance(): cross(ids, following, exchange(mixed), y, mod_p, mod_e, tout_p, sqkv_e, s...  14.9 us
  transfers between devices with their start and end apart: 28, of which 14 were waited for; matrix products, arithmetic and copies ran while one was open for 1% of the time, Pallas kernels for 6%

profile of v5, /device:TPU:225, one launch (start us, length us, event | category | flops | bytes accessed | tf_op | source)
XLA Modules:
  0.0 650.5 jit_solution(3950367677619803664)
XLA Ops:
  41.5 543.2 %while.15 = (s32[1]{0:T(128)}, bf16[2,128,1152]{2,1,0:T(8,128)(2,1)S(1)}, bf16[2,128,1152]{2,1,0:T(8,128)(2,1)S(1)}, f32[128,1152]{1,0:T(8,128)S(1)}, bf16[128,1...) while((s32[1]{0:T(128)}, ...), condition=%region_1.2_spmd, body=%region_0.1_spmd | while | flops 1 | bytes 37011836 | solution.py:367
  42.1 14.4 %all_to_all.36 = bf16[16,8,1152]{2,1,0:T(8,128)(2,1)S(1)} all-to-all(bf16[16,8,1152]{2,1,0:T(8,128)(2,1)S(1)} %bitcast.63), channel_id=1, replica_groups=mesh['section'=16,'seq'=16] {'seq'}, dimensions={0} | all-to-all | bytes 589824 | tf_op jit(solution)/shard_map/while/body/all_to_all | solution.py:331
  59.7 10.6 %all_to_all.37 = bf16[16,8,576]{2,1,0:T(8,128)(2,1)S(1)} all-to-all(bf16[16,8,576]{2,1,0:T(8,128)(2,1)S(1)} %bitcast.51), channel_id=1, replica_groups=mesh['section'=16,'seq'=16] {'seq'}, dimensions={0} | all-to-all | bytes 294912 | tf_op jit(solution)/shard_map/while/body/all_to_all | solution.py:331
  80.0 11.2 %all_to_all.38 = bf16[16,8,1152]{2,1,0:T(8,128)(2,1)S(1)} all-to-all(bf16[16,8,1152]{2,1,0:T(8,128)(2,1)S(1)} %bitcast.54), channel_id=1, replica_groups=mesh['section'=16,'seq'=16] {'seq'}, dimensions={0} | all-to-all | bytes 589824 | tf_op jit(solution)/shard_map/while/body/all_to_all | solution.py:331
  97.9 10.4 %all_to_all.39 = bf16[16,8,576]{2,1,0:T(8,128)(2,1)S(1)} all-to-all(bf16[16,8,576]{2,1,0:T(8,128)(2,1)S(1)} %bitcast.65), channel_id=1, replica_groups=mesh['section'=16,'seq'=16] {'seq'}, dimensions={0} | all-to-all | bytes 294912 | tf_op jit(solution)/shard_map/while/body/all_to_all | solution.py:331
  110.7 11.4 %all_to_all.36 = bf16[16,8,1152]{2,1,0:T(8,128)(2,1)S(1)} all-to-all(bf16[16,8,1152]{2,1,0:T(8,128)(2,1)S(1)} %bitcast.63), channel_id=1, replica_groups=mesh['section'=16,'seq'=16] {'seq'}, dimensions={0} | all-to-all | bytes 589824 | tf_op jit(solution)/shard_map/while/body/all_to_all | solution.py:331
  125.3 10.1 %all_to_all.37 = bf16[16,8,576]{2,1,0:T(8,128)(2,1)S(1)} all-to-all(bf16[16,8,576]{2,1,0:T(8,128)(2,1)S(1)} %bitcast.51), channel_id=1, replica_groups=mesh['section'=16,'seq'=16] {'seq'}, dimensions={0} | all-to-all | bytes 294912 | tf_op jit(solution)/shard_map/while/body/all_to_all | solution.py:331
  137.5 12.5 %collective-permute-start.1 = (f32[128,1152]{1,0:T(8,128)S(1)}, f32[128,1152]{1,0:T(8,128)S(1)}, u32[]{:S(2)}, u32[]{:S(2)}) collective-permute-start(f32[128,1152]{1,0:T(8,128)S(1)} %get-tuple-element.94), channel_id=1, source_target_pairs={{0,48},{16,32},{32,80},{48,64},{64,112},{80,96},{96,144},{112,128}... | collective-permute-start | bytes 1769480 | tf_op jit(solution)/shard_map/while/body/ppermute | solution.py:348
  150.0 10.7 %all_to_all.38 = bf16[16,8,1152]{2,1,0:T(8,128)(2,1)S(1)} all-to-all(bf16[16,8,1152]{2,1,0:T(8,128)(2,1)S(1)} %bitcast.54), channel_id=1, replica_groups=mesh['section'=16,'seq'=16] {'seq'}, dimensions={0} | all-to-all | bytes 589824 | tf_op jit(solution)/shard_map/while/body/all_to_all | solution.py:331
  179.6 11.3 %all_to_all.36 = bf16[16,8,1152]{2,1,0:T(8,128)(2,1)S(1)} all-to-all(bf16[16,8,1152]{2,1,0:T(8,128)(2,1)S(1)} %bitcast.63), channel_id=1, replica_groups=mesh['section'=16,'seq'=16] {'seq'}, dimensions={0} | all-to-all | bytes 589824 | tf_op jit(solution)/shard_map/while/body/all_to_all | solution.py:331
  194.0 10.5 %all_to_all.37 = bf16[16,8,576]{2,1,0:T(8,128)(2,1)S(1)} all-to-all(bf16[16,8,576]{2,1,0:T(8,128)(2,1)S(1)} %bitcast.51), channel_id=1, replica_groups=mesh['section'=16,'seq'=16] {'seq'}, dimensions={0} | all-to-all | bytes 294912 | tf_op jit(solution)/shard_map/while/body/all_to_all | solution.py:331
  213.6 10.7 %all_to_all.38 = bf16[16,8,1152]{2,1,0:T(8,128)(2,1)S(1)} all-to-all(bf16[16,8,1152]{2,1,0:T(8,128)(2,1)S(1)} %bitcast.54), channel_id=1, replica_groups=mesh['section'=16,'seq'=16] {'seq'}, dimensions={0} | all-to-all | bytes 589824 | tf_op jit(solution)/shard_map/while/body/all_to_all | solution.py:331
  234.1 10.8 %all_to_all.39 = bf16[16,8,576]{2,1,0:T(8,128)(2,1)S(1)} all-to-all(bf16[16,8,576]{2,1,0:T(8,128)(2,1)S(1)} %bitcast.65), channel_id=1, replica_groups=mesh['section'=16,'seq'=16] {'seq'}, dimensions={0} | all-to-all | bytes 294912 | tf_op jit(solution)/shard_map/while/body/all_to_all | solution.py:331
  247.3 11.0 %all_to_all.36 = bf16[16,8,1152]{2,1,0:T(8,128)(2,1)S(1)} all-to-all(bf16[16,8,1152]{2,1,0:T(8,128)(2,1)S(1)} %bitcast.63), channel_id=1, replica_groups=mesh['section'=16,'seq'=16] {'seq'}, dimensions={0} | all-to-all | bytes 589824 | tf_op jit(solution)/shard_map/while/body/all_to_all | solution.py:331
  261.5 10.3 %all_to_all.37 = bf16[16,8,576]{2,1,0:T(8,128)(2,1)S(1)} all-to-all(bf16[16,8,576]{2,1,0:T(8,128)(2,1)S(1)} %bitcast.51), channel_id=1, replica_groups=mesh['section'=16,'seq'=16] {'seq'}, dimensions={0} | all-to-all | bytes 294912 | tf_op jit(solution)/shard_map/while/body/all_to_all | solution.py:331
  281.2 10.7 %all_to_all.38 = bf16[16,8,1152]{2,1,0:T(8,128)(2,1)S(1)} all-to-all(bf16[16,8,1152]{2,1,0:T(8,128)(2,1)S(1)} %bitcast.54), channel_id=1, replica_groups=mesh['section'=16,'seq'=16] {'seq'}, dimensions={0} | all-to-all | bytes 589824 | tf_op jit(solution)/shard_map/while/body/all_to_all | solution.py:331
  298.1 10.5 %all_to_all.39 = bf16[16,8,576]{2,1,0:T(8,128)(2,1)S(1)} all-to-all(bf16[16,8,576]{2,1,0:T(8,128)(2,1)S(1)} %bitcast.65), channel_id=1, replica_groups=mesh['section'=16,'seq'=16] {'seq'}, dimensions={0} | all-to-all | bytes 294912 | tf_op jit(solution)/shard_map/while/body/all_to_all | solution.py:331
  310.9 11.1 %all_to_all.36 = bf16[16,8,1152]{2,1,0:T(8,128)(2,1)S(1)} all-to-all(bf16[16,8,1152]{2,1,0:T(8,128)(2,1)S(1)} %bitcast.63), channel_id=1, replica_groups=mesh['section'=16,'seq'=16] {'seq'}, dimensions={0} | all-to-all | bytes 589824 | tf_op jit(solution)/shard_map/while/body/all_to_all | solution.py:331
  325.2 10.5 %all_to_all.37 = bf16[16,8,576]{2,1,0:T(8,128)(2,1)S(1)} all-to-all(bf16[16,8,576]{2,1,0:T(8,128)(2,1)S(1)} %bitcast.51), channel_id=1, replica_groups=mesh['section'=16,'seq'=16] {'seq'}, dimensions={0} | all-to-all | bytes 294912 | tf_op jit(solution)/shard_map/while/body/all_to_all | solution.py:331
  345.0 10.7 %all_to_all.38 = bf16[16,8,1152]{2,1,0:T(8,128)(2,1)S(1)} all-to-all(bf16[16,8,1152]{2,1,0:T(8,128)(2,1)S(1)} %bitcast.54), channel_id=1, replica_groups=mesh['section'=16,'seq'=16] {'seq'}, dimensions={0} | all-to-all | bytes 589824 | tf_op jit(solution)/shard_map/while/body/all_to_all | solution.py:331
  361.9 11.0 %all_to_all.39 = bf16[16,8,576]{2,1,0:T(8,128)(2,1)S(1)} all-to-all(bf16[16,8,576]{2,1,0:T(8,128)(2,1)S(1)} %bitcast.65), channel_id=1, replica_groups=mesh['section'=16,'seq'=16] {'seq'}, dimensions={0} | all-to-all | bytes 294912 | tf_op jit(solution)/shard_map/while/body/all_to_all | solution.py:331
  375.3 11.1 %all_to_all.36 = bf16[16,8,1152]{2,1,0:T(8,128)(2,1)S(1)} all-to-all(bf16[16,8,1152]{2,1,0:T(8,128)(2,1)S(1)} %bitcast.63), channel_id=1, replica_groups=mesh['section'=16,'seq'=16] {'seq'}, dimensions={0} | all-to-all | bytes 589824 | tf_op jit(solution)/shard_map/while/body/all_to_all | solution.py:331
  389.6 10.3 %all_to_all.37 = bf16[16,8,576]{2,1,0:T(8,128)(2,1)S(1)} all-to-all(bf16[16,8,576]{2,1,0:T(8,128)(2,1)S(1)} %bitcast.51), channel_id=1, replica_groups=mesh['section'=16,'seq'=16] {'seq'}, dimensions={0} | all-to-all | bytes 294912 | tf_op jit(solution)/shard_map/while/body/all_to_all | solution.py:331
  409.4 10.7 %all_to_all.38 = bf16[16,8,1152]{2,1,0:T(8,128)(2,1)S(1)} all-to-all(bf16[16,8,1152]{2,1,0:T(8,128)(2,1)S(1)} %bitcast.54), channel_id=1, replica_groups=mesh['section'=16,'seq'=16] {'seq'}, dimensions={0} | all-to-all | bytes 589824 | tf_op jit(solution)/shard_map/while/body/all_to_all | solution.py:331
  438.6 10.8 %all_to_all.36 = bf16[16,8,1152]{2,1,0:T(8,128)(2,1)S(1)} all-to-all(bf16[16,8,1152]{2,1,0:T(8,128)(2,1)S(1)} %bitcast.63), channel_id=1, replica_groups=mesh['section'=16,'seq'=16] {'seq'}, dimensions={0} | all-to-all | bytes 589824 | tf_op jit(solution)/shard_map/while/body/all_to_all | solution.py:331
  474.7 10.7 %all_to_all.38 = bf16[16,8,1152]{2,1,0:T(8,128)(2,1)S(1)} all-to-all(bf16[16,8,1152]{2,1,0:T(8,128)(2,1)S(1)} %bitcast.54), channel_id=1, replica_groups=mesh['section'=16,'seq'=16] {'seq'}, dimensions={0} | all-to-all | bytes 589824 | tf_op jit(solution)/shard_map/while/body/all_to_all | solution.py:331
  488.6 11.3 %collective-permute-done = bf16[128,576]{1,0:T(8,128)(2,1)S(1)} collective-permute-done((bf16[128,576]{1,0:T(8,128)(2,1)S(1)}, bf16[128,576]{1,0:T(8,128)(2,1)S(1)}, u32[]{:S(2)}, u32[]{:S(2)}) %collective-permute-start) | collective-permute-done | bytes 147488 | tf_op jit(solution)/shard_map/while/body/ppermute | solution.py:349
  515.0 12.8 %all_to_all.36 = bf16[16,8,1152]{2,1,0:T(8,128)(2,1)S(1)} all-to-all(bf16[16,8,1152]{2,1,0:T(8,128)(2,1)S(1)} %bitcast.63), channel_id=1, replica_groups=mesh['section'=16,'seq'=16] {'seq'}, dimensions={0} | all-to-all | bytes 589824 | tf_op jit(solution)/shard_map/while/body/all_to_all | solution.py:331
  547.0 10.9 %all_to_all.38 = bf16[16,8,1152]{2,1,0:T(8,128)(2,1)S(1)} all-to-all(bf16[16,8,1152]{2,1,0:T(8,128)(2,1)S(1)} %bitcast.54), channel_id=1, replica_groups=mesh['section'=16,'seq'=16] {'seq'}, dimensions={0} | all-to-all | bytes 589824 | tf_op jit(solution)/shard_map/while/body/all_to_all | solution.py:331
  570.1 10.1 %all_to_all.39 = bf16[16,8,576]{2,1,0:T(8,128)(2,1)S(1)} all-to-all(bf16[16,8,576]{2,1,0:T(8,128)(2,1)S(1)} %bitcast.65), channel_id=1, replica_groups=mesh['section'=16,'seq'=16] {'seq'}, dimensions={0} | all-to-all | bytes 294912 | tf_op jit(solution)/shard_map/while/body/all_to_all | solution.py:331
  602.6 10.9 %all_to_all.40 = bf16[16,8,576]{2,1,0:T(8,128)(2,1)S(1)} all-to-all(bf16[16,8,576]{2,1,0:T(8,128)(2,1)S(1)} %bitcast.58), channel_id=1, replica_groups=mesh['section'=16,'seq'=16] {'seq'}, dimensions={0} | all-to-all | bytes 294912 | tf_op jit(solution)/shard_map/all_to_all | solution.py:331
  618.1 10.8 %all_to_all.41 = bf16[16,8,1152]{2,1,0:T(8,128)(2,1)S(1)} all-to-all(bf16[16,8,1152]{2,1,0:T(8,128)(2,1)S(1)} %bitcast.60), channel_id=1, replica_groups=mesh['section'=16,'seq'=16] {'seq'}, dimensions={0} | all-to-all | bytes 589824 | tf_op jit(solution)/shard_map/all_to_all | solution.py:331
  (235 shorter events, 303.7 us)
Async XLA Ops:
  0.0 10.1 %collective-permute-start.3 = (bf16[1,1152,1728]{1,2,0:T(8,128)(2,1)}, bf16[1,1152,1728]{1,2,0:T(8,128)(2,1)}, u32[]{:S(2)}, u32[]{:S(2)}) collective-permute-start(bf16[1,1152,1728]{1,2,0:T(8,128)(2,1)} %param.9), channel_id=1, source_target_pairs={{0,16},{16,0},{32,48},{48,32},{64,80},{80,64},{96,112},{112,96},{1... | collective-permute-start | bytes 11943944 | tf_op jit(solution)/shard_map/ppermute | solution.py:272
  0.7 8.8 %collective-permute-start.4 = (bf16[1,576,1152]{2,1,0:T(8,128)(2,1)}, bf16[1,576,1152]{2,1,0:T(8,128)(2,1)S(1)}, u32[]{:S(2)}, u32[]{:S(2)}) collective-permute-start(bf16[1,576,1152]{2,1,0:T(8,128)(2,1)} %param.10), channel_id=1, source_target_pairs={{0,16},{16,0},{32,48},{48,32},{64,80},{80,64},{96,112},{112,96},{1... | collective-permute-start | bytes 3981320 | tf_op jit(solution)/shard_map/ppermute | solution.py:272
  1.6 7.9 %collective-permute-start.2 = (f32[4,6,1152]{2,1,0:T(8,128)S(1)}, f32[4,6,1152]{2,1,0:T(8,128)S(1)}, u32[]{:S(2)}, u32[]{:S(2)}) collective-permute-start(f32[4,6,1152]{2,1,0:T(8,128)S(1)} %bitcast.72), channel_id=1, source_target_pairs={{0,16},{16,0},{32,48},{48,32},{64,80},{80,64},{96,112},{112,96},{1... | collective-permute-start | bytes 331784 | tf_op jit(solution)/shard_map/ppermute | solution.py:272
  10.1 14.9 %collective-permute-start.5 = (bf16[1,1152,1728]{1,2,0:T(8,128)(2,1)}, bf16[1,1152,1728]{1,2,0:T(8,128)(2,1)}, u32[]{:S(2)}, u32[]{:S(2)}) collective-permute-start(bf16[1,1152,1728]{1,2,0:T(8,128)(2,1)} %param.11), channel_id=1, source_target_pairs={{0,16},{16,0},{32,48},{48,32},{64,80},{80,64},{96,112},{112,96},{1... | collective-permute-start | bytes 11943944 | tf_op jit(solution)/shard_map/ppermute | solution.py:272
  10.5 14.5 %collective-permute-start.6 = (bf16[1,576,1152]{2,1,0:T(8,128)(2,1)}, bf16[1,576,1152]{2,1,0:T(8,128)(2,1)}, u32[]{:S(2)}, u32[]{:S(2)}) collective-permute-start(bf16[1,576,1152]{2,1,0:T(8,128)(2,1)} %param.12), channel_id=1, source_target_pairs={{0,16},{16,0},{32,48},{48,32},{64,80},{80,64},{96,112},{112,96},{1... | collective-permute-start | bytes 3981320 | tf_op jit(solution)/shard_map/ppermute | solution.py:272
  10.7 22.6 %collective-permute-start.8 = (bf16[576,1152]{1,0:T(8,128)(2,1)}, bf16[576,1152]{1,0:T(8,128)(2,1)}, u32[]{:S(2)}, u32[]{:S(2)}) collective-permute-start(bf16[576,1152]{1,0:T(8,128)(2,1)} %bitcast.69), channel_id=1, source_target_pairs={{16,48},{48,80},{80,112},{112,144},{144,176},{176,208},{208,240},{... | collective-permute-start | bytes 3981320 | tf_op jit(solution)/shard_map/ppermute | solution.py:361
  33.3 4.9 collective-permute-start.9
  35.5 5.9 collective-permute-start.7
  41.5 28.7 %copy-start.19 = (f32[4,6,1152]{2,1,0:T(8,128)S(1)}, f32[4,6,1152]{2,1,0:T(8,128)}, u32[]{:S(2)}) copy-start(f32[4,6,1152]{2,1,0:T(8,128)} %get-tuple-element.261.following) | copy-start | bytes 331780 | tf_op jit(solution)/shard_map/while
  42.1 28.2 %copy-start.7 = (bf16[576,1152]{1,0:T(8,128)(2,1)S(1)}, bf16[576,1152]{1,0:T(8,128)(2,1)}, u32[]{:S(2)}) copy-start(bf16[576,1152]{1,0:T(8,128)(2,1)} %get-tuple-element.264.out) | copy-start | bytes 3981316 | tf_op jit(solution)/shard_map/while
  72.3 36.1 %collective-permute-start.1 = (f32[128,1152]{1,0:T(8,128)S(1)}, f32[128,1152]{1,0:T(8,128)S(1)}, u32[]{:S(2)}, u32[]{:S(2)}) collective-permute-start(f32[128,1152]{1,0:T(8,128)S(1)} %get-tuple-element.94), channel_id=1, source_target_pairs={{0,48},{16,32},{32,80},{48,64},{64,112},{80,96},{96,144},{112,128}... | collective-permute-start | bytes 1769480 | tf_op jit(solution)/shard_map/while/body/ppermute | solution.py:348
  92.6 5.4 collective-permute-start
  137.5 39.7 %collective-permute-start.1 = (f32[128,1152]{1,0:T(8,128)S(1)}, f32[128,1152]{1,0:T(8,128)S(1)}, u32[]{:S(2)}, u32[]{:S(2)}) collective-permute-start(f32[128,1152]{1,0:T(8,128)S(1)} %get-tuple-element.94), channel_id=1, source_target_pairs={{0,48},{16,32},{32,80},{48,64},{64,112},{80,96},{96,144},{112,128}... | collective-permute-start | bytes 1769480 | tf_op jit(solution)/shard_map/while/body/ppermute | solution.py:348
  162.0 5.2 collective-permute-start
  206.5 38.4 %collective-permute-start.1 = (f32[128,1152]{1,0:T(8,128)S(1)}, f32[128,1152]{1,0:T(8,128)S(1)}, u32[]{:S(2)}, u32[]{:S(2)}) collective-permute-start(f32[128,1152]{1,0:T(8,128)S(1)} %get-tuple-element.94), channel_id=1, source_target_pairs={{0,48},{16,32},{32,80},{48,64},{64,112},{80,96},{96,144},{112,128}... | collective-permute-start | bytes 1769480 | tf_op jit(solution)/shard_map/while/body/ppermute | solution.py:348
  225.6 8.5 %collective-permute-start = (bf16[128,576]{1,0:T(8,128)(2,1)S(1)}, bf16[128,576]{1,0:T(8,128)(2,1)S(1)}, u32[]{:S(2)}, u32[]{:S(2)}) collective-permute-start(bf16[128,576]{1,0:T(8,128)(2,1)S(1)} %temporal.5), channel_id=1, source_target_pairs={{0,48},{16,32},{32,80},{48,64},{64,112},{80,96},{96,144},{112,128}... | collective-permute-start | bytes 442376 | tf_op jit(solution)/shard_map/while/body/ppermute | solution.py:349
  273.7 34.8 %collective-permute-start.1 = (f32[128,1152]{1,0:T(8,128)S(1)}, f32[128,1152]{1,0:T(8,128)S(1)}, u32[]{:S(2)}, u32[]{:S(2)}) collective-permute-start(f32[128,1152]{1,0:T(8,128)S(1)} %get-tuple-element.94), channel_id=1, source_target_pairs={{0,48},{16,32},{32,80},{48,64},{64,112},{80,96},{96,144},{112,128}... | collective-permute-start | bytes 1769480 | tf_op jit(solution)/shard_map/while/body/ppermute | solution.py:348
  293.2 4.8 collective-permute-start
  337.7 35.2 %collective-permute-start.1 = (f32[128,1152]{1,0:T(8,128)S(1)}, f32[128,1152]{1,0:T(8,128)S(1)}, u32[]{:S(2)}, u32[]{:S(2)}) collective-permute-start(f32[128,1152]{1,0:T(8,128)S(1)} %get-tuple-element.94), channel_id=1, source_target_pairs={{0,48},{16,32},{32,80},{48,64},{64,112},{80,96},{96,144},{112,128}... | collective-permute-start | bytes 1769480 | tf_op jit(solution)/shard_map/while/body/ppermute | solution.py:348
  357.0 4.9 collective-permute-start
  401.8 34.4 %collective-permute-start.1 = (f32[128,1152]{1,0:T(8,128)S(1)}, f32[128,1152]{1,0:T(8,128)S(1)}, u32[]{:S(2)}, u32[]{:S(2)}) collective-permute-start(f32[128,1152]{1,0:T(8,128)S(1)} %get-tuple-element.94), channel_id=1, source_target_pairs={{0,48},{16,32},{32,80},{48,64},{64,112},{80,96},{96,144},{112,128}... | collective-permute-start | bytes 1769480 | tf_op jit(solution)/shard_map/while/body/ppermute | solution.py:348
  421.4 4.8 collective-permute-start
  464.6 45.3 %collective-permute-start.1 = (f32[128,1152]{1,0:T(8,128)S(1)}, f32[128,1152]{1,0:T(8,128)S(1)}, u32[]{:S(2)}, u32[]{:S(2)}) collective-permute-start(f32[128,1152]{1,0:T(8,128)S(1)} %get-tuple-element.94), channel_id=1, source_target_pairs={{0,48},{16,32},{32,80},{48,64},{64,112},{80,96},{96,144},{112,128}... | collective-permute-start | bytes 1769480 | tf_op jit(solution)/shard_map/while/body/ppermute | solution.py:348
  486.7 13.2 %collective-permute-start = (bf16[128,576]{1,0:T(8,128)(2,1)S(1)}, bf16[128,576]{1,0:T(8,128)(2,1)S(1)}, u32[]{:S(2)}, u32[]{:S(2)}) collective-permute-start(bf16[128,576]{1,0:T(8,128)(2,1)S(1)} %temporal.5), channel_id=1, source_target_pairs={{0,48},{16,32},{32,80},{48,64},{64,112},{80,96},{96,144},{112,128}... | collective-permute-start | bytes 442376 | tf_op jit(solution)/shard_map/while/body/ppermute | solution.py:349
  514.4 27.8 %copy-start.19 = (f32[4,6,1152]{2,1,0:T(8,128)S(1)}, f32[4,6,1152]{2,1,0:T(8,128)}, u32[]{:S(2)}) copy-start(f32[4,6,1152]{2,1,0:T(8,128)} %get-tuple-element.261.following) | copy-start | bytes 331780 | tf_op jit(solution)/shard_map/while
  514.9 27.2 %copy-start.7 = (bf16[576,1152]{1,0:T(8,128)(2,1)S(1)}, bf16[576,1152]{1,0:T(8,128)(2,1)}, u32[]{:S(2)}) copy-start(bf16[576,1152]{1,0:T(8,128)(2,1)} %get-tuple-element.264.out) | copy-start | bytes 3981316 | tf_op jit(solution)/shard_map/while
  546.9 33.3 %collective-permute-start.1 = (f32[128,1152]{1,0:T(8,128)S(1)}, f32[128,1152]{1,0:T(8,128)S(1)}, u32[]{:S(2)}, u32[]{:S(2)}) collective-permute-start(f32[128,1152]{1,0:T(8,128)S(1)} %get-tuple-element.94), channel_id=1, source_target_pairs={{0,48},{16,32},{32,80},{48,64},{64,112},{80,96},{96,144},{112,128}... | collective-permute-start | bytes 1769480 | tf_op jit(solution)/shard_map/while/body/ppermute | solution.py:348
  560.6 9.4 %collective-permute-start = (bf16[128,576]{1,0:T(8,128)(2,1)S(1)}, bf16[128,576]{1,0:T(8,128)(2,1)S(1)}, u32[]{:S(2)}, u32[]{:S(2)}) collective-permute-start(bf16[128,576]{1,0:T(8,128)(2,1)S(1)} %temporal.5), channel_id=1, source_target_pairs={{0,48},{16,32},{32,80},{48,64},{64,112},{80,96},{96,144},{112,128}... | collective-permute-start | bytes 442376 | tf_op jit(solution)/shard_map/while/body/ppermute | solution.py:349
  586.7 12.0 %all-to-all-start.4 = ((bf16[16,8,1152]{2,1,0:T(8,128)(2,1)}), bf16[16,8,1152]{2,1,0:T(8,128)(2,1)S(1)}, u32[]{:S(2)}, u32[]{:S(2)}) async-start(bf16[16,8,1152]{2,1,0:T(8,128)(2,1)} %bitcast.64), calls=%async_computation.4 | async-start | bytes 589824 | tf_op jit(solution)/shard_map/all_to_all | solution.py:331
  590.3 44.9 %collective-permute-start.10 = (bf16[2,128,1152]{2,1,0:T(8,128)(2,1)}, bf16[2,128,1152]{2,1,0:T(8,128)(2,1)S(1)}, u32[]{:S(2)}, u32[]{:S(2)}) collective-permute-start(bf16[2,128,1152]{2,1,0:T(8,128)(2,1)} %copy-done.18), channel_id=1, source_target_pairs={{48,0},{32,16},{80,32},{64,48},{112,64},{96,80},{144,96},{128,112}... | collective-permute-start | bytes 1769480 | tf_op jit(solution)/shard_map/ppermute | solution.py:370
  631.5 10.5 %all-to-all-start.7 = ((bf16[16,8,576]{2,1,0:T(8,128)(2,1)}), bf16[16,8,576]{2,1,0:T(8,128)(2,1)S(1)}, u32[]{:S(2)}, u32[]{:S(2)}) async-start(bf16[16,8,576]{2,1,0:T(8,128)(2,1)} %bitcast.33), calls=%async_computation.7 | async-start | bytes 327680 | tf_op jit(solution)/shard_map/all_to_all | solution.py:331
  643.1 6.1 collective-permute-start.11
  (56 other events, 876.8 us)

commit v6 on v5

--- a/solution.py
+++ b/solution.py
@@ -139,11 +139,11 @@
         copy.wait()
 
 
-def place_of(ids, step, per_core):
-    micro = step[0] - ids[0]
+def place_of(flags, per_core, late=0):
+    micro = flags[2] - late - flags[0]
     inside = jnp.logical_and(micro >= 0, micro < per_core)
     clipped = jnp.clip(micro, 0, per_core - 1)
-    return inside, ids[1] * per_core + clipped, clipped
+    return inside, flags[1] * per_core + clipped, clipped
 
 
 def spatial_part(x, factors, qkv, out, y, g, ready=None):
@@ -156,43 +156,44 @@
     g[...] = norm_modulate(middle, factors[3:4], factors[4:5])
 
 
-def tick_kernel(step, g_in, now, following, g):
-    now[0] = step[0]
-    following[0] = step[0] + 1
-
-
-def first_kernel(per_core, ids, frames, mod, qkv, out, y, g):
-    video = ids[1] * per_core
-
-    @pl.when(ids[0] == 0)
+def tick_kernel(flags, g_in, following, g):
+    following[0] = flags[0]
+    following[1] = flags[1]
+    following[2] = flags[2] + 1
+
+
+def first_kernel(per_core, flags, frames, mod, qkv, out, y, g):
+    video = flags[1] * per_core
+
+    @pl.when(flags[0] == 0)
     def _():
         spatial_part(frames[video].astype(F32), mod[video], qkv, out, y, g)
 
 
 def cross_kernel(
-    per_core, stages, ids, step, returned, y_in, mod_p, mod, tout_p, qkv, out, frames, kept_in,
+    per_core, stages, flags, returned, y_in, mod_p, mod, tout_p, qkv, out, frames, kept_in,
     y, g, kept, x_v, new_v, sems,
 ):
-    inside, video, _ = place_of(ids, step, per_core)
-    micro = jnp.where(ids[0] == 0, step[0] - stages, step[0] - ids[0])
+    inside, video, _ = place_of(flags, per_core)
+    micro = jnp.where(flags[0] == 0, flags[2] - stages, flags[2] - flags[0])
     finishing = jnp.logical_and(micro >= 0, micro < per_core)
     slot = jnp.clip(micro, 0, per_core - 1)
 
     @pl.when(finishing)
     def _():
-        factor = mod_p[ids[1] * per_core + slot][5:6]
+        factor = mod_p[flags[1] * per_core + slot][5:6]
         x_v[...] = (y_in[...] + factor * dot(returned[...], tout_p[...])).astype(BF16)
         pltpu.make_async_copy(x_v, kept.at[slot], sems.at[0]).start()
 
     @pl.when(inside)
     def _():
-        @pl.when(ids[0] == 0)
+        @pl.when(flags[0] == 0)
         def _():
             copy = pltpu.make_async_copy(frames.at[video], new_v, sems.at[1])
             copy.start()
             copy.wait()
 
-        x = jnp.where(ids[0] == 0, new_v[...], x_v[...])
+        x = jnp.where(flags[0] == 0, new_v[...], x_v[...])
         spatial_part(x.astype(F32), mod[video], qkv, out, y, g)
 
     @pl.when(finishing)
@@ -200,19 +201,15 @@
         pltpu.make_async_copy(x_v, kept.at[slot], sems.at[0]).wait()
 
 
-def temporal_kernel(per_core, share, ids, step, arrived, qkv, mixed):
-    inside, _, _ = place_of(ids, step, per_core)
-
-    @pl.when(inside)
-    def _():
-        mixed[...] = attention(dot(arrived[...], qkv[...]), mixed.shape[1], share)
+def temporal_kernel(share, arrived, qkv, mixed):
+    mixed[...] = attention(dot(arrived[...], qkv[...]), mixed.shape[1], share)
 
 
 def joint_kernel(
-    per_core, ids, step, returned, y_in, mod, following, tout, qkv, out, kept_in,
+    per_core, late, flags, returned, y_in, mod, following, tout, qkv, out, kept_in,
     y, g, kept, x_v, sem,
 ):
-    inside, video, slot = place_of(ids, step, per_core)
+    inside, video, slot = place_of(flags, per_core, late)
 
     @pl.when(inside)
     def _():
@@ -224,8 +221,8 @@
         store.wait()
 
 
-def tail_kernel(per_core, ids, step, returned, y_in, mod, tout, kept_in, kept, x_v, sem):
-    inside, video, slot = place_of(ids, step, per_core)
+def tail_kernel(per_core, flags, returned, y_in, mod, tout, kept_in, kept, x_v, sem):
+    inside, video, slot = place_of(flags, per_core)
 
     @pl.when(inside)
     def _():
@@ -242,7 +239,7 @@
 HBM = pl.BlockSpec(memory_space=pltpu.HBM)
 
 
-def call(kernel, name, ins, outs, specs, scratch, aliases={}, limit=14):
+def call(kernel, name, ins, outs, specs, scratch, aliases={}, limit=14, flops=0):
     return pl.pallas_call(
         kernel,
         name=name,
@@ -251,6 +248,9 @@
         out_shape=outs,
         scratch_shapes=scratch,
         input_output_aliases=aliases,
+        cost_estimate=None if not flops else pl.CostEstimate(
+            flops=flops, transcendentals=0, bytes_accessed=flops // 1000
+        ),
         compiler_params=pltpu.CompilerParams(vmem_limit_bytes=limit * 2**20),
     )
 
@@ -282,7 +282,7 @@
     )
     chain = (stage + core) % 2
     core_id = core.reshape(1).astype(jnp.int32)
-    ids = jnp.stack([stage, chain]).astype(jnp.int32)
+    flags = jnp.stack([stage, chain, jnp.zeros_like(stage)]).astype(jnp.int32)
     def prepared(qkv, out, qkv2, out2):
         return prepare(
             core_id, jnp.swapaxes(qkv[0], 0, 1), jnp.swapaxes(qkv2[0], 0, 1), out[0], out2[0]
@@ -301,9 +301,10 @@
     x_s, y_s = shape((tokens, model), BF16), shape((tokens, model), F32)
     kept_s = shape((per_core, tokens, model), BF16)
     hold = [pltpu.VMEM((tokens, model), BF16), pltpu.SemaphoreType.DMA]
-    at_s = shape((1,), jnp.int32)
+    at_s = shape((3,), jnp.int32)
     tick = call(
-        tick_kernel, "tick", [SMEM, ANY], [at_s, at_s, x_s], [SMEM, SMEM, ANY], [], {1: 2}
+        tick_kernel, "tick", [SMEM, ANY], [at_s, x_s], [SMEM, ANY], [], {1: 1},
+        flops=2 * 10**9,
     )
     first = call(
         functools.partial(first_kernel, per_core), "first", [SMEM] + [VMEM] * 4, [y_s, x_s],
@@ -311,30 +312,30 @@
     )
     cross = call(
         functools.partial(cross_kernel, per_core, stages), "cross",
-        [SMEM, SMEM] + [VMEM] * 7 + [ANY, ANY], [y_s, x_s, kept_s], [VMEM, VMEM, ANY],
-        [pltpu.VMEM((tokens, model), BF16)] * 2 + [pltpu.SemaphoreType.DMA((2,))], {10: 2},
+        [SMEM] + [VMEM] * 7 + [ANY, ANY], [y_s, x_s, kept_s], [VMEM, VMEM, ANY],
+        [pltpu.VMEM((tokens, model), BF16)] * 2 + [pltpu.SemaphoreType.DMA((2,))], {9: 2},
+        flops=0,
     )
     temporal = call(
-        functools.partial(temporal_kernel, per_core, share), "temporal",
-        [SMEM, SMEM, VMEM, VMEM], shape((tokens, hw), BF16), VMEM, [],
-    )
-    joint = call(
-        functools.partial(joint_kernel, per_core), "joint",
-        [SMEM, SMEM] + [VMEM] * 7 + [ANY], [y_s, x_s, kept_s], [VMEM, VMEM, ANY], hold, {9: 2},
+        functools.partial(temporal_kernel, share), "temporal", [VMEM, VMEM], shape((tokens, hw), BF16), VMEM, [], flops=0,
+    )
+    joint = lambda late: call(
+        functools.partial(joint_kernel, per_core, late), "joint",
+        [SMEM] + [VMEM] * 7 + [ANY], [y_s, x_s, kept_s], [VMEM, VMEM, ANY], hold, {8: 2}, flops=0,
     )
     tail = call(
         functools.partial(tail_kernel, per_core), "tail",
-        [SMEM, SMEM] + [VMEM] * 4 + [ANY], [kept_s], [ANY], hold, {6: 0},
+        [SMEM] + [VMEM] * 4 + [ANY], [kept_s], [ANY], hold, {5: 0},
     )
 
     def exchange(a):
         out = lax.all_to_all(a.reshape(ranks, share, a.shape[1]), "seq", 0, 0, tiled=True)
         return out.reshape(a.shape)
 
-    def sections_of(at, even, y, g):
-        mixed = temporal(ids, at, exchange(g), tqkv_e)
-        y, g, even = joint(
-            ids, at, exchange(mixed), y, mod_e, mod_o, tout_e, sqkv_o, sout_o, even
+    def sections_of(late, flags, even, y, g):
+        mixed = temporal(exchange(g), tqkv_e)
+        y, g, even = joint(late)(
+            flags, exchange(mixed), y, mod_e, mod_o, tout_e, sqkv_o, sout_o, even
         )
         return even, y, g
 
@@ -342,35 +343,34 @@
     back = [(j, i) for i, j in onward]
 
     def advance(carried):
-        step, even, odd, y, g = carried
-        now, following, g = tick(step, g)
-        even, y, g = sections_of(now, even, y, g)
+        flags, even, odd, y, g = carried
+        following, g = tick(flags, g)
+        even, y, g = sections_of(1, following, even, y, g)
         y = lax.ppermute(y, "section", onward)
-        mixed = lax.ppermute(temporal(ids, now, exchange(g), tqkv_o), "section", onward)
+        mixed = lax.ppermute(temporal(exchange(g), tqkv_o), "section", onward)
         y, g, odd = cross(
-            ids, following, exchange(mixed), y, mod_p, mod_e, tout_p, sqkv_e, sout_e, source, odd
+            following, exchange(mixed), y, mod_p, mod_e, tout_p, sqkv_e, sout_e, source, odd
         )
         return following, even, odd, y, g
 
     kept = jnp.zeros(kept_s.shape, BF16)
     last = stages + per_core - 2
-    y, g = first(ids, source, mod_e, sqkv_e, sout_e)
-    tqkv2, g = lax.optimization_barrier((tqkv2, g))
-    tqkv_e, tqkv_o, tout_e, tout_o = prepared(tqkv, tout, tqkv2, tout2)
+    y, g = first(flags, source, mod_e, sqkv_e, sout_e)
     before = [(i, (i + 2) % sections) for i in range(1, sections, 2)]
     tout_p = lax.ppermute(temporal_out[0], "section", before)
-    tout_p, tout_o = lax.optimization_barrier((tout_p, tout_o))
+    mod_p = lax.ppermute(mod_o, "section", [(i, (i + 2) % sections) for i in range(sections)])
+    tqkv2, g, tout_p, mod_p = lax.optimization_barrier((tqkv2, g, tout_p, mod_p))
     tout_p2 = lax.ppermute(tout_p, "section", [(i, i - 1) for i in range(1, sections, 2)])
+    tqkv_e, tqkv_o, tout_e, tout_o = prepared(tqkv, tout, tqkv2, tout2)
+    tout_p2, tout_o = lax.optimization_barrier((tout_p2, tout_o))
     tout_p = jnp.where(core == 0, tout_p2, tout_p)
-    mod_p = lax.ppermute(mod_o, "section", [(i, (i + 2) % sections) for i in range(sections)])
-    start = jnp.zeros((1,), jnp.int32)
-    at, even, odd, y, g = lax.while_loop(
-        lambda carried: carried[0][0] < last, advance, (start, kept, kept, y, g)
+    flags, even, odd, y, g = lax.while_loop(
+        lambda carried: carried[0][2] < last, advance, (flags, kept, kept, y, g)
     )
     odd = lax.ppermute(odd, "section", back)
-    even, y, g = sections_of(at, even, y, g)
-    mixed = temporal(ids, at, exchange(g), tqkv_o)
-    (odd,) = tail(ids, at, exchange(mixed), y, mod_o, tout_o, odd)
+    even, y, g = sections_of(0, flags, even, y, g)
+    mixed = temporal(exchange(g), tqkv_o)
+    (odd,) = tail(flags, exchange(mixed), y, mod_o, tout_o, odd)
     own = jnp.where(core == 0, even, odd)
     other = swapped(jnp.where(core == 0, odd, even))
     low, high = jnp.where(chain == 0, own, other), jnp.where(chain == 0, other, own)

time: 653 us -> 631 us (0.966)
  Pallas kernels: 107 us -> 84 us
  starting transfers between devices: 96.8 us -> 78 us
  local copies, waits for them, and re-layouts: 3.84 us -> 19.2 us
    pallas_call x45, Pallas kernels: 91.2 us -> 68.2 us  [the longest x9 14.8 us: sections_of(): joint(late)]
    ppermute x8, starting transfers between devices: 59.8 us -> 45.7 us  [advance(): y = lax.ppermute(y, 'section', onward)]
    slice x0 -> x9, local copies, waits for them, and re-layouts: none -> 10.4 us  [on_device(): carried[0][2] < last]
  transfers between devices with their start and end apart: 28 -> 28, of which waited for: 14 -> 14; matrix products, arithmetic and copies ran while one was open for 1% -> 0% of each run, Pallas kernels for 6% -> 6%
where the time goes in v6:
time: 631 us; the launch traced here: 629 us
  blocking collectives  368 us (58%)
  Pallas kernels  84 us (13%)
  starting transfers between devices  78 us (12%)
  waiting for transfers between devices  67.4 us (11%)
  local copies, waits for them, and re-layouts  19.2 us (3%)
  loops' own time  6.6 us (1%)
    all_to_all x34, blocking collectives, exchange(): lax.all_to_all(a.reshape(ranks, share, a.shape[1]), 'seq', 0, 0, tiled=True)  368 us
    ppermute x8, starting transfers between devices, advance(): y = lax.ppermute(y, 'section', onward)  45.7 us
    ppermute x8, waiting for transfers between devices, advance(): mixed = lax.ppermute(temporal(exchange(g), tqkv_o), 'section', onward)  36.6 us
    pallas_call x2, Pallas kernels, prepared(): prepare(core_id, jnp.swapaxes(qkv[0], 0, 1), jnp.swapaxes(qkv2[0], 0, 1),...  15.8 us
    pallas_call x9, Pallas kernels, sections_of(): joint(late)  14.8 us
    pallas_call x9, Pallas kernels, sections_of(): mixed = temporal(exchange(g), tqkv_e)  14.5 us
    all_to_all x2, waiting for transfers between devices, exchange(): lax.all_to_all(a.reshape(ranks, share, a.shape[1]), 'seq', 0, 0, tiled=True)  14.3 us
    ppermute x8, starting transfers between devices, advance(): mixed = lax.ppermute(temporal(exchange(g), tqkv_o), 'section', onward)  14.3 us
  transfers between devices with their start and end apart: 28, of which 14 were waited for; matrix products, arithmetic and copies ran while one was open for 0% of the time, Pallas kernels for 6%

profile of v6, /device:TPU:225, one launch (start us, length us, event | category | flops | bytes accessed | tf_op | source)
XLA Modules:
  0.0 628.6 jit_solution(13937195377215436095)
XLA Ops:
  45.5 518.5 %while.15 = (s32[3]{0:T(128)}, bf16[2,128,1152]{2,1,0:T(8,128)(2,1)S(1)}, bf16[2,128,1152]{2,1,0:T(8,128)(2,1)S(1)}, f32[128,1152]{1,0:T(8,128)S(1)}, bf16[128,1...) while((s32[3]{0:T(128)}, ...), condition=%region_1.2_spmd, body=%region_0.1_spmd | while | flops 2000000000 | bytes 60393000 | solution.py:367
  49.2 14.3 %all_to_all.36 = bf16[16,8,1152]{2,1,0:T(8,128)(2,1)S(1)} all-to-all(bf16[16,8,1152]{2,1,0:T(8,128)(2,1)S(1)} %bitcast.63), channel_id=1, replica_groups=mesh['section'=16,'seq'=16] {'seq'}, dimensions={0} | all-to-all | bytes 589824 | tf_op jit(solution)/shard_map/while/body/all_to_all | solution.py:332
  76.5 10.7 %all_to_all.38 = bf16[16,8,1152]{2,1,0:T(8,128)(2,1)S(1)} all-to-all(bf16[16,8,1152]{2,1,0:T(8,128)(2,1)S(1)} %bitcast.54), channel_id=1, replica_groups=mesh['section'=16,'seq'=16] {'seq'}, dimensions={0} | all-to-all | bytes 589824 | tf_op jit(solution)/shard_map/while/body/all_to_all | solution.py:332
  108.7 11.0 %all_to_all.36 = bf16[16,8,1152]{2,1,0:T(8,128)(2,1)S(1)} all-to-all(bf16[16,8,1152]{2,1,0:T(8,128)(2,1)S(1)} %bitcast.63), channel_id=1, replica_groups=mesh['section'=16,'seq'=16] {'seq'}, dimensions={0} | all-to-all | bytes 589824 | tf_op jit(solution)/shard_map/while/body/all_to_all | solution.py:332
  121.0 10.0 %all_to_all.37 = bf16[16,8,576]{2,1,0:T(8,128)(2,1)S(1)} all-to-all(bf16[16,8,576]{2,1,0:T(8,128)(2,1)S(1)} %bitcast.51), channel_id=1, replica_groups=mesh['section'=16,'seq'=16] {'seq'}, dimensions={0} | all-to-all | bytes 294912 | tf_op jit(solution)/shard_map/while/body/all_to_all | solution.py:332
  131.9 12.2 %collective-permute-start.1 = (f32[128,1152]{1,0:T(8,128)S(1)}, f32[128,1152]{1,0:T(8,128)S(1)}, u32[]{:S(2)}, u32[]{:S(2)}) collective-permute-start(f32[128,1152]{1,0:T(8,128)S(1)} %get-tuple-element.88), channel_id=1, source_target_pairs={{0,48},{16,32},{32,80},{48,64},{64,112},{80,96},{96,144},{112,128}... | collective-permute-start | bytes 1769480 | tf_op jit(solution)/shard_map/while/body/ppermute | solution.py:349
  144.1 11.8 %all_to_all.38 = bf16[16,8,1152]{2,1,0:T(8,128)(2,1)S(1)} all-to-all(bf16[16,8,1152]{2,1,0:T(8,128)(2,1)S(1)} %bitcast.54), channel_id=1, replica_groups=mesh['section'=16,'seq'=16] {'seq'}, dimensions={0} | all-to-all | bytes 589824 | tf_op jit(solution)/shard_map/while/body/all_to_all | solution.py:332
  163.8 10.7 %all_to_all.39 = bf16[16,8,576]{2,1,0:T(8,128)(2,1)S(1)} all-to-all(bf16[16,8,576]{2,1,0:T(8,128)(2,1)S(1)} %bitcast.65), channel_id=1, replica_groups=mesh['section'=16,'seq'=16] {'seq'}, dimensions={0} | all-to-all | bytes 294912 | tf_op jit(solution)/shard_map/while/body/all_to_all | solution.py:332
  178.9 11.0 %all_to_all.36 = bf16[16,8,1152]{2,1,0:T(8,128)(2,1)S(1)} all-to-all(bf16[16,8,1152]{2,1,0:T(8,128)(2,1)S(1)} %bitcast.63), channel_id=1, replica_groups=mesh['section'=16,'seq'=16] {'seq'}, dimensions={0} | all-to-all | bytes 589824 | tf_op jit(solution)/shard_map/while/body/all_to_all | solution.py:332
  191.3 10.3 %all_to_all.37 = bf16[16,8,576]{2,1,0:T(8,128)(2,1)S(1)} all-to-all(bf16[16,8,576]{2,1,0:T(8,128)(2,1)S(1)} %bitcast.51), channel_id=1, replica_groups=mesh['section'=16,'seq'=16] {'seq'}, dimensions={0} | all-to-all | bytes 294912 | tf_op jit(solution)/shard_map/while/body/all_to_all | solution.py:332
  208.3 11.7 %all_to_all.38 = bf16[16,8,1152]{2,1,0:T(8,128)(2,1)S(1)} all-to-all(bf16[16,8,1152]{2,1,0:T(8,128)(2,1)S(1)} %bitcast.54), channel_id=1, replica_groups=mesh['section'=16,'seq'=16] {'seq'}, dimensions={0} | all-to-all | bytes 589824 | tf_op jit(solution)/shard_map/while/body/all_to_all | solution.py:332
  227.0 10.5 %all_to_all.39 = bf16[16,8,576]{2,1,0:T(8,128)(2,1)S(1)} all-to-all(bf16[16,8,576]{2,1,0:T(8,128)(2,1)S(1)} %bitcast.65), channel_id=1, replica_groups=mesh['section'=16,'seq'=16] {'seq'}, dimensions={0} | all-to-all | bytes 294912 | tf_op jit(solution)/shard_map/while/body/all_to_all | solution.py:332
  242.0 11.3 %all_to_all.36 = bf16[16,8,1152]{2,1,0:T(8,128)(2,1)S(1)} all-to-all(bf16[16,8,1152]{2,1,0:T(8,128)(2,1)S(1)} %bitcast.63), channel_id=1, replica_groups=mesh['section'=16,'seq'=16] {'seq'}, dimensions={0} | all-to-all | bytes 589824 | tf_op jit(solution)/shard_map/while/body/all_to_all | solution.py:332
  254.6 10.3 %all_to_all.37 = bf16[16,8,576]{2,1,0:T(8,128)(2,1)S(1)} all-to-all(bf16[16,8,576]{2,1,0:T(8,128)(2,1)S(1)} %bitcast.51), channel_id=1, replica_groups=mesh['section'=16,'seq'=16] {'seq'}, dimensions={0} | all-to-all | bytes 294912 | tf_op jit(solution)/shard_map/while/body/all_to_all | solution.py:332
  271.1 11.7 %all_to_all.38 = bf16[16,8,1152]{2,1,0:T(8,128)(2,1)S(1)} all-to-all(bf16[16,8,1152]{2,1,0:T(8,128)(2,1)S(1)} %bitcast.54), channel_id=1, replica_groups=mesh['section'=16,'seq'=16] {'seq'}, dimensions={0} | all-to-all | bytes 589824 | tf_op jit(solution)/shard_map/while/body/all_to_all | solution.py:332
  290.1 10.4 %all_to_all.39 = bf16[16,8,576]{2,1,0:T(8,128)(2,1)S(1)} all-to-all(bf16[16,8,576]{2,1,0:T(8,128)(2,1)S(1)} %bitcast.65), channel_id=1, replica_groups=mesh['section'=16,'seq'=16] {'seq'}, dimensions={0} | all-to-all | bytes 294912 | tf_op jit(solution)/shard_map/while/body/all_to_all | solution.py:332
  304.9 11.3 %all_to_all.36 = bf16[16,8,1152]{2,1,0:T(8,128)(2,1)S(1)} all-to-all(bf16[16,8,1152]{2,1,0:T(8,128)(2,1)S(1)} %bitcast.63), channel_id=1, replica_groups=mesh['section'=16,'seq'=16] {'seq'}, dimensions={0} | all-to-all | bytes 589824 | tf_op jit(solution)/shard_map/while/body/all_to_all | solution.py:332
  317.5 10.3 %all_to_all.37 = bf16[16,8,576]{2,1,0:T(8,128)(2,1)S(1)} all-to-all(bf16[16,8,576]{2,1,0:T(8,128)(2,1)S(1)} %bitcast.51), channel_id=1, replica_groups=mesh['section'=16,'seq'=16] {'seq'}, dimensions={0} | all-to-all | bytes 294912 | tf_op jit(solution)/shard_map/while/body/all_to_all | solution.py:332
  335.8 10.7 %all_to_all.38 = bf16[16,8,1152]{2,1,0:T(8,128)(2,1)S(1)} all-to-all(bf16[16,8,1152]{2,1,0:T(8,128)(2,1)S(1)} %bitcast.54), channel_id=1, replica_groups=mesh['section'=16,'seq'=16] {'seq'}, dimensions={0} | all-to-all | bytes 589824 | tf_op jit(solution)/shard_map/while/body/all_to_all | solution.py:332
  354.4 10.5 %all_to_all.39 = bf16[16,8,576]{2,1,0:T(8,128)(2,1)S(1)} all-to-all(bf16[16,8,576]{2,1,0:T(8,128)(2,1)S(1)} %bitcast.65), channel_id=1, replica_groups=mesh['section'=16,'seq'=16] {'seq'}, dimensions={0} | all-to-all | bytes 294912 | tf_op jit(solution)/shard_map/while/body/all_to_all | solution.py:332
  369.3 11.1 %all_to_all.36 = bf16[16,8,1152]{2,1,0:T(8,128)(2,1)S(1)} all-to-all(bf16[16,8,1152]{2,1,0:T(8,128)(2,1)S(1)} %bitcast.63), channel_id=1, replica_groups=mesh['section'=16,'seq'=16] {'seq'}, dimensions={0} | all-to-all | bytes 589824 | tf_op jit(solution)/shard_map/while/body/all_to_all | solution.py:332
  381.8 10.3 %all_to_all.37 = bf16[16,8,576]{2,1,0:T(8,128)(2,1)S(1)} all-to-all(bf16[16,8,576]{2,1,0:T(8,128)(2,1)S(1)} %bitcast.51), channel_id=1, replica_groups=mesh['section'=16,'seq'=16] {'seq'}, dimensions={0} | all-to-all | bytes 294912 | tf_op jit(solution)/shard_map/while/body/all_to_all | solution.py:332
  400.5 10.7 %all_to_all.38 = bf16[16,8,1152]{2,1,0:T(8,128)(2,1)S(1)} all-to-all(bf16[16,8,1152]{2,1,0:T(8,128)(2,1)S(1)} %bitcast.54), channel_id=1, replica_groups=mesh['section'=16,'seq'=16] {'seq'}, dimensions={0} | all-to-all | bytes 589824 | tf_op jit(solution)/shard_map/while/body/all_to_all | solution.py:332
  417.7 10.7 %all_to_all.39 = bf16[16,8,576]{2,1,0:T(8,128)(2,1)S(1)} all-to-all(bf16[16,8,576]{2,1,0:T(8,128)(2,1)S(1)} %bitcast.65), channel_id=1, replica_groups=mesh['section'=16,'seq'=16] {'seq'}, dimensions={0} | all-to-all | bytes 294912 | tf_op jit(solution)/shard_map/while/body/all_to_all | solution.py:332
  432.8 11.5 %all_to_all.36 = bf16[16,8,1152]{2,1,0:T(8,128)(2,1)S(1)} all-to-all(bf16[16,8,1152]{2,1,0:T(8,128)(2,1)S(1)} %bitcast.63), channel_id=1, replica_groups=mesh['section'=16,'seq'=16] {'seq'}, dimensions={0} | all-to-all | bytes 589824 | tf_op jit(solution)/shard_map/while/body/all_to_all | solution.py:332
  445.7 10.1 %all_to_all.37 = bf16[16,8,576]{2,1,0:T(8,128)(2,1)S(1)} all-to-all(bf16[16,8,576]{2,1,0:T(8,128)(2,1)S(1)} %bitcast.51), channel_id=1, replica_groups=mesh['section'=16,'seq'=16] {'seq'}, dimensions={0} | all-to-all | bytes 294912 | tf_op jit(solution)/shard_map/while/body/all_to_all | solution.py:332
  464.0 10.7 %all_to_all.38 = bf16[16,8,1152]{2,1,0:T(8,128)(2,1)S(1)} all-to-all(bf16[16,8,1152]{2,1,0:T(8,128)(2,1)S(1)} %bitcast.54), channel_id=1, replica_groups=mesh['section'=16,'seq'=16] {'seq'}, dimensions={0} | all-to-all | bytes 589824 | tf_op jit(solution)/shard_map/while/body/all_to_all | solution.py:332
  498.9 12.0 %all_to_all.36 = bf16[16,8,1152]{2,1,0:T(8,128)(2,1)S(1)} all-to-all(bf16[16,8,1152]{2,1,0:T(8,128)(2,1)S(1)} %bitcast.63), channel_id=1, replica_groups=mesh['section'=16,'seq'=16] {'seq'}, dimensions={0} | all-to-all | bytes 589824 | tf_op jit(solution)/shard_map/while/body/all_to_all | solution.py:332
  512.2 10.0 %all_to_all.37 = bf16[16,8,576]{2,1,0:T(8,128)(2,1)S(1)} all-to-all(bf16[16,8,576]{2,1,0:T(8,128)(2,1)S(1)} %bitcast.51), channel_id=1, replica_groups=mesh['section'=16,'seq'=16] {'seq'}, dimensions={0} | all-to-all | bytes 294912 | tf_op jit(solution)/shard_map/while/body/all_to_all | solution.py:332
  526.0 11.0 %all_to_all.38 = bf16[16,8,1152]{2,1,0:T(8,128)(2,1)S(1)} all-to-all(bf16[16,8,1152]{2,1,0:T(8,128)(2,1)S(1)} %bitcast.54), channel_id=1, replica_groups=mesh['section'=16,'seq'=16] {'seq'}, dimensions={0} | all-to-all | bytes 589824 | tf_op jit(solution)/shard_map/while/body/all_to_all | solution.py:332
  581.8 10.3 %all_to_all.40 = bf16[16,8,576]{2,1,0:T(8,128)(2,1)S(1)} all-to-all(bf16[16,8,576]{2,1,0:T(8,128)(2,1)S(1)} %bitcast.58), channel_id=1, replica_groups=mesh['section'=16,'seq'=16] {'seq'}, dimensions={0} | all-to-all | bytes 294912 | tf_op jit(solution)/shard_map/all_to_all | solution.py:332
  596.8 11.2 %all_to_all.41 = bf16[16,8,1152]{2,1,0:T(8,128)(2,1)S(1)} all-to-all(bf16[16,8,1152]{2,1,0:T(8,128)(2,1)S(1)} %bitcast.60), channel_id=1, replica_groups=mesh['section'=16,'seq'=16] {'seq'}, dimensions={0} | all-to-all | bytes 589824 | tf_op jit(solution)/shard_map/all_to_all | solution.py:332
  (258 shorter events, 281.5 us)
Async XLA Ops:
  0.0 9.5 %collective-permute-start.3 = (bf16[1,1152,1728]{1,2,0:T(8,128)(2,1)}, bf16[1,1152,1728]{1,2,0:T(8,128)(2,1)}, u32[]{:S(2)}, u32[]{:S(2)}) collective-permute-start(bf16[1,1152,1728]{1,2,0:T(8,128)(2,1)} %param.9), channel_id=1, source_target_pairs={{0,16},{16,0},{32,48},{48,32},{64,80},{80,64},{96,112},{112,96},{1... | collective-permute-start | bytes 11943944 | tf_op jit(solution)/shard_map/ppermute | solution.py:272
  0.7 8.8 %collective-permute-start.4 = (bf16[1,576,1152]{2,1,0:T(8,128)(2,1)}, bf16[1,576,1152]{2,1,0:T(8,128)(2,1)S(1)}, u32[]{:S(2)}, u32[]{:S(2)}) collective-permute-start(bf16[1,576,1152]{2,1,0:T(8,128)(2,1)} %param.10), channel_id=1, source_target_pairs={{0,16},{16,0},{32,48},{48,32},{64,80},{80,64},{96,112},{112,96},{1... | collective-permute-start | bytes 3981320 | tf_op jit(solution)/shard_map/ppermute | solution.py:272
  1.6 7.9 %collective-permute-start.2 = (f32[4,6,1152]{2,1,0:T(8,128)S(1)}, f32[4,6,1152]{2,1,0:T(8,128)S(1)}, u32[]{:S(2)}, u32[]{:S(2)}) collective-permute-start(f32[4,6,1152]{2,1,0:T(8,128)S(1)} %bitcast.72), channel_id=1, source_target_pairs={{0,16},{16,0},{32,48},{48,32},{64,80},{80,64},{96,112},{112,96},{1... | collective-permute-start | bytes 331784 | tf_op jit(solution)/shard_map/ppermute | solution.py:272
  9.5 22.5 %collective-permute-start.5 = (bf16[1,1152,1728]{1,2,0:T(8,128)(2,1)}, bf16[1,1152,1728]{1,2,0:T(8,128)(2,1)}, u32[]{:S(2)}, u32[]{:S(2)}) collective-permute-start(bf16[1,1152,1728]{1,2,0:T(8,128)(2,1)} %param.11), channel_id=1, source_target_pairs={{0,16},{16,0},{32,48},{48,32},{64,80},{80,64},{96,112},{112,96},{1... | collective-permute-start | bytes 11943944 | tf_op jit(solution)/shard_map/ppermute | solution.py:272
  9.9 20.4 %collective-permute-start.6 = (bf16[576,1152]{1,0:T(8,128)(2,1)}, bf16[576,1152]{1,0:T(8,128)(2,1)}, u32[]{:S(2)}, u32[]{:S(2)}) collective-permute-start(bf16[576,1152]{1,0:T(8,128)(2,1)} %bitcast.69), channel_id=1, source_target_pairs={{16,48},{48,80},{80,112},{112,144},{144,176},{176,208},{208,240},{... | collective-permute-start | bytes 3981320 | tf_op jit(solution)/shard_map/ppermute | solution.py:360
  13.6 18.4 %collective-permute-start.7 = (f32[4,6,1152]{2,1,0:T(8,128)}, f32[4,6,1152]{2,1,0:T(8,128)}, u32[]{:S(2)}, u32[]{:S(2)}) collective-permute-start(f32[4,6,1152]{2,1,0:T(8,128)} %get-tuple-element.219.following.mod), channel_id=1, source_target_pairs={{0,32},{16,48},{32,64},{48,80},{64,96},{80,112},{96,128},{112,144}... | collective-permute-start | bytes 331784 | tf_op jit(solution)/shard_map/ppermute | solution.py:361
  14.1 20.3 %collective-permute-start.8 = (bf16[1,576,1152]{2,1,0:T(8,128)(2,1)}, bf16[1,576,1152]{2,1,0:T(8,128)(2,1)}, u32[]{:S(2)}, u32[]{:S(2)}) collective-permute-start(bf16[1,576,1152]{2,1,0:T(8,128)(2,1)} %param.12), channel_id=1, source_target_pairs={{0,16},{16,0},{32,48},{48,32},{64,80},{80,64},{96,112},{112,96},{1... | collective-permute-start | bytes 3981320 | tf_op jit(solution)/shard_map/ppermute | solution.py:272
  31.9 10.7 %collective-permute-start.9 = (bf16[576,1152]{1,0:T(8,128)(2,1)}, bf16[576,1152]{1,0:T(8,128)(2,1)}, u32[]{:S(2)}, u32[]{:S(2)}) collective-permute-start(bf16[576,1152]{1,0:T(8,128)(2,1)} %collective-permute-done.6), channel_id=1, source_target_pairs={{16,0},{48,32},{80,64},{112,96},{144,128},{176,160},{208,192},{240... | collective-permute-start | bytes 3981320 | tf_op jit(solution)/shard_map/ppermute | solution.py:363
  48.1 26.8 %copy-start.10 = (bf16[576,1152]{1,0:T(8,128)(2,1)S(1)}, bf16[576,1152]{1,0:T(8,128)(2,1)}, u32[]{:S(2)}) copy-start(bf16[576,1152]{1,0:T(8,128)(2,1)} %get-tuple-element.254.tout) | copy-start | bytes 3981316 | tf_op jit(solution)/shard_map/while
  49.1 25.7 %copy-start.9 = (bf16[576,1152]{1,0:T(8,128)(2,1)S(1)}, bf16[576,1152]{1,0:T(8,128)(2,1)}, u32[]{:S(2)}) copy-start(bf16[576,1152]{1,0:T(8,128)(2,1)} %get-tuple-element.256.out) | copy-start | bytes 3981316 | tf_op jit(solution)/shard_map/while
  75.8 28.4 %collective-permute-start.1 = (f32[128,1152]{1,0:T(8,128)S(1)}, f32[128,1152]{1,0:T(8,128)S(1)}, u32[]{:S(2)}, u32[]{:S(2)}) collective-permute-start(f32[128,1152]{1,0:T(8,128)S(1)} %get-tuple-element.88), channel_id=1, source_target_pairs={{0,48},{16,32},{32,80},{48,64},{64,112},{80,96},{96,144},{112,128}... | collective-permute-start | bytes 1769480 | tf_op jit(solution)/shard_map/while/body/ppermute | solution.py:349
  88.6 5.6 collective-permute-start
  131.9 42.5 %collective-permute-start.1 = (f32[128,1152]{1,0:T(8,128)S(1)}, f32[128,1152]{1,0:T(8,128)S(1)}, u32[]{:S(2)}, u32[]{:S(2)}) collective-permute-start(f32[128,1152]{1,0:T(8,128)S(1)} %get-tuple-element.88), channel_id=1, source_target_pairs={{0,48},{16,32},{32,80},{48,64},{64,112},{80,96},{96,144},{112,128}... | collective-permute-start | bytes 1769480 | tf_op jit(solution)/shard_map/while/body/ppermute | solution.py:349
  157.4 6.4 %collective-permute-start = (bf16[128,576]{1,0:T(8,128)(2,1)S(1)}, bf16[128,576]{1,0:T(8,128)(2,1)S(1)}, u32[]{:S(2)}, u32[]{:S(2)}) collective-permute-start(bf16[128,576]{1,0:T(8,128)(2,1)S(1)} %temporal.5), channel_id=1, source_target_pairs={{0,48},{16,32},{32,80},{48,64},{64,112},{80,96},{96,144},{112,128}... | collective-permute-start | bytes 442376 | tf_op jit(solution)/shard_map/while/body/ppermute | solution.py:350
  202.5 35.0 %collective-permute-start.1 = (f32[128,1152]{1,0:T(8,128)S(1)}, f32[128,1152]{1,0:T(8,128)S(1)}, u32[]{:S(2)}, u32[]{:S(2)}) collective-permute-start(f32[128,1152]{1,0:T(8,128)S(1)} %get-tuple-element.88), channel_id=1, source_target_pairs={{0,48},{16,32},{32,80},{48,64},{64,112},{80,96},{96,144},{112,128}... | collective-permute-start | bytes 1769480 | tf_op jit(solution)/shard_map/while/body/ppermute | solution.py:349
  221.4 5.6 collective-permute-start
  265.8 34.6 %collective-permute-start.1 = (f32[128,1152]{1,0:T(8,128)S(1)}, f32[128,1152]{1,0:T(8,128)S(1)}, u32[]{:S(2)}, u32[]{:S(2)}) collective-permute-start(f32[128,1152]{1,0:T(8,128)S(1)} %get-tuple-element.88), channel_id=1, source_target_pairs={{0,48},{16,32},{32,80},{48,64},{64,112},{80,96},{96,144},{112,128}... | collective-permute-start | bytes 1769480 | tf_op jit(solution)/shard_map/while/body/ppermute | solution.py:349
  284.3 5.8 collective-permute-start
  328.8 36.1 %collective-permute-start.1 = (f32[128,1152]{1,0:T(8,128)S(1)}, f32[128,1152]{1,0:T(8,128)S(1)}, u32[]{:S(2)}, u32[]{:S(2)}) collective-permute-start(f32[128,1152]{1,0:T(8,128)S(1)} %get-tuple-element.88), channel_id=1, source_target_pairs={{0,48},{16,32},{32,80},{48,64},{64,112},{80,96},{96,144},{112,128}... | collective-permute-start | bytes 1769480 | tf_op jit(solution)/shard_map/while/body/ppermute | solution.py:349
  347.9 6.5 %collective-permute-start = (bf16[128,576]{1,0:T(8,128)(2,1)S(1)}, bf16[128,576]{1,0:T(8,128)(2,1)S(1)}, u32[]{:S(2)}, u32[]{:S(2)}) collective-permute-start(bf16[128,576]{1,0:T(8,128)(2,1)S(1)} %temporal.5), channel_id=1, source_target_pairs={{0,48},{16,32},{32,80},{48,64},{64,112},{80,96},{96,144},{112,128}... | collective-permute-start | bytes 442376 | tf_op jit(solution)/shard_map/while/body/ppermute | solution.py:350
  393.0 35.3 %collective-permute-start.1 = (f32[128,1152]{1,0:T(8,128)S(1)}, f32[128,1152]{1,0:T(8,128)S(1)}, u32[]{:S(2)}, u32[]{:S(2)}) collective-permute-start(f32[128,1152]{1,0:T(8,128)S(1)} %get-tuple-element.88), channel_id=1, source_target_pairs={{0,48},{16,32},{32,80},{48,64},{64,112},{80,96},{96,144},{112,128}... | collective-permute-start | bytes 1769480 | tf_op jit(solution)/shard_map/while/body/ppermute | solution.py:349
  412.6 5.1 collective-permute-start
  456.8 35.0 %collective-permute-start.1 = (f32[128,1152]{1,0:T(8,128)S(1)}, f32[128,1152]{1,0:T(8,128)S(1)}, u32[]{:S(2)}, u32[]{:S(2)}) collective-permute-start(f32[128,1152]{1,0:T(8,128)S(1)} %get-tuple-element.88), channel_id=1, source_target_pairs={{0,48},{16,32},{32,80},{48,64},{64,112},{80,96},{96,144},{112,128}... | collective-permute-start | bytes 1769480 | tf_op jit(solution)/shard_map/while/body/ppermute | solution.py:349
  476.1 5.7 collective-permute-start
  497.8 24.4 %copy-start.10 = (bf16[576,1152]{1,0:T(8,128)(2,1)S(1)}, bf16[576,1152]{1,0:T(8,128)(2,1)}, u32[]{:S(2)}) copy-start(bf16[576,1152]{1,0:T(8,128)(2,1)} %get-tuple-element.254.tout) | copy-start | bytes 3981316 | tf_op jit(solution)/shard_map/while
  525.9 32.7 %collective-permute-start.1 = (f32[128,1152]{1,0:T(8,128)S(1)}, f32[128,1152]{1,0:T(8,128)S(1)}, u32[]{:S(2)}, u32[]{:S(2)}) collective-permute-start(f32[128,1152]{1,0:T(8,128)S(1)} %get-tuple-element.88), channel_id=1, source_target_pairs={{0,48},{16,32},{32,80},{48,64},{64,112},{80,96},{96,144},{112,128}... | collective-permute-start | bytes 1769480 | tf_op jit(solution)/shard_map/while/body/ppermute | solution.py:349
  538.4 10.2 %collective-permute-start = (bf16[128,576]{1,0:T(8,128)(2,1)S(1)}, bf16[128,576]{1,0:T(8,128)(2,1)S(1)}, u32[]{:S(2)}, u32[]{:S(2)}) collective-permute-start(bf16[128,576]{1,0:T(8,128)(2,1)S(1)} %temporal.5), channel_id=1, source_target_pairs={{0,48},{16,32},{32,80},{48,64},{64,112},{80,96},{96,144},{112,128}... | collective-permute-start | bytes 442376 | tf_op jit(solution)/shard_map/while/body/ppermute | solution.py:350
  566.0 26.2 %copy-start.16 = (f32[128,1152]{1,0:T(8,128)S(1)}, f32[128,1152]{1,0:T(8,128)}, u32[]{:S(2)}) copy-start(f32[128,1152]{1,0:T(8,128)} %copy-done.15) | copy-start | bytes 1769476
  566.0 12.2 %all-to-all-start.4 = ((bf16[16,8,1152]{2,1,0:T(8,128)(2,1)}), bf16[16,8,1152]{2,1,0:T(8,128)(2,1)S(1)}, u32[]{:S(2)}, u32[]{:S(2)}) async-start(bf16[16,8,1152]{2,1,0:T(8,128)(2,1)} %bitcast.64), calls=%async_computation.4 | async-start | bytes 589824 | tf_op jit(solution)/shard_map/all_to_all | solution.py:332
  569.7 43.9 %collective-permute-start.10 = (bf16[2,128,1152]{2,1,0:T(8,128)(2,1)}, bf16[2,128,1152]{2,1,0:T(8,128)(2,1)S(1)}, u32[]{:S(2)}, u32[]{:S(2)}) collective-permute-start(bf16[2,128,1152]{2,1,0:T(8,128)(2,1)} %copy-done.17), channel_id=1, source_target_pairs={{48,0},{32,16},{80,32},{64,48},{112,64},{96,80},{144,96},{128,112}... | collective-permute-start | bytes 1769480 | tf_op jit(solution)/shard_map/ppermute | solution.py:370
  610.1 10.3 %all-to-all-start.7 = ((bf16[16,8,576]{2,1,0:T(8,128)(2,1)}), bf16[16,8,576]{2,1,0:T(8,128)(2,1)S(1)}, u32[]{:S(2)}, u32[]{:S(2)}) async-start(bf16[16,8,576]{2,1,0:T(8,128)(2,1)} %bitcast.33), calls=%async_computation.7 | async-start | bytes 327680 | tf_op jit(solution)/shard_map/all_to_all | solution.py:332
  621.9 5.4 collective-permute-start.11
  (59 other events, 876.6 us)

commit v7 on v6

--- a/solution.py
+++ b/solution.py
@@ -156,10 +156,11 @@
     g[...] = norm_modulate(middle, factors[3:4], factors[4:5])
 
 
-def tick_kernel(flags, g_in, following, g):
+def tick_kernel(flags, g_in, following, after, g):
     following[0] = flags[0]
     following[1] = flags[1]
     following[2] = flags[2] + 1
+    after[0] = flags[2] + 1
 
 
 def first_kernel(per_core, flags, frames, mod, qkv, out, y, g):
@@ -301,9 +302,9 @@
     x_s, y_s = shape((tokens, model), BF16), shape((tokens, model), F32)
     kept_s = shape((per_core, tokens, model), BF16)
     hold = [pltpu.VMEM((tokens, model), BF16), pltpu.SemaphoreType.DMA]
-    at_s = shape((3,), jnp.int32)
+    one_s, at_s = shape((1,), jnp.int32), shape((3,), jnp.int32)
     tick = call(
-        tick_kernel, "tick", [SMEM, ANY], [at_s, x_s], [SMEM, ANY], [], {1: 1},
+        tick_kernel, "tick", [SMEM, ANY], [at_s, one_s, x_s], [SMEM, SMEM, ANY], [], {1: 2},
         flops=2 * 10**9,
     )
     first = call(
@@ -343,15 +344,15 @@
     back = [(j, i) for i, j in onward]
 
     def advance(carried):
-        flags, even, odd, y, g = carried
-        following, g = tick(flags, g)
+        _, flags, even, odd, y, g = carried
+        following, after, g = tick(flags, g)
         even, y, g = sections_of(1, following, even, y, g)
         y = lax.ppermute(y, "section", onward)
         mixed = lax.ppermute(temporal(exchange(g), tqkv_o), "section", onward)
         y, g, odd = cross(
             following, exchange(mixed), y, mod_p, mod_e, tout_p, sqkv_e, sout_e, source, odd
         )
-        return following, even, odd, y, g
+        return after, following, even, odd, y, g
 
     kept = jnp.zeros(kept_s.shape, BF16)
     last = stages + per_core - 2
@@ -364,8 +365,9 @@
     tqkv_e, tqkv_o, tout_e, tout_o = prepared(tqkv, tout, tqkv2, tout2)
     tout_p2, tout_o = lax.optimization_barrier((tout_p2, tout_o))
     tout_p = jnp.where(core == 0, tout_p2, tout_p)
-    flags, even, odd, y, g = lax.while_loop(
-        lambda carried: carried[0][2] < last, advance, (flags, kept, kept, y, g)
+    start = jnp.zeros((1,), jnp.int32)
+    _, flags, even, odd, y, g = lax.while_loop(
+        lambda carried: carried[0][0] < last, advance, (start, flags, kept, kept, y, g)
     )
     odd = lax.ppermute(odd, "section", back)
     even, y, g = sections_of(0, flags, even, y, g)

time: 631 us -> 616 us (0.976)
  local copies, waits for them, and re-layouts: 19.2 us -> 4.22 us
    slice x9 -> x0, local copies, waits for them, and re-layouts: 10.4 us -> none  [on_device(): carried[0][2] < last]
  transfers between devices with their start and end apart: 28 -> 28, of which waited for: 14 -> 14; matrix products, arithmetic and copies ran while one was open for 0% -> 1% of each run, Pallas kernels for 6% -> 7%
where the time goes in v7:
time: 616 us; the launch traced here: 614 us
  blocking collectives  368 us (60%)
  Pallas kernels  84.6 us (14%)
  starting transfers between devices  79.8 us (13%)
  waiting for transfers between devices  65.6 us (11%)
    all_to_all x34, blocking collectives, exchange(): lax.all_to_all(a.reshape(ranks, share, a.shape[1]), 'seq', 0, 0, tiled=True)  368 us
    ppermute x8, starting transfers between devices, advance(): y = lax.ppermute(y, 'section', onward)  46.4 us
    ppermute x8, waiting for transfers between devices, advance(): mixed = lax.ppermute(temporal(exchange(g), tqkv_o), 'section', onward)  34.7 us
    pallas_call x2, Pallas kernels, prepared(): prepare(core_id, jnp.swapaxes(qkv[0], 0, 1), jnp.swapaxes(qkv2[0], 0, 1),...  15.7 us
    pallas_call x9, Pallas kernels, sections_of(): joint(late)  14.8 us
    ppermute x8, starting transfers between devices, advance(): mixed = lax.ppermute(temporal(exchange(g), tqkv_o), 'section', onward)  14.6 us
    pallas_call x9, Pallas kernels, sections_of(): mixed = temporal(exchange(g), tqkv_e)  14.5 us
    all_to_all x2, waiting for transfers between devices, exchange(): lax.all_to_all(a.reshape(ranks, share, a.shape[1]), 'seq', 0, 0, tiled=True)  14.3 us
  transfers between devices with their start and end apart: 28, of which 14 were waited for; matrix products, arithmetic and copies ran while one was open for 1% of the time, Pallas kernels for 7%

profile of v7, /device:TPU:225, one launch (start us, length us, event | category | flops | bytes accessed | tf_op | source)
XLA Modules:
  0.0 614.2 jit_solution(15007184408161377736)
XLA Ops:
  45.5 503.3 %while.17 = (s32[1]{0:T(128)}, s32[3]{0:T(128)S(1)}, bf16[2,128,1152]{2,1,0:T(8,128)(2,1)S(1)}, bf16[2,128,1152]{2,1,0:T(8,128)(2,1)S(1)}, f32[128,1152]{1,0:T(8...) while((s32[1]{0:T(128)}, s32[3]{0:T(128)S(1)}, ...), condition=%region_1.2_spmd, body=%region_0.1_spmd | while | flops 2000000000 | bytes 60393000 | solution.py:369
  46.7 14.3 %all_to_all.36 = bf16[16,8,1152]{2,1,0:T(8,128)(2,1)S(1)} all-to-all(bf16[16,8,1152]{2,1,0:T(8,128)(2,1)S(1)} %bitcast.63), channel_id=1, replica_groups=mesh['section'=16,'seq'=16] {'seq'}, dimensions={0} | all-to-all | bytes 589824 | tf_op jit(solution)/shard_map/while/body/all_to_all | solution.py:333
  74.0 10.7 %all_to_all.38 = bf16[16,8,1152]{2,1,0:T(8,128)(2,1)S(1)} all-to-all(bf16[16,8,1152]{2,1,0:T(8,128)(2,1)S(1)} %bitcast.54), channel_id=1, replica_groups=mesh['section'=16,'seq'=16] {'seq'}, dimensions={0} | all-to-all | bytes 589824 | tf_op jit(solution)/shard_map/while/body/all_to_all | solution.py:333
  104.6 11.0 %all_to_all.36 = bf16[16,8,1152]{2,1,0:T(8,128)(2,1)S(1)} all-to-all(bf16[16,8,1152]{2,1,0:T(8,128)(2,1)S(1)} %bitcast.63), channel_id=1, replica_groups=mesh['section'=16,'seq'=16] {'seq'}, dimensions={0} | all-to-all | bytes 589824 | tf_op jit(solution)/shard_map/while/body/all_to_all | solution.py:333
  127.9 12.2 %collective-permute-start.1 = (f32[128,1152]{1,0:T(8,128)S(1)}, f32[128,1152]{1,0:T(8,128)S(1)}, u32[]{:S(2)}, u32[]{:S(2)}) collective-permute-start(f32[128,1152]{1,0:T(8,128)S(1)} %get-tuple-element.93), channel_id=1, source_target_pairs={{0,48},{16,32},{32,80},{48,64},{64,112},{80,96},{96,144},{112,128}... | collective-permute-start | bytes 1769480 | tf_op jit(solution)/shard_map/while/body/ppermute | solution.py:350
  140.1 11.5 %all_to_all.38 = bf16[16,8,1152]{2,1,0:T(8,128)(2,1)S(1)} all-to-all(bf16[16,8,1152]{2,1,0:T(8,128)(2,1)S(1)} %bitcast.54), channel_id=1, replica_groups=mesh['section'=16,'seq'=16] {'seq'}, dimensions={0} | all-to-all | bytes 589824 | tf_op jit(solution)/shard_map/while/body/all_to_all | solution.py:333
  159.2 11.1 %all_to_all.39 = bf16[16,8,576]{2,1,0:T(8,128)(2,1)S(1)} all-to-all(bf16[16,8,576]{2,1,0:T(8,128)(2,1)S(1)} %bitcast.65), channel_id=1, replica_groups=mesh['section'=16,'seq'=16] {'seq'}, dimensions={0} | all-to-all | bytes 294912 | tf_op jit(solution)/shard_map/while/body/all_to_all | solution.py:333
  173.1 11.1 %all_to_all.36 = bf16[16,8,1152]{2,1,0:T(8,128)(2,1)S(1)} all-to-all(bf16[16,8,1152]{2,1,0:T(8,128)(2,1)S(1)} %bitcast.63), channel_id=1, replica_groups=mesh['section'=16,'seq'=16] {'seq'}, dimensions={0} | all-to-all | bytes 589824 | tf_op jit(solution)/shard_map/while/body/all_to_all | solution.py:333
  185.5 10.3 %all_to_all.37 = bf16[16,8,576]{2,1,0:T(8,128)(2,1)S(1)} all-to-all(bf16[16,8,576]{2,1,0:T(8,128)(2,1)S(1)} %bitcast.51), channel_id=1, replica_groups=mesh['section'=16,'seq'=16] {'seq'}, dimensions={0} | all-to-all | bytes 294912 | tf_op jit(solution)/shard_map/while/body/all_to_all | solution.py:333
  202.6 11.6 %all_to_all.38 = bf16[16,8,1152]{2,1,0:T(8,128)(2,1)S(1)} all-to-all(bf16[16,8,1152]{2,1,0:T(8,128)(2,1)S(1)} %bitcast.54), channel_id=1, replica_groups=mesh['section'=16,'seq'=16] {'seq'}, dimensions={0} | all-to-all | bytes 589824 | tf_op jit(solution)/shard_map/while/body/all_to_all | solution.py:333
  221.1 10.5 %all_to_all.39 = bf16[16,8,576]{2,1,0:T(8,128)(2,1)S(1)} all-to-all(bf16[16,8,576]{2,1,0:T(8,128)(2,1)S(1)} %bitcast.65), channel_id=1, replica_groups=mesh['section'=16,'seq'=16] {'seq'}, dimensions={0} | all-to-all | bytes 294912 | tf_op jit(solution)/shard_map/while/body/all_to_all | solution.py:333
  234.5 11.3 %all_to_all.36 = bf16[16,8,1152]{2,1,0:T(8,128)(2,1)S(1)} all-to-all(bf16[16,8,1152]{2,1,0:T(8,128)(2,1)S(1)} %bitcast.63), channel_id=1, replica_groups=mesh['section'=16,'seq'=16] {'seq'}, dimensions={0} | all-to-all | bytes 589824 | tf_op jit(solution)/shard_map/while/body/all_to_all | solution.py:333
  247.1 10.2 %all_to_all.37 = bf16[16,8,576]{2,1,0:T(8,128)(2,1)S(1)} all-to-all(bf16[16,8,576]{2,1,0:T(8,128)(2,1)S(1)} %bitcast.51), channel_id=1, replica_groups=mesh['section'=16,'seq'=16] {'seq'}, dimensions={0} | all-to-all | bytes 294912 | tf_op jit(solution)/shard_map/while/body/all_to_all | solution.py:333
  263.8 11.4 %all_to_all.38 = bf16[16,8,1152]{2,1,0:T(8,128)(2,1)S(1)} all-to-all(bf16[16,8,1152]{2,1,0:T(8,128)(2,1)S(1)} %bitcast.54), channel_id=1, replica_groups=mesh['section'=16,'seq'=16] {'seq'}, dimensions={0} | all-to-all | bytes 589824 | tf_op jit(solution)/shard_map/while/body/all_to_all | solution.py:333
  282.4 10.5 %all_to_all.39 = bf16[16,8,576]{2,1,0:T(8,128)(2,1)S(1)} all-to-all(bf16[16,8,576]{2,1,0:T(8,128)(2,1)S(1)} %bitcast.65), channel_id=1, replica_groups=mesh['section'=16,'seq'=16] {'seq'}, dimensions={0} | all-to-all | bytes 294912 | tf_op jit(solution)/shard_map/while/body/all_to_all | solution.py:333
  295.8 11.1 %all_to_all.36 = bf16[16,8,1152]{2,1,0:T(8,128)(2,1)S(1)} all-to-all(bf16[16,8,1152]{2,1,0:T(8,128)(2,1)S(1)} %bitcast.63), channel_id=1, replica_groups=mesh['section'=16,'seq'=16] {'seq'}, dimensions={0} | all-to-all | bytes 589824 | tf_op jit(solution)/shard_map/while/body/all_to_all | solution.py:333
  308.2 10.3 %all_to_all.37 = bf16[16,8,576]{2,1,0:T(8,128)(2,1)S(1)} all-to-all(bf16[16,8,576]{2,1,0:T(8,128)(2,1)S(1)} %bitcast.51), channel_id=1, replica_groups=mesh['section'=16,'seq'=16] {'seq'}, dimensions={0} | all-to-all | bytes 294912 | tf_op jit(solution)/shard_map/while/body/all_to_all | solution.py:333
  326.9 10.7 %all_to_all.38 = bf16[16,8,1152]{2,1,0:T(8,128)(2,1)S(1)} all-to-all(bf16[16,8,1152]{2,1,0:T(8,128)(2,1)S(1)} %bitcast.54), channel_id=1, replica_groups=mesh['section'=16,'seq'=16] {'seq'}, dimensions={0} | all-to-all | bytes 589824 | tf_op jit(solution)/shard_map/while/body/all_to_all | solution.py:333
  345.5 10.5 %all_to_all.39 = bf16[16,8,576]{2,1,0:T(8,128)(2,1)S(1)} all-to-all(bf16[16,8,576]{2,1,0:T(8,128)(2,1)S(1)} %bitcast.65), channel_id=1, replica_groups=mesh['section'=16,'seq'=16] {'seq'}, dimensions={0} | all-to-all | bytes 294912 | tf_op jit(solution)/shard_map/while/body/all_to_all | solution.py:333
  358.9 11.1 %all_to_all.36 = bf16[16,8,1152]{2,1,0:T(8,128)(2,1)S(1)} all-to-all(bf16[16,8,1152]{2,1,0:T(8,128)(2,1)S(1)} %bitcast.63), channel_id=1, replica_groups=mesh['section'=16,'seq'=16] {'seq'}, dimensions={0} | all-to-all | bytes 589824 | tf_op jit(solution)/shard_map/while/body/all_to_all | solution.py:333
  371.3 10.3 %all_to_all.37 = bf16[16,8,576]{2,1,0:T(8,128)(2,1)S(1)} all-to-all(bf16[16,8,576]{2,1,0:T(8,128)(2,1)S(1)} %bitcast.51), channel_id=1, replica_groups=mesh['section'=16,'seq'=16] {'seq'}, dimensions={0} | all-to-all | bytes 294912 | tf_op jit(solution)/shard_map/while/body/all_to_all | solution.py:333
  390.0 10.7 %all_to_all.38 = bf16[16,8,1152]{2,1,0:T(8,128)(2,1)S(1)} all-to-all(bf16[16,8,1152]{2,1,0:T(8,128)(2,1)S(1)} %bitcast.54), channel_id=1, replica_groups=mesh['section'=16,'seq'=16] {'seq'}, dimensions={0} | all-to-all | bytes 589824 | tf_op jit(solution)/shard_map/while/body/all_to_all | solution.py:333
  407.2 10.7 %all_to_all.39 = bf16[16,8,576]{2,1,0:T(8,128)(2,1)S(1)} all-to-all(bf16[16,8,576]{2,1,0:T(8,128)(2,1)S(1)} %bitcast.65), channel_id=1, replica_groups=mesh['section'=16,'seq'=16] {'seq'}, dimensions={0} | all-to-all | bytes 294912 | tf_op jit(solution)/shard_map/while/body/all_to_all | solution.py:333
  420.7 11.5 %all_to_all.36 = bf16[16,8,1152]{2,1,0:T(8,128)(2,1)S(1)} all-to-all(bf16[16,8,1152]{2,1,0:T(8,128)(2,1)S(1)} %bitcast.63), channel_id=1, replica_groups=mesh['section'=16,'seq'=16] {'seq'}, dimensions={0} | all-to-all | bytes 589824 | tf_op jit(solution)/shard_map/while/body/all_to_all | solution.py:333
  433.6 10.1 %all_to_all.37 = bf16[16,8,576]{2,1,0:T(8,128)(2,1)S(1)} all-to-all(bf16[16,8,576]{2,1,0:T(8,128)(2,1)S(1)} %bitcast.51), channel_id=1, replica_groups=mesh['section'=16,'seq'=16] {'seq'}, dimensions={0} | all-to-all | bytes 294912 | tf_op jit(solution)/shard_map/while/body/all_to_all | solution.py:333
  451.9 10.7 %all_to_all.38 = bf16[16,8,1152]{2,1,0:T(8,128)(2,1)S(1)} all-to-all(bf16[16,8,1152]{2,1,0:T(8,128)(2,1)S(1)} %bitcast.54), channel_id=1, replica_groups=mesh['section'=16,'seq'=16] {'seq'}, dimensions={0} | all-to-all | bytes 589824 | tf_op jit(solution)/shard_map/while/body/all_to_all | solution.py:333
  469.2 10.0 %all_to_all.39 = bf16[16,8,576]{2,1,0:T(8,128)(2,1)S(1)} all-to-all(bf16[16,8,576]{2,1,0:T(8,128)(2,1)S(1)} %bitcast.65), channel_id=1, replica_groups=mesh['section'=16,'seq'=16] {'seq'}, dimensions={0} | all-to-all | bytes 294912 | tf_op jit(solution)/shard_map/while/body/all_to_all | solution.py:333
  484.7 13.0 %all_to_all.36 = bf16[16,8,1152]{2,1,0:T(8,128)(2,1)S(1)} all-to-all(bf16[16,8,1152]{2,1,0:T(8,128)(2,1)S(1)} %bitcast.63), channel_id=1, replica_groups=mesh['section'=16,'seq'=16] {'seq'}, dimensions={0} | all-to-all | bytes 589824 | tf_op jit(solution)/shard_map/while/body/all_to_all | solution.py:333
  512.6 10.9 %all_to_all.38 = bf16[16,8,1152]{2,1,0:T(8,128)(2,1)S(1)} all-to-all(bf16[16,8,1152]{2,1,0:T(8,128)(2,1)S(1)} %bitcast.54), channel_id=1, replica_groups=mesh['section'=16,'seq'=16] {'seq'}, dimensions={0} | all-to-all | bytes 589824 | tf_op jit(solution)/shard_map/while/body/all_to_all | solution.py:333
  534.5 10.1 %all_to_all.39 = bf16[16,8,576]{2,1,0:T(8,128)(2,1)S(1)} all-to-all(bf16[16,8,576]{2,1,0:T(8,128)(2,1)S(1)} %bitcast.65), channel_id=1, replica_groups=mesh['section'=16,'seq'=16] {'seq'}, dimensions={0} | all-to-all | bytes 294912 | tf_op jit(solution)/shard_map/while/body/all_to_all | solution.py:333
  566.5 10.9 %all_to_all.40 = bf16[16,8,576]{2,1,0:T(8,128)(2,1)S(1)} all-to-all(bf16[16,8,576]{2,1,0:T(8,128)(2,1)S(1)} %bitcast.58), channel_id=1, replica_groups=mesh['section'=16,'seq'=16] {'seq'}, dimensions={0} | all-to-all | bytes 294912 | tf_op jit(solution)/shard_map/all_to_all | solution.py:333
  582.0 10.8 %all_to_all.41 = bf16[16,8,1152]{2,1,0:T(8,128)(2,1)S(1)} all-to-all(bf16[16,8,1152]{2,1,0:T(8,128)(2,1)S(1)} %bitcast.60), channel_id=1, replica_groups=mesh['section'=16,'seq'=16] {'seq'}, dimensions={0} | all-to-all | bytes 589824 | tf_op jit(solution)/shard_map/all_to_all | solution.py:333
  (255 shorter events, 266.8 us)
Async XLA Ops:
  0.0 9.5 %collective-permute-start.3 = (bf16[1,1152,1728]{1,2,0:T(8,128)(2,1)}, bf16[1,1152,1728]{1,2,0:T(8,128)(2,1)}, u32[]{:S(2)}, u32[]{:S(2)}) collective-permute-start(bf16[1,1152,1728]{1,2,0:T(8,128)(2,1)} %param.9), channel_id=1, source_target_pairs={{0,16},{16,0},{32,48},{48,32},{64,80},{80,64},{96,112},{112,96},{1... | collective-permute-start | bytes 11943944 | tf_op jit(solution)/shard_map/ppermute | solution.py:273
  0.7 8.8 %collective-permute-start.4 = (bf16[1,576,1152]{2,1,0:T(8,128)(2,1)}, bf16[1,576,1152]{2,1,0:T(8,128)(2,1)S(1)}, u32[]{:S(2)}, u32[]{:S(2)}) collective-permute-start(bf16[1,576,1152]{2,1,0:T(8,128)(2,1)} %param.10), channel_id=1, source_target_pairs={{0,16},{16,0},{32,48},{48,32},{64,80},{80,64},{96,112},{112,96},{1... | collective-permute-start | bytes 3981320 | tf_op jit(solution)/shard_map/ppermute | solution.py:273
  1.6 7.9 %collective-permute-start.2 = (f32[4,6,1152]{2,1,0:T(8,128)S(1)}, f32[4,6,1152]{2,1,0:T(8,128)S(1)}, u32[]{:S(2)}, u32[]{:S(2)}) collective-permute-start(f32[4,6,1152]{2,1,0:T(8,128)S(1)} %bitcast.72), channel_id=1, source_target_pairs={{0,16},{16,0},{32,48},{48,32},{64,80},{80,64},{96,112},{112,96},{1... | collective-permute-start | bytes 331784 | tf_op jit(solution)/shard_map/ppermute | solution.py:273
  9.5 22.5 %collective-permute-start.5 = (bf16[1,1152,1728]{1,2,0:T(8,128)(2,1)}, bf16[1,1152,1728]{1,2,0:T(8,128)(2,1)}, u32[]{:S(2)}, u32[]{:S(2)}) collective-permute-start(bf16[1,1152,1728]{1,2,0:T(8,128)(2,1)} %param.11), channel_id=1, source_target_pairs={{0,16},{16,0},{32,48},{48,32},{64,80},{80,64},{96,112},{112,96},{1... | collective-permute-start | bytes 11943944 | tf_op jit(solution)/shard_map/ppermute | solution.py:273
  9.9 20.4 %collective-permute-start.6 = (bf16[576,1152]{1,0:T(8,128)(2,1)}, bf16[576,1152]{1,0:T(8,128)(2,1)}, u32[]{:S(2)}, u32[]{:S(2)}) collective-permute-start(bf16[576,1152]{1,0:T(8,128)(2,1)} %bitcast.69), channel_id=1, source_target_pairs={{16,48},{48,80},{80,112},{112,144},{144,176},{176,208},{208,240},{... | collective-permute-start | bytes 3981320 | tf_op jit(solution)/shard_map/ppermute | solution.py:361
  13.6 18.4 %collective-permute-start.7 = (f32[4,6,1152]{2,1,0:T(8,128)}, f32[4,6,1152]{2,1,0:T(8,128)}, u32[]{:S(2)}, u32[]{:S(2)}) collective-permute-start(f32[4,6,1152]{2,1,0:T(8,128)} %get-tuple-element.228.following.mod), channel_id=1, source_target_pairs={{0,32},{16,48},{32,64},{48,80},{64,96},{80,112},{96,128},{112,144}... | collective-permute-start | bytes 331784 | tf_op jit(solution)/shard_map/ppermute | solution.py:362
  14.1 20.3 %collective-permute-start.8 = (bf16[1,576,1152]{2,1,0:T(8,128)(2,1)}, bf16[1,576,1152]{2,1,0:T(8,128)(2,1)}, u32[]{:S(2)}, u32[]{:S(2)}) collective-permute-start(bf16[1,576,1152]{2,1,0:T(8,128)(2,1)} %param.12), channel_id=1, source_target_pairs={{0,16},{16,0},{32,48},{48,32},{64,80},{80,64},{96,112},{112,96},{1... | collective-permute-start | bytes 3981320 | tf_op jit(solution)/shard_map/ppermute | solution.py:273
  31.9 10.7 %collective-permute-start.9 = (bf16[576,1152]{1,0:T(8,128)(2,1)}, bf16[576,1152]{1,0:T(8,128)(2,1)}, u32[]{:S(2)}, u32[]{:S(2)}) collective-permute-start(bf16[576,1152]{1,0:T(8,128)(2,1)} %collective-permute-done.6), channel_id=1, source_target_pairs={{16,0},{48,32},{80,64},{112,96},{144,128},{176,160},{208,192},{240... | collective-permute-start | bytes 3981320 | tf_op jit(solution)/shard_map/ppermute | solution.py:364
  45.5 26.8 %copy-start.10 = (bf16[576,1152]{1,0:T(8,128)(2,1)S(1)}, bf16[576,1152]{1,0:T(8,128)(2,1)}, u32[]{:S(2)}) copy-start(bf16[576,1152]{1,0:T(8,128)(2,1)} %get-tuple-element.265.tout) | copy-start | bytes 3981316 | tf_op jit(solution)/shard_map/while
  46.7 25.7 %copy-start.9 = (bf16[576,1152]{1,0:T(8,128)(2,1)S(1)}, bf16[576,1152]{1,0:T(8,128)(2,1)}, u32[]{:S(2)}) copy-start(bf16[576,1152]{1,0:T(8,128)(2,1)} %get-tuple-element.267.out) | copy-start | bytes 3981316 | tf_op jit(solution)/shard_map/while
  73.3 28.4 %collective-permute-start.1 = (f32[128,1152]{1,0:T(8,128)S(1)}, f32[128,1152]{1,0:T(8,128)S(1)}, u32[]{:S(2)}, u32[]{:S(2)}) collective-permute-start(f32[128,1152]{1,0:T(8,128)S(1)} %get-tuple-element.93), channel_id=1, source_target_pairs={{0,48},{16,32},{32,80},{48,64},{64,112},{80,96},{96,144},{112,128}... | collective-permute-start | bytes 1769480 | tf_op jit(solution)/shard_map/while/body/ppermute | solution.py:350
  86.1 5.7 collective-permute-start
  127.9 42.4 %collective-permute-start.1 = (f32[128,1152]{1,0:T(8,128)S(1)}, f32[128,1152]{1,0:T(8,128)S(1)}, u32[]{:S(2)}, u32[]{:S(2)}) collective-permute-start(f32[128,1152]{1,0:T(8,128)S(1)} %get-tuple-element.93), channel_id=1, source_target_pairs={{0,48},{16,32},{32,80},{48,64},{64,112},{80,96},{96,144},{112,128}... | collective-permute-start | bytes 1769480 | tf_op jit(solution)/shard_map/while/body/ppermute | solution.py:350
  153.0 6.1 collective-permute-start
  196.7 34.9 %collective-permute-start.1 = (f32[128,1152]{1,0:T(8,128)S(1)}, f32[128,1152]{1,0:T(8,128)S(1)}, u32[]{:S(2)}, u32[]{:S(2)}) collective-permute-start(f32[128,1152]{1,0:T(8,128)S(1)} %get-tuple-element.93), channel_id=1, source_target_pairs={{0,48},{16,32},{32,80},{48,64},{64,112},{80,96},{96,144},{112,128}... | collective-permute-start | bytes 1769480 | tf_op jit(solution)/shard_map/while/body/ppermute | solution.py:350
  215.6 5.5 collective-permute-start
  258.3 34.6 %collective-permute-start.1 = (f32[128,1152]{1,0:T(8,128)S(1)}, f32[128,1152]{1,0:T(8,128)S(1)}, u32[]{:S(2)}, u32[]{:S(2)}) collective-permute-start(f32[128,1152]{1,0:T(8,128)S(1)} %get-tuple-element.93), channel_id=1, source_target_pairs={{0,48},{16,32},{32,80},{48,64},{64,112},{80,96},{96,144},{112,128}... | collective-permute-start | bytes 1769480 | tf_op jit(solution)/shard_map/while/body/ppermute | solution.py:350
  276.7 5.7 collective-permute-start
  319.4 36.6 %collective-permute-start.1 = (f32[128,1152]{1,0:T(8,128)S(1)}, f32[128,1152]{1,0:T(8,128)S(1)}, u32[]{:S(2)}, u32[]{:S(2)}) collective-permute-start(f32[128,1152]{1,0:T(8,128)S(1)} %get-tuple-element.93), channel_id=1, source_target_pairs={{0,48},{16,32},{32,80},{48,64},{64,112},{80,96},{96,144},{112,128}... | collective-permute-start | bytes 1769480 | tf_op jit(solution)/shard_map/while/body/ppermute | solution.py:350
  339.0 6.5 %collective-permute-start = (bf16[128,576]{1,0:T(8,128)(2,1)S(1)}, bf16[128,576]{1,0:T(8,128)(2,1)S(1)}, u32[]{:S(2)}, u32[]{:S(2)}) collective-permute-start(bf16[128,576]{1,0:T(8,128)(2,1)S(1)} %temporal.5), channel_id=1, source_target_pairs={{0,48},{16,32},{32,80},{48,64},{64,112},{80,96},{96,144},{112,128}... | collective-permute-start | bytes 442376 | tf_op jit(solution)/shard_map/while/body/ppermute | solution.py:351
  382.5 35.3 %collective-permute-start.1 = (f32[128,1152]{1,0:T(8,128)S(1)}, f32[128,1152]{1,0:T(8,128)S(1)}, u32[]{:S(2)}, u32[]{:S(2)}) collective-permute-start(f32[128,1152]{1,0:T(8,128)S(1)} %get-tuple-element.93), channel_id=1, source_target_pairs={{0,48},{16,32},{32,80},{48,64},{64,112},{80,96},{96,144},{112,128}... | collective-permute-start | bytes 1769480 | tf_op jit(solution)/shard_map/while/body/ppermute | solution.py:350
  402.1 5.1 collective-permute-start
  444.7 34.5 %collective-permute-start.1 = (f32[128,1152]{1,0:T(8,128)S(1)}, f32[128,1152]{1,0:T(8,128)S(1)}, u32[]{:S(2)}, u32[]{:S(2)}) collective-permute-start(f32[128,1152]{1,0:T(8,128)S(1)} %get-tuple-element.93), channel_id=1, source_target_pairs={{0,48},{16,32},{32,80},{48,64},{64,112},{80,96},{96,144},{112,128}... | collective-permute-start | bytes 1769480 | tf_op jit(solution)/shard_map/while/body/ppermute | solution.py:350
  464.0 5.2 collective-permute-start
  483.5 25.4 %copy-start.10 = (bf16[576,1152]{1,0:T(8,128)(2,1)S(1)}, bf16[576,1152]{1,0:T(8,128)(2,1)}, u32[]{:S(2)}) copy-start(bf16[576,1152]{1,0:T(8,128)(2,1)} %get-tuple-element.265.tout) | copy-start | bytes 3981316 | tf_op jit(solution)/shard_map/while
  512.5 32.0 %collective-permute-start.1 = (f32[128,1152]{1,0:T(8,128)S(1)}, f32[128,1152]{1,0:T(8,128)S(1)}, u32[]{:S(2)}, u32[]{:S(2)}) collective-permute-start(f32[128,1152]{1,0:T(8,128)S(1)} %get-tuple-element.93), channel_id=1, source_target_pairs={{0,48},{16,32},{32,80},{48,64},{64,112},{80,96},{96,144},{112,128}... | collective-permute-start | bytes 1769480 | tf_op jit(solution)/shard_map/while/body/ppermute | solution.py:350
  525.0 9.5 %collective-permute-start = (bf16[128,576]{1,0:T(8,128)(2,1)S(1)}, bf16[128,576]{1,0:T(8,128)(2,1)S(1)}, u32[]{:S(2)}, u32[]{:S(2)}) collective-permute-start(bf16[128,576]{1,0:T(8,128)(2,1)S(1)} %temporal.5), channel_id=1, source_target_pairs={{0,48},{16,32},{32,80},{48,64},{64,112},{80,96},{96,144},{112,128}... | collective-permute-start | bytes 442376 | tf_op jit(solution)/shard_map/while/body/ppermute | solution.py:351
  550.8 26.6 %copy-start.16 = (f32[128,1152]{1,0:T(8,128)S(1)}, f32[128,1152]{1,0:T(8,128)}, u32[]{:S(2)}) copy-start(f32[128,1152]{1,0:T(8,128)} %copy-done.15) | copy-start | bytes 1769476
  550.8 12.0 %all-to-all-start.4 = ((bf16[16,8,1152]{2,1,0:T(8,128)(2,1)}), bf16[16,8,1152]{2,1,0:T(8,128)(2,1)S(1)}, u32[]{:S(2)}, u32[]{:S(2)}) async-start(bf16[16,8,1152]{2,1,0:T(8,128)(2,1)} %bitcast.64), calls=%async_computation.4 | async-start | bytes 589824 | tf_op jit(solution)/shard_map/all_to_all | solution.py:333
  554.5 44.1 %collective-permute-start.10 = (bf16[2,128,1152]{2,1,0:T(8,128)(2,1)}, bf16[2,128,1152]{2,1,0:T(8,128)(2,1)S(1)}, u32[]{:S(2)}, u32[]{:S(2)}) collective-permute-start(bf16[2,128,1152]{2,1,0:T(8,128)(2,1)} %copy-done.17), channel_id=1, source_target_pairs={{48,0},{32,16},{80,32},{64,48},{112,64},{96,80},{144,96},{128,112}... | collective-permute-start | bytes 1769480 | tf_op jit(solution)/shard_map/ppermute | solution.py:372
  594.9 10.5 %all-to-all-start.7 = ((bf16[16,8,576]{2,1,0:T(8,128)(2,1)}), bf16[16,8,576]{2,1,0:T(8,128)(2,1)S(1)}, u32[]{:S(2)}, u32[]{:S(2)}) async-start(bf16[16,8,576]{2,1,0:T(8,128)(2,1)} %bitcast.33), calls=%async_computation.7 | async-start | bytes 327680 | tf_op jit(solution)/shard_map/all_to_all | solution.py:333
  606.8 6.1 collective-permute-start.11
  (62 other events, 896.8 us)
